TPU v7x, 256 devices: a whole 4x4x8 slice. The times are simulated.
256 devices in a mesh: slab: 64 (over z, x, core), grp: 4 (over y).
Axes of the slice: x: 4, y: 4, z: 8, core: 2. Of those that a mesh axis runs over, the one named last changes fastest.
Arguments:
- iterate: float32 [24576, 256], P(('slab', 'grp')), may hold values from -6 to 6
- residual: float32 [24576, 256], P(('slab', 'grp')), may hold values from -6 to 6
- direction: float32 [24576, 256], P(('slab', 'grp')), may hold values from -6 to 6
- prior_rho: float32 [256], replicated, may hold values from 12288 to 49152
- diag_blocks: float32 [24576, 384], P(('slab', 'grp')), as said below
- lower_coupling: float32 [24576, 128], P(('slab', 'grp')), may hold values from -0.125 to 0.125
- upper_coupling: float32 [24576, 128], P(('slab', 'grp')), may hold values from -0.125 to 0.125
- interface: int32 [64, 128], P('slab'), may hold values from 0 to 383, as said below
- jacobi_inverse: float32 [24576, 96], P(('slab', 'grp'))
- slab_inverse: float32 [24576, 384], P(('slab', 'grp'))
- lower_factor: float32 [24576, 128], P(('slab', 'grp')), may hold values from -0.875 to 0.875
- upper_factor: float32 [24576, 128], P(('slab', 'grp')), may hold values from -0.5 to 0.5
Outputs:
- new_iterate: float32 [24576, 256], P(('slab', 'grp'))
- new_residual: float32 [24576, 256], P(('slab', 'grp'))
- new_direction: float32 [24576, 256], P(('slab', 'grp'))
- new_rho: float32 [256], replicated
Inputs may be any that keep to these rules, and one draw needn't show every extreme that they name: `interface`: row k lists 128 distinct dof numbers of slab k. `diag_blocks`: each diagonal block is a positive diagonal plus a skew-symmetric part.
All inputs are finite; a program needn't handle non-finite values.
Results may differ from a plain program's by a relative error of at most 0.0003.
Values sent between devices are 32-bit elements; how exact they have to be, the bound alone decides.
No kernel may reach another device: no remote copies, remote signals or barrier semaphores. Data moves between devices by JAX's collectives and lax.ppermute only.
A program may use at most 64 MiB of HBM per device.

v0:
```python
import jax
import jax.numpy as jnp
from jax import lax
from jax.experimental import pallas as pl
from jax.experimental.pallas import tpu as pltpu
from jax.sharding import Mesh
from jax.sharding import PartitionSpec as P

SLAB = ("slab_0", "slab_1", "slab_2")
PLANE = ("slab_1", "slab_2")
SLAB_GRP = ("slab_0", "slab_1", "slab_2", "grp")
VMEM = pl.BlockSpec(memory_space=pltpu.VMEM)
SMEM = pl.BlockSpec(memory_space=pltpu.SMEM)


def halves(x):
    high = x.astype(jnp.bfloat16)
    return high, (x - high.astype(jnp.float32)).astype(jnp.bfloat16)


def mm(left, right, right_dim=0):
    high, low = halves(left)
    right_high, right_low = right if isinstance(right, tuple) else halves(right)

    def dot(a, b):
        return lax.dot_general(
            a, b, (((1,), (right_dim,)), ((), ())), preferred_element_type=jnp.float32
        )

    n = left.shape[0]
    both = dot(jnp.concatenate([high, low], axis=0), right_high)
    return both[:n] + (both[n:] + dot(high, right_low))


def keep(ref, at, x):
    high, low = halves(x)
    ref[0, at] = high
    ref[1, at] = low


def kept(ref, at, rows=slice(None)):
    return ref[0, at, rows], ref[1, at, rows]


def shaped(*shape, dtype=jnp.float32):
    return jax.ShapeDtypeStruct(shape, dtype)


def call(body, outs, smem, *args, scratch=()):
    return pl.pallas_call(
        body,
        out_shape=outs,
        in_specs=[SMEM] * smem + [VMEM] * (len(args) - smem),
        out_specs=jax.tree.map(lambda _: VMEM, outs),
        scratch_shapes=list(scratch),
        compiler_params=pltpu.CompilerParams(vmem_limit_bytes=16 * 1024 * 1024),
    )(*args)


def to_each(pieces, axes):
    return lax.all_to_all(pieces, axes, split_axis=0, concat_axis=0, tiled=True)


def ring(x, axis, step):
    count = lax.axis_size(axis)
    return lax.ppermute(x, axis, [(i, (i + step) % count) for i in range(count)])


def beside(faces):
    count = lax.axis_size(SLAB)
    below = lax.ppermute(faces, SLAB, [(i, i + 1) for i in range(count - 1)])
    above = lax.ppermute(faces, SLAB, [(i + 1, i) for i in range(count - 1)])
    return below, above


def swapped(rows):
    half = rows.shape[0] // 2
    return jnp.concatenate([rows[half:], rows[:half]], axis=0)


def flipped(x):
    half = x.shape[1] // 2
    return jnp.concatenate([x[:, half:], x[:, :half]], axis=1)


def pick(index_ref, source_ref, out_ref):
    for j in range(128):
        out_ref[j : j + 1, :] = source_ref[pl.ds(index_ref[0, j], 1), :]


def pack(direction_ref, residual_ref, inverse_ref, lower_ref, upper_ref, out_ref):
    d = direction_ref[...]
    r = residual_ref[...]
    for q in range(4):
        out_ref[q, :, 0:128] = jnp.concatenate([d[:, 64 * q : 64 * q + 64], r[:, 64 * q : 64 * q + 64]], axis=1)
        out_ref[q, :, 128:512] = inverse_ref[...]
        out_ref[q, :, 512:640] = lower_ref[...]
        out_ref[q, :, 640:768] = upper_ref[...]


def make_maps(index_ref, got_ref, factor_ref, maps_ref, faces_ref, all_scr, face_scr):
    factor = mm(got_ref[:, 128:512], got_ref[:, 512:640])
    factor_ref[...] = factor
    all_scr[:, 0:128] = got_ref[:, 0:128]
    all_scr[:, 128:256] = factor
    all_scr[:, 256:384] = got_ref[:, 640:768]
    pick(index_ref, all_scr, face_scr)
    faces_ref[...] = jnp.concatenate([face_scr[0:64, 0:64], face_scr[64:128, 0:64]], axis=1)
    maps_ref[0:128] = -face_scr[:, 128:256]
    maps_ref[128:256] = -face_scr[:, 256:384]


def smooth(index_ref, grp_ref, got_ref, p0, p1, p2, p3, below_ref, above_ref, x_ref, s_ref, faces_ref):
    below = jnp.concatenate([below_ref[:, 0:64], below_ref[:, 64:128]], axis=0)
    above = jnp.concatenate([above_ref[:, 0:64], above_ref[:, 64:128]], axis=0)
    v = jnp.concatenate([got_ref[:, 0:64], below, above], axis=0)
    pieces = (p0, p1, p2, p3)
    image = mm(jnp.concatenate([piece[:, 0:640] for piece in pieces], axis=0), v)
    for step, piece in enumerate(pieces):
        rows = pl.ds(pl.multiple_of(96 * ((grp_ref[0] + 4 - step) % 4), 8), 96)
        x = jnp.concatenate([got_ref[rows, 64:128], image[96 * step : 96 * step + 96]], axis=1)
        x_ref[rows, :] = x
        s_ref[rows, :] = mm(piece[:, 640:736], x)
    pick(index_ref, s_ref, faces_ref)


def solve_slab(
    index_ref, grp_ref, got_ref, p0, p1, p2, p3, factor_ref, x_ref, s_ref, below_ref, above_ref,
    defect_ref, out_ref, solved_scr, face_scr
):
    v = jnp.concatenate([s_ref[...], below_ref[...], above_ref[...]], axis=0)
    pieces = (p0, p1, p2, p3)
    applied = mm(jnp.concatenate([piece[:, 0:640] for piece in pieces], axis=0), v)
    for step in range(4):
        rows = pl.ds(pl.multiple_of(96 * ((grp_ref[0] + 4 - step) % 4), 8), 96)
        defect_ref[rows, :] = x_ref[rows, :] - applied[96 * step : 96 * step + 96]
    x = x_ref[...]
    solved = mm(got_ref[:, 128:512], defect_ref[...])
    solved_scr[...] = solved
    pick(index_ref, solved_scr, face_scr)
    offsets = face_scr[...].T
    turned = x.T
    pulled = -mm(turned, jnp.concatenate([factor_ref[...], got_ref[:, 640:768]], axis=1))
    y = s_ref[...] + solved
    known = jnp.concatenate(
        [
            jnp.sum(x * y, axis=0, keepdims=True),
            jnp.sum(x * flipped(y), axis=0, keepdims=True),
            jnp.sum(got_ref[:, 0:128] * flipped(x), axis=0, keepdims=True),
            jnp.zeros((5, 128), jnp.float32),
        ],
        axis=0,
    )
    for p in range(8):
        for at, part in enumerate((offsets, pulled[:, 0:128], pulled[:, 128:256])):
            out_ref[p, 16 * at : 16 * at + 8] = part[8 * p : 8 * p + 8]
            out_ref[p, 16 * at + 8 : 16 * at + 16] = part[64 + 8 * p : 72 + 8 * p]
        out_ref[p, 48:56] = known


def map_plane(
    x_ref, c_ref, m0, m1, m2, m3, n0, n1, n2, n3, maps_ref, states_f_ref, states_b_ref, plane_ref,
    all_scr, f_scr
):
    for step, (mine, other) in enumerate(((m0, n0), (m1, n1), (m2, n2), (m3, n3))):
        at = 2 * ((x_ref[0] + 4 - step) % 4)
        all_scr[at + c_ref[0]] = mine[...]
        all_scr[at + 1 - c_ref[0]] = other[...]
    for i in range(8):
        keep(maps_ref, i, all_scr[i])
    row = lax.broadcasted_iota(jnp.int32, (128, 128), 0)
    lane = lax.broadcasted_iota(jnp.int32, (128, 128), 1)
    eye = jnp.where(row == lane, 1.0, 0.0).astype(jnp.float32)
    keep(states_f_ref, 0, eye)
    f_scr[0] = all_scr[0, 0:128].T
    for i in range(1, 8):
        keep(states_f_ref, i, f_scr[i - 1])
        f_scr[i] = mm(f_scr[i - 1], kept(maps_ref, i, slice(0, 128)), 1)
    plane_ref[0:128] = f_scr[7]
    keep(states_b_ref, 7, jnp.concatenate([eye, jnp.zeros((128, 128), jnp.float32)], axis=0))
    plane_ref[128:256] = all_scr[7, 128:256].T
    plane_ref[256:384] = f_scr[7]
    for i in reversed(range(7)):
        keep(states_b_ref, i, plane_ref[128:384])
        b = mm(plane_ref[128:384], kept(maps_ref, i, slice(128, 256)), 1)
        plane_ref[128:256] = b[0:128]
        plane_ref[256:384] = b[128:256] + f_scr[i]


def in_lanes(values, place):
    row = lax.broadcasted_iota(jnp.int32, (16, 128), 0)
    lane = lax.broadcasted_iota(jnp.int32, (16, 128), 1)
    target = jnp.where(row < 8, row + 8 * place, row + 56 + 8 * place)
    return jnp.sum(jnp.where(lane == target, values, 0.0), axis=0, keepdims=True)


def sweep_plane(place_ref, got_ref, maps_ref, states_f_ref, states_b_ref, own_f_ref, own_b_ref, out_ref):
    own_f_ref[0] = jnp.zeros((16, 128), jnp.float32)
    own_f_ref[1] = got_ref[0, 0:16]
    for i in range(1, 8):
        f = mm(own_f_ref[i], kept(maps_ref, i, slice(0, 128)), 1) + got_ref[i, 0:16]
        own_f_ref[i + 1] = f
    own_b_ref[7] = jnp.zeros((16, 128), jnp.float32)
    own_b_ref[6] = own_f_ref[8]
    for i in reversed(range(7)):
        b = mm(own_b_ref[i], kept(maps_ref, i, slice(128, 256)), 1) + own_f_ref[i + 1]
        if i > 0:
            own_b_ref[i - 1] = b
    gamma = jnp.zeros((16, 128), jnp.float32)
    delta = gamma
    same = gamma
    cross = gamma
    total = jnp.zeros((8, 128), jnp.float32)
    for i in range(8):
        g = got_ref[i, 16:32]
        h = got_ref[i, 32:48]
        total = total + got_ref[i, 48:56]
        gamma = gamma + mm(g, kept(states_f_ref, i), 1) + mm(h, kept(states_b_ref, i, slice(128, 256)), 1)
        delta = delta + mm(h, kept(states_b_ref, i, slice(0, 128)), 1)
        own_f = own_f_ref[i]
        own_b = own_b_ref[i]
        same = same + g * own_f + h * own_b
        cross = cross + g * swapped(own_f) + h * swapped(own_b)
    place = place_ref[0]
    known = jnp.concatenate(
        [
            total[0:3],
            in_lanes(jnp.sum(same, axis=1, keepdims=True), place),
            in_lanes(jnp.sum(cross, axis=1, keepdims=True), place),
            jnp.zeros((3, 128), jnp.float32),
        ],
        axis=0,
    )
    for z in range(8):
        out_ref[z, 0:16] = own_f_ref[8]
        out_ref[z, 16:32] = b
        out_ref[z, 32:48] = gamma
        out_ref[z, 48:64] = delta
        out_ref[z, 64:72] = known


def solve_planes(
    z_ref, place_ref, sums_ref, a0, a1, a2, a3, a4, b1, b2, b3,
    states_f_ref, states_b_ref, own_f_ref, own_b_ref, out_ref, total_ref, maps_scr, f_scr, b_scr
):
    for step, piece in ((0, a0), (1, a1), (2, a2), (3, a3), (4, a4), (-1, b1), (-2, b2), (-3, b3)):
        maps_scr[(z_ref[0] + 8 - step) % 8] = piece[...]
    f_scr[0] = jnp.zeros((16, 128), jnp.float32)
    f_scr[1] = sums_ref[0, 0:16]
    for z in range(1, 7):
        f_scr[z + 1] = mm(f_scr[z], maps_scr[z, 0:128]) + sums_ref[z, 0:16]
    b_scr[7] = jnp.zeros((16, 128), jnp.float32)
    for z in range(1, 8):
        b_scr[z - 1] = mm(f_scr[z], maps_scr[z, 256:384]) + sums_ref[z, 16:32]
    for z in reversed(range(1, 7)):
        b_scr[z - 1] = b_scr[z - 1] + mm(b_scr[z], maps_scr[z, 128:256])
    same = jnp.zeros((16, 128), jnp.float32)
    cross = same
    known = jnp.zeros((8, 128), jnp.float32)
    for z in range(8):
        gamma = sums_ref[z, 32:48]
        delta = sums_ref[z, 48:64]
        same = same + gamma * f_scr[z] + delta * b_scr[z]
        cross = cross + gamma * swapped(f_scr[z]) + delta * swapped(b_scr[z])
        known = known + sums_ref[z, 64:72]
    total_ref[...] = known
    place = place_ref[0]
    dots = jnp.concatenate(
        [
            known[3:4] + in_lanes(jnp.sum(same, axis=1, keepdims=True), place),
            known[4:5] + in_lanes(jnp.sum(cross, axis=1, keepdims=True), place),
            jnp.zeros((6, 128), jnp.float32),
        ],
        axis=0,
    )
    f = f_scr[z_ref[0]]
    b = b_scr[z_ref[0]]
    for i in range(8):
        out_ref[i, 0:16] = mm(f, kept(states_f_ref, i)) + own_f_ref[i]
        out_ref[i, 16:32] = (
            mm(b, kept(states_b_ref, i, slice(0, 128)))
            + mm(f, kept(states_b_ref, i, slice(128, 256)))
            + own_b_ref[i]
        )
        out_ref[i, 32:40] = dots


def finish(got_ref, back_ref, total_ref, rho_ref, defect_ref, x_ref, s_ref, out_ref):
    def rows(start):
        return jnp.concatenate(
            [back_ref[p, start : start + 8] for p in range(8)]
            + [back_ref[p, start + 8 : start + 16] for p in range(8)],
            axis=0,
        )

    dots = back_ref[0, 32:40]
    for p in range(1, 8):
        dots = dots + back_ref[p, 32:40]
    rest = defect_ref[...] - mm(got_ref[:, 512:640], rows(0), 1)
    precond = s_ref[...] + mm(got_ref[:, 128:512], rest) - mm(got_ref[:, 640:768], rows(16), 1)
    total = total_ref[...]
    step = rho_ref[...] / total[2:3, 0:64]
    same = total[0:1] + dots[0:1]
    cross = total[1:2] + dots[1:2]
    rho = same[:, 0:64] - step * (cross[:, 0:64] + cross[:, 64:128]) + step * (step * same[:, 64:128])
    result = precond[:, 0:64] - step * precond[:, 64:128]
    both = jnp.concatenate([result, x_ref[:, 64:128]], axis=1)
    scales = jnp.broadcast_to(jnp.concatenate([step, rho], axis=1), (8, 128))
    for q in range(4):
        out_ref[q, 0:96] = both[96 * q : 96 * q + 96]
        out_ref[q, 96:104] = scales


def body(
    iterate,
    residual,
    direction,
    prior_rho,
    diag_blocks,
    lower_coupling,
    upper_coupling,
    interface,
    jacobi_inverse,
    slab_inverse,
    lower_factor,
    upper_factor,
):
    def here(axes):
        return lax.axis_index(axes).astype(jnp.int32).reshape(1)

    grp = here("grp")
    part = 64
    operator = jnp.concatenate([diag_blocks, lower_coupling, upper_coupling, jacobi_inverse], axis=1)
    got = to_each(
        call(pack, shaped(4, 96, 768), 0, direction, residual, slab_inverse, lower_factor, upper_factor),
        "grp",
    ).reshape(384, 768)
    pieces = [operator] + [ring(operator, "grp", step) for step in (1, 2, 3)]
    factor, maps, faces = call(
        make_maps,
        (shaped(384, 128), shaped(256, 128), shaped(64, 128)),
        1,
        interface,
        got,
        scratch=[pltpu.VMEM((384, 384), jnp.float32), pltpu.VMEM((128, 384), jnp.float32)],
    )
    along = [maps] + [ring(maps, "slab_1", step) for step in (1, 2, 3)]
    across = [ring(m, "slab_2", 1) for m in along]
    below, above = beside(faces)
    x, s, faces = call(
        smooth,
        (shaped(384, 128), shaped(384, 128), shaped(128, 128)),
        2,
        interface,
        grp,
        got,
        *pieces,
        below,
        above,
    )
    below, above = beside(faces)
    defect, sent = call(
        solve_slab,
        (shaped(384, 128), shaped(8, 56, 128)),
        2,
        interface,
        grp,
        got,
        *pieces,
        factor,
        x,
        s,
        below,
        above,
        scratch=[pltpu.VMEM((384, 128), jnp.float32), pltpu.VMEM((128, 128), jnp.float32)],
    )
    maps, states_f, states_b, plane = call(
        map_plane,
        (
            shaped(2, 8, 256, 128, dtype=jnp.bfloat16),
            shaped(2, 8, 128, 128, dtype=jnp.bfloat16),
            shaped(2, 8, 256, 128, dtype=jnp.bfloat16),
            shaped(384, 128),
        ),
        2,
        here("slab_1"),
        here("slab_2"),
        *along,
        *across,
        scratch=[pltpu.VMEM((8, 256, 128), jnp.float32), pltpu.VMEM((8, 128, 128), jnp.float32)],
    )
    ups = [plane]
    for _ in range(1, 5):
        ups.append(ring(ups[-1], "slab_0", 1))
    downs = [plane]
    for _ in range(1, 4):
        downs.append(ring(downs[-1], "slab_0", -1))
    place = here(PLANE)
    own_f, own_b, sums = call(
        sweep_plane,
        (shaped(9, 16, 128), shaped(8, 16, 128), shaped(8, 72, 128)),
        1,
        place,
        to_each(sent, PLANE),
        maps,
        states_f,
        states_b,
    )
    entering, total = call(
        solve_planes,
        (shaped(8, 40, 128), shaped(8, 128)),
        2,
        here("slab_0"),
        place,
        to_each(sums, "slab_0"),
        *ups,
        *downs[1:],
        states_f,
        states_b,
        own_f,
        own_b,
        scratch=[
            pltpu.VMEM((8, 384, 128), jnp.float32),
            pltpu.VMEM((8, 16, 128), jnp.float32),
            pltpu.VMEM((8, 16, 128), jnp.float32),
        ],
    )
    own_rho = lax.dynamic_slice_in_dim(prior_rho, part * grp[0], part).reshape(1, part)
    out = to_each(
        call(
            finish,
            shaped(4, 104, 128),
            0,
            got,
            to_each(entering, PLANE),
            total,
            own_rho,
            defect,
            x,
            s,
        ),
        "grp",
    )
    result = jnp.concatenate([out[q, :96, :part] for q in range(4)], axis=1)
    image = jnp.concatenate([out[q, :96, part:] for q in range(4)], axis=1)
    step_size = jnp.concatenate([out[q, 96, :part] for q in range(4)])
    new_rho = jnp.concatenate([out[q, 96, part:] for q in range(4)])
    new_iterate = iterate + step_size * direction
    new_residual = residual - step_size * image
    new_direction = result + new_rho / prior_rho * direction
    return (new_iterate, new_residual, new_direction, new_rho)


def solution(mesh):
    split = Mesh(
        mesh.devices.reshape(8, 4, 2, mesh.shape["grp"]), ("slab_0", "slab_1", "slab_2", "grp")
    )
    rows = P(SLAB_GRP, None)
    placed = (rows, rows, rows, P(), rows, rows, rows, P(SLAB, None), rows, rows, rows, rows)
    return jax.shard_map(
        body, mesh=split, in_specs=placed, out_specs=(rows, rows, rows, P()), check_vma=False
    )
```

profile of v0, /device:TPU:1, one launch (start us, length us, event | category | flops | bytes accessed | tf_op | source)
XLA Modules:
  0.0 158.5 jit_solution(4592779249753398325)
XLA Ops:
  0.6 0.9 copy-done.4
  1.5 0.9 copy-done.6
  2.4 0.9 copy-done.18
  3.3 0.8 copy-done.37
  4.1 0.8 copy-done.38
  4.9 1.1 shard_map.147
  6.1 5.1 %all-to-all-start = ((f32[4,96,768]{2,1,0:T(8,128)}), f32[4,96,768]{2,1,0:T(8,128)S(1)}, u32[]{:S(2)}, u32[]{:S(2)}) async-start(f32[4,96,768]{2,1,0:T(8,128)} %shard_map.147), calls=%async_computation | async-start | bytes 2359296 | tf_op jit(solution)/shard_map/all_to_all | solution.py:61
  11.3 14.9 %all-to-all-done = f32[4,96,768]{2,1,0:T(8,128)S(1)} async-done(((f32[4,96,768]{2,1,0:T(8,128)}), f32[4,96,768]{2,1,0:T(8,128)S(1)}, u32[]{:S(2)}, u32[]{:S(2)}) %all-to-all-start) | async-done | bytes 1179680 | tf_op jit(solution)/shard_map/all_to_all | solution.py:61
  26.1 1.7 %shard_map.148 = (f32[384,128]{1,0:T(8,128)S(1)}, f32[256,128]{1,0:T(8,128)S(1)}, f32[64,128]{1,0:T(8,128)}) custom-call(s32[1,128]{1,0:T(1,128)S(1)} %copy-done.39, f32[384,768]{1,0:T(8,128)S(1)} %bitcast.40), custom_call_target="tpu_custom_call" | custom-call | tf_op jit(solution)/shard_map/pallas_call | solution.py:50
  27.8 2.0 %collective-permute-start.7 = (f32[256,128]{1,0:T(8,128)S(1)}, f32[256,128]{1,0:T(8,128)S(1)}, u32[]{:S(2)}, u32[]{:S(2)}) collective-permute-start(f32[256,128]{1,0:T(8,128)S(1)} %get-tuple-element.27.m0), channel_id=1, source_target_pairs={{0,8},{8,16},{16,24},{24,0},{1,9},{9,17},{17,25},{25,1},{2,10},{10... | collective-permute-start | bytes 393224 | tf_op jit(solution)/shard_map/ppermute | solution.py:66
  29.8 2.5 %collective-permute-start.8 = (f32[256,128]{1,0:T(8,128)S(1)}, f32[256,128]{1,0:T(8,128)S(1)}, u32[]{:S(2)}, u32[]{:S(2)}) collective-permute-start(f32[256,128]{1,0:T(8,128)S(1)} %get-tuple-element.27.m0), channel_id=1, source_target_pairs={{0,16},{8,24},{16,0},{24,8},{1,17},{9,25},{17,1},{25,9},{2,18},{10... | collective-permute-start | bytes 393224 | tf_op jit(solution)/shard_map/ppermute | solution.py:66
  32.3 1.2 collective-permute-start.9
  33.5 2.7 %collective-permute-start.10 = (f32[256,128]{1,0:T(8,128)S(1)}, f32[256,128]{1,0:T(8,128)S(1)}, u32[]{:S(2)}, u32[]{:S(2)}) collective-permute-start(f32[256,128]{1,0:T(8,128)S(1)} %get-tuple-element.27.m0), channel_id=1, source_target_pairs={{0,4},{4,0},{1,5},{5,1},{2,6},{6,2},{3,7},{7,3},{8,12},{12,8},{9,1... | collective-permute-start | bytes 393224 | tf_op jit(solution)/shard_map/ppermute | solution.py:66
  36.9 1.1 collective-permute-start.11
  39.0 1.8 %collective-permute-start.1 = (f32[96,736]{1,0:T(8,128)S(1)}, f32[96,736]{1,0:T(8,128)}, u32[]{:S(2)}, u32[]{:S(2)}) collective-permute-start(f32[96,736]{1,0:T(8,128)S(1)} %constant_dynamic-update-slice_fusion.p0), channel_id=1, source_target_pairs={{0,2},{1,3},{2,0},{3,1},{4,6},{5,7},{6,4},{7,5},{8,10},{9,11},{10,... | collective-permute-start | bytes 847880 | tf_op jit(solution)/shard_map/ppermute | solution.py:66
  40.8 0.7 collective-permute-start.2
  41.5 0.7 copy-done.27
  42.2 1.2 collective-permute-start.12
  43.4 0.7 copy-done.23
  45.4 0.7 copy-done.31
  46.0 2.9 %collective-permute-start.3 = (f32[64,128]{1,0:T(8,128)}, f32[64,128]{1,0:T(8,128)}, u32[]{:S(2)}, u32[]{:S(2)}) collective-permute-start(f32[64,128]{1,0:T(8,128)} %get-tuple-element.22), channel_id=1, source_target_pairs={{0,4},{4,8},{8,12},{12,16},{16,20},{20,24},{24,28},{28,32},{32,36}... | collective-permute-start | bytes 98312 | tf_op jit(solution)/shard_map/ppermute | solution.py:71
  49.6 2.0 %collective-permute-start.4 = (f32[64,128]{1,0:T(8,128)}, f32[64,128]{1,0:T(8,128)}, u32[]{:S(2)}, u32[]{:S(2)}) collective-permute-start(f32[64,128]{1,0:T(8,128)} %get-tuple-element.22), channel_id=1, source_target_pairs={{4,0},{8,4},{12,8},{16,12},{20,16},{24,20},{28,24},{32,28},{36,32}... | collective-permute-start | bytes 98312 | tf_op jit(solution)/shard_map/ppermute | solution.py:72
  51.6 0.9 copy-done.20
  52.5 0.9 copy-done.22
  53.4 0.9 copy-done.24
  54.3 0.9 copy-done.26
  55.3 0.9 copy-done.28
  56.2 0.9 copy-done.30
  57.1 0.9 copy-done.32
  58.0 0.9 copy-done.34
  58.9 3.3 %shard_map.151 = (bf16[2,8,256,128]{3,2,1,0:T(8,128)(2,1)S(1)}, bf16[2,8,128,128]{3,2,1,0:T(8,128)(2,1)S(1)}, bf16[2,8,256,128]{3,2,1,0:T(8,128)(2,1)S(1)}, f32[384,128]{1,0:T(8,128)}) custom-call(s32[1]{0:T(128)} %bitcast.4.x_ref, s32[1]{0:T(128)} %bitcast.5.c_ref, f32[256,128]{1,0:T(8,128)S(1)} %copy-done.20, f32[256,128]{1,0:T(8,128)S(1)} %copy-done.22, ...), custom_call_target="tpu_custom_call" | custom-call | tf_op jit(solution)/shard_map/pallas_call | solution.py:50
  62.2 1.0 copy-done
  63.2 1.5 collective-permute-start.14
  64.7 2.0 %shard_map.149 = (f32[384,128]{1,0:T(8,128)S(1)}, f32[384,128]{1,0:T(8,128)S(1)}, f32[128,128]{1,0:T(8,128)S(1)}) custom-call(s32[1,128]{1,0:T(1,128)S(1)} %copy-done.39, s32[1]{0:T(128)} %bitcast.3.grp_ref, f32[384,768]{1,0:T(8,128)S(1)} %bitcast.41, f32[96,736]{1,0:T(8,128)S(1)} %constant_dynamic-update-slice_fusion.p0, ...), custom_call_target="tpu_custom_call" | custom-call | tf_op jit(solution)/shard_map/pallas_call | solution.py:50
  66.7 3.9 %collective-permute-start.5 = (f32[128,128]{1,0:T(8,128)S(1)}, f32[128,128]{1,0:T(8,128)S(1)}, u32[]{:S(2)}, u32[]{:S(2)}) collective-permute-start(f32[128,128]{1,0:T(8,128)S(1)} %get-tuple-element.25), channel_id=1, source_target_pairs={{0,4},{4,8},{8,12},{12,16},{16,20},{20,24},{24,28},{28,32},{32,36}... | collective-permute-start | bytes 196616 | tf_op jit(solution)/shard_map/ppermute | solution.py:71
  70.7 3.0 %collective-permute-start.6 = (f32[128,128]{1,0:T(8,128)S(1)}, f32[128,128]{1,0:T(8,128)S(1)}, u32[]{:S(2)}, u32[]{:S(2)}) collective-permute-start(f32[128,128]{1,0:T(8,128)S(1)} %get-tuple-element.25), channel_id=1, source_target_pairs={{4,0},{8,4},{12,8},{16,12},{20,16},{24,20},{28,24},{32,28},{36,32}... | collective-permute-start | bytes 196616 | tf_op jit(solution)/shard_map/ppermute | solution.py:72
  73.6 2.6 %collective-permute-done.6.above_ref = f32[128,128]{1,0:T(8,128)S(1)} collective-permute-done((f32[128,128]{1,0:T(8,128)S(1)}, f32[128,128]{1,0:T(8,128)S(1)}, u32[]{:S(2)}, u32[]{:S(2)}) %collective-permute-start.6) | collective-permute-done | bytes 65568 | tf_op jit(solution)/shard_map/ppermute | solution.py:72
  76.3 2.3 %shard_map.150 = (f32[384,128]{1,0:T(8,128)S(1)}, f32[8,56,128]{2,1,0:T(8,128)S(1)}) custom-call(s32[1,128]{1,0:T(1,128)S(1)} %copy-done.39, s32[1]{0:T(128)} %bitcast.3.grp_ref, f32[384,768]{1,0:T(8,128)S(1)} %bitcast.42, f32[96,736]{1,0:T(8,128)S(1)} %constant_dynamic-update-slice_fusion.p0, f32[96,736]{1,0:T(8,128)S(1)} %collective-permute-done.p1, ...), custom_call_target="tpu_custom_call" | custom-call | tf_op jit(solution)/shard_map/pallas_call | solution.py:50
  78.6 0.7 copy-done.8
  79.2 0.7 copy-done.11
  79.9 9.4 %all-to-all-start.1 = ((f32[8,56,128]{2,1,0:T(8,128)}), f32[8,56,128]{2,1,0:T(8,128)S(1)}, u32[]{:S(2)}, u32[]{:S(2)}) async-start(f32[8,56,128]{2,1,0:T(8,128)} %copy-done.8), calls=%async_computation.1 | async-start | bytes 458752 | tf_op jit(solution)/shard_map/all_to_all | solution.py:61
  89.3 1.4 collective-permute-start.18
  91.0 4.4 %all-to-all-done.1.got_ref = f32[8,56,128]{2,1,0:T(8,128)S(1)} async-done(((f32[8,56,128]{2,1,0:T(8,128)}), f32[8,56,128]{2,1,0:T(8,128)S(1)}, u32[]{:S(2)}, u32[]{:S(2)}) %all-to-all-start.1) | async-done | bytes 229408 | tf_op jit(solution)/shard_map/all_to_all | solution.py:61
  95.5 1.2 copy-done.1
  96.7 3.3 %shard_map.152 = (f32[9,16,128]{2,1,0:T(8,128)S(1)}, f32[8,16,128]{2,1,0:T(8,128)S(1)}, f32[8,72,128]{2,1,0:T(8,128)}) custom-call(s32[1]{0:T(128)} %bitcast.2.place_ref, f32[8,56,128]{2,1,0:T(8,128)S(1)} %all-to-all-done.1.got_ref, bf16[2,8,256,128]{3,2,1,0:T(8,128)(2,1)S(1)} %copy-done.1, bf16[2,8,128,128]{3,2,1,0:T(8,128)(2,1)S(1)} %get-tuple-element.29.states_f_ref, ...), custom_call_target="tpu_custom_call" | custom-call | tf_op jit(solution)/shard_map/pallas_call | solution.py:50
  100.6 7.3 %all-to-all-start.2 = ((f32[8,72,128]{2,1,0:T(8,128)}), f32[8,72,128]{2,1,0:T(8,128)S(1)}, u32[]{:S(2)}, u32[]{:S(2)}) async-start(f32[8,72,128]{2,1,0:T(8,128)} %get-tuple-element.31), calls=%async_computation.2 | async-start | bytes 589824 | tf_op jit(solution)/shard_map/all_to_all | solution.py:61
  107.9 2.7 %collective-permute-start.19 = (f32[384,128]{1,0:T(8,128)S(1)}, f32[384,128]{1,0:T(8,128)}, u32[]{:S(2)}, u32[]{:S(2)}) collective-permute-start(f32[384,128]{1,0:T(8,128)S(1)} %collective-permute-done.18.b1), channel_id=1, source_target_pairs={{0,224},{32,0},{64,32},{96,64},{128,96},{160,128},{192,160},{224,1... | collective-permute-start | bytes 589832 | tf_op jit(solution)/shard_map/ppermute | solution.py:66
  110.6 0.7 copy-done.13
  111.3 8.8 %collective-permute-done.19.b2 = f32[384,128]{1,0:T(8,128)} collective-permute-done((f32[384,128]{1,0:T(8,128)S(1)}, f32[384,128]{1,0:T(8,128)}, u32[]{:S(2)}, u32[]{:S(2)}) %collective-permute-start.19) | collective-permute-done | bytes 196640 | tf_op jit(solution)/shard_map/ppermute | solution.py:66
  120.1 1.9 %collective-permute-start.20 = (f32[384,128]{1,0:T(8,128)}, f32[384,128]{1,0:T(8,128)S(1)}, u32[]{:S(2)}, u32[]{:S(2)}) collective-permute-start(f32[384,128]{1,0:T(8,128)} %collective-permute-done.19.b2), channel_id=1, source_target_pairs={{0,224},{32,0},{64,32},{96,64},{128,96},{160,128},{192,160},{224,1... | collective-permute-start | bytes 589832 | tf_op jit(solution)/shard_map/ppermute | solution.py:66
  122.1 3.1 %collective-permute-done.20.b3 = f32[384,128]{1,0:T(8,128)S(1)} collective-permute-done((f32[384,128]{1,0:T(8,128)}, f32[384,128]{1,0:T(8,128)S(1)}, u32[]{:S(2)}, u32[]{:S(2)}) %collective-permute-start.20) | collective-permute-done | bytes 196640 | tf_op jit(solution)/shard_map/ppermute | solution.py:66
  125.2 0.7 copy-done.15
  125.9 2.7 %collective-permute-done.17.a4 = f32[384,128]{1,0:T(8,128)} collective-permute-done((f32[384,128]{1,0:T(8,128)}, f32[384,128]{1,0:T(8,128)}, u32[]{:S(2)}, u32[]{:S(2)}) %collective-permute-start.17) | collective-permute-done | bytes 196640 | tf_op jit(solution)/shard_map/ppermute | solution.py:66
  128.6 0.9 copy-done.14
  129.5 0.9 copy-done.16
  130.4 0.8 copy-done.36
  131.3 3.6 %shard_map.153 = (f32[8,40,128]{2,1,0:T(8,128)S(1)}, f32[8,128]{1,0:T(8,128)S(1)}) custom-call(s32[1]{0:T(128)} %bitcast.1.z_ref, s32[1]{0:T(128)} %bitcast.2.place_ref, f32[8,72,128]{2,1,0:T(8,128)S(1)} %all-to-all-done.2.sums_ref, f32[384,128]{1,0:T(8,128)} %get-tuple-element.32.a0, f32[384,128]{1,0:T(8,128)} %collective-permute-done.14.a1, ...), custom_call_target="tpu_custom_call" | custom-call | tf_op jit(solution)/shard_map/pallas_call | solution.py:50
  134.9 0.7 copy-done.17
  135.5 5.7 %all-to-all-start.3 = ((f32[8,40,128]{2,1,0:T(8,128)}), f32[8,40,128]{2,1,0:T(8,128)S(1)}, u32[]{:S(2)}, u32[]{:S(2)}) async-start(f32[8,40,128]{2,1,0:T(8,128)} %copy-done.17), calls=%async_computation.3 | async-start | bytes 327680 | tf_op jit(solution)/shard_map/all_to_all | solution.py:61
  141.3 5.5 %all-to-all-done.3.back_ref = f32[8,40,128]{2,1,0:T(8,128)S(1)} async-done(((f32[8,40,128]{2,1,0:T(8,128)}), f32[8,40,128]{2,1,0:T(8,128)S(1)}, u32[]{:S(2)}, u32[]{:S(2)}) %all-to-all-start.3) | async-done | bytes 163872 | tf_op jit(solution)/shard_map/all_to_all | solution.py:61
  146.8 0.9 copy-done.12
  147.7 0.9 shard_map.154
  148.6 8.2 %all_to_all.25 = f32[4,104,128]{2,1,0:T(8,128)S(1)} all-to-all(f32[4,104,128]{2,1,0:T(8,128)S(1)} %shard_map.154), channel_id=1, replica_groups=mesh['slab_0'=8,'slab_1'=4,'slab_2'=2,'grp'=4] {'grp'}, dimensions={0} | all-to-all | bytes 425984 | tf_op jit(solution)/shard_map/all_to_all | solution.py:61
  157.6 0.8 maximum_add_fusion
  (96 shorter events, 5.8 us)
Async XLA Ops:
  0.6 0.9 copy-start.4
  1.5 0.9 copy-start.6
  2.4 0.9 copy-start.18
  3.3 0.8 copy-start.37
  4.1 0.8 copy-start.38
  6.1 5.1 %copy-start.40 = (f32[96,384]{1,0:T(8,128)S(1)}, f32[96,384]{1,0:T(8,128)}, u32[]{:S(2)}) copy-start(f32[96,384]{1,0:T(8,128)} %param.16) | copy-start | bytes 442372
  6.1 20.0 %copy-start.39 = (s32[1,128]{1,0:T(1,128)S(1)}, s32[1,128]{1,0:T(1,128)}, u32[]{:S(2)}) copy-start(s32[1,128]{1,0:T(1,128)} %index_ref.5) | copy-start | bytes 1540
  6.1 20.0 %all-to-all-start = ((f32[4,96,768]{2,1,0:T(8,128)}), f32[4,96,768]{2,1,0:T(8,128)S(1)}, u32[]{:S(2)}, u32[]{:S(2)}) async-start(f32[4,96,768]{2,1,0:T(8,128)} %shard_map.147), calls=%async_computation | async-start | bytes 2359296 | tf_op jit(solution)/shard_map/all_to_all | solution.py:61
  11.2 18.6 %copy-start.42 = (f32[96,128]{1,0:T(8,128)S(1)}, f32[96,128]{1,0:T(8,128)}, u32[]{:S(2)}) copy-start(f32[96,128]{1,0:T(8,128)} %param.17) | copy-start | bytes 147460
  11.2 22.3 %copy-start.43 = (f32[96,128]{1,0:T(8,128)S(1)}, f32[96,128]{1,0:T(8,128)}, u32[]{:S(2)}) copy-start(f32[96,128]{1,0:T(8,128)} %param.18) | copy-start | bytes 147460
  11.2 27.4 %copy-start.44 = (f32[96,96]{1,0:T(8,128)S(1)}, f32[96,96]{1,0:T(8,128)}, u32[]{:S(2)}) copy-start(f32[96,96]{1,0:T(8,128)} %param.20) | copy-start | bytes 110596
  27.8 23.8 %copy-start.9 = (f32[384,128]{1,0:T(8,128)}, f32[384,128]{1,0:T(8,128)S(1)}, u32[]{:S(2)}) copy-start(f32[384,128]{1,0:T(8,128)S(1)} %get-tuple-element.21.factor_ref) | copy-start | bytes 589828
  27.8 9.0 %collective-permute-start.7 = (f32[256,128]{1,0:T(8,128)S(1)}, f32[256,128]{1,0:T(8,128)S(1)}, u32[]{:S(2)}, u32[]{:S(2)}) collective-permute-start(f32[256,128]{1,0:T(8,128)S(1)} %get-tuple-element.27.m0), channel_id=1, source_target_pairs={{0,8},{8,16},{16,24},{24,0},{1,9},{9,17},{17,25},{25,1},{2,10},{10... | collective-permute-start | bytes 393224 | tf_op jit(solution)/shard_map/ppermute | solution.py:66
  29.8 9.2 %collective-permute-start.8 = (f32[256,128]{1,0:T(8,128)S(1)}, f32[256,128]{1,0:T(8,128)S(1)}, u32[]{:S(2)}, u32[]{:S(2)}) collective-permute-start(f32[256,128]{1,0:T(8,128)S(1)} %get-tuple-element.27.m0), channel_id=1, source_target_pairs={{0,16},{8,24},{16,0},{24,8},{1,17},{9,25},{17,1},{25,9},{2,18},{10... | collective-permute-start | bytes 393224 | tf_op jit(solution)/shard_map/ppermute | solution.py:66
  32.3 8.4 %collective-permute-start.9 = (f32[256,128]{1,0:T(8,128)S(1)}, f32[256,128]{1,0:T(8,128)S(1)}, u32[]{:S(2)}, u32[]{:S(2)}) collective-permute-start(f32[256,128]{1,0:T(8,128)S(1)} %get-tuple-element.27.m0), channel_id=1, source_target_pairs={{0,24},{8,0},{16,8},{24,16},{1,25},{9,1},{17,9},{25,17},{2,26},{10... | collective-permute-start | bytes 393224 | tf_op jit(solution)/shard_map/ppermute | solution.py:66
  33.5 8.0 %collective-permute-start.10 = (f32[256,128]{1,0:T(8,128)S(1)}, f32[256,128]{1,0:T(8,128)S(1)}, u32[]{:S(2)}, u32[]{:S(2)}) collective-permute-start(f32[256,128]{1,0:T(8,128)S(1)} %get-tuple-element.27.m0), channel_id=1, source_target_pairs={{0,4},{4,0},{1,5},{5,1},{2,6},{6,2},{3,7},{7,3},{8,12},{12,8},{9,1... | collective-permute-start | bytes 393224 | tf_op jit(solution)/shard_map/ppermute | solution.py:66
  36.9 7.2 %collective-permute-start.11 = (f32[256,128]{1,0:T(8,128)S(1)}, f32[256,128]{1,0:T(8,128)S(1)}, u32[]{:S(2)}, u32[]{:S(2)}) collective-permute-start(f32[256,128]{1,0:T(8,128)S(1)} %collective-permute-done.7.m1), channel_id=1, source_target_pairs={{0,4},{4,0},{1,5},{5,1},{2,6},{6,2},{3,7},{7,3},{8,12},{12,8},{9,1... | collective-permute-start | bytes 393224 | tf_op jit(solution)/shard_map/ppermute | solution.py:66
  38.6 24.6 %collective-permute-start = (f32[96,736]{1,0:T(8,128)S(1)}, f32[96,736]{1,0:T(8,128)S(1)}, u32[]{:S(2)}, u32[]{:S(2)}) collective-permute-start(f32[96,736]{1,0:T(8,128)S(1)} %constant_dynamic-update-slice_fusion.p0), channel_id=1, source_target_pairs={{0,1},{1,2},{2,3},{3,0},{4,5},{5,6},{6,7},{7,4},{8,9},{9,10},{10,1... | collective-permute-start | bytes 847880 | tf_op jit(solution)/shard_map/ppermute | solution.py:66
  39.0 25.7 %collective-permute-start.1 = (f32[96,736]{1,0:T(8,128)S(1)}, f32[96,736]{1,0:T(8,128)}, u32[]{:S(2)}, u32[]{:S(2)}) collective-permute-start(f32[96,736]{1,0:T(8,128)S(1)} %constant_dynamic-update-slice_fusion.p0), channel_id=1, source_target_pairs={{0,2},{1,3},{2,0},{3,1},{4,6},{5,7},{6,4},{7,5},{8,10},{9,11},{10,... | collective-permute-start | bytes 847880 | tf_op jit(solution)/shard_map/ppermute | solution.py:66
  40.8 23.9 %collective-permute-start.2 = (f32[96,736]{1,0:T(8,128)S(1)}, f32[96,736]{1,0:T(8,128)}, u32[]{:S(2)}, u32[]{:S(2)}) collective-permute-start(f32[96,736]{1,0:T(8,128)S(1)} %constant_dynamic-update-slice_fusion.p0), channel_id=1, source_target_pairs={{0,3},{1,0},{2,1},{3,2},{4,7},{5,4},{6,5},{7,6},{8,11},{9,8},{10,9... | collective-permute-start | bytes 847880 | tf_op jit(solution)/shard_map/ppermute | solution.py:66
  42.2 3.2 %collective-permute-start.12 = (f32[256,128]{1,0:T(8,128)S(1)}, f32[256,128]{1,0:T(8,128)S(1)}, u32[]{:S(2)}, u32[]{:S(2)}) collective-permute-start(f32[256,128]{1,0:T(8,128)S(1)} %collective-permute-done.8.m2), channel_id=1, source_target_pairs={{0,4},{4,0},{1,5},{5,1},{2,6},{6,2},{3,7},{7,3},{8,12},{12,8},{9,1... | collective-permute-start | bytes 393224 | tf_op jit(solution)/shard_map/ppermute | solution.py:66
  43.4 0.7 copy-start.23
  44.7 4.2 %collective-permute-start.13 = (f32[256,128]{1,0:T(8,128)S(1)}, f32[256,128]{1,0:T(8,128)S(1)}, u32[]{:S(2)}, u32[]{:S(2)}) collective-permute-start(f32[256,128]{1,0:T(8,128)S(1)} %collective-permute-done.9.m3), channel_id=1, source_target_pairs={{0,4},{4,0},{1,5},{5,1},{2,6},{6,2},{3,7},{7,3},{8,12},{12,8},{9,1... | collective-permute-start | bytes 393224 | tf_op jit(solution)/shard_map/ppermute | solution.py:66
  45.4 0.7 copy-start.31
  46.0 18.7 %collective-permute-start.3 = (f32[64,128]{1,0:T(8,128)}, f32[64,128]{1,0:T(8,128)}, u32[]{:S(2)}, u32[]{:S(2)}) collective-permute-start(f32[64,128]{1,0:T(8,128)} %get-tuple-element.22), channel_id=1, source_target_pairs={{0,4},{4,8},{8,12},{12,16},{16,20},{20,24},{24,28},{28,32},{32,36}... | collective-permute-start | bytes 98312 | tf_op jit(solution)/shard_map/ppermute | solution.py:71
  49.6 15.1 %collective-permute-start.4 = (f32[64,128]{1,0:T(8,128)}, f32[64,128]{1,0:T(8,128)}, u32[]{:S(2)}, u32[]{:S(2)}) collective-permute-start(f32[64,128]{1,0:T(8,128)} %get-tuple-element.22), channel_id=1, source_target_pairs={{4,0},{8,4},{12,8},{16,12},{20,16},{24,20},{28,24},{32,28},{36,32}... | collective-permute-start | bytes 98312 | tf_op jit(solution)/shard_map/ppermute | solution.py:72
  51.6 0.9 copy-start.20
  52.5 0.9 copy-start.22
  53.4 0.9 copy-start.24
  54.3 0.9 copy-start.26
  55.2 0.9 copy-start.28
  56.2 0.9 copy-start.30
  57.1 0.9 copy-start.32
  58.0 0.9 copy-start.34
  62.2 1.0 copy-start
  63.2 27.5 %collective-permute-start.14 = (f32[384,128]{1,0:T(8,128)}, f32[384,128]{1,0:T(8,128)}, u32[]{:S(2)}, u32[]{:S(2)}) collective-permute-start(f32[384,128]{1,0:T(8,128)} %get-tuple-element.32.a0), channel_id=1, source_target_pairs={{0,32},{32,64},{64,96},{96,128},{128,160},{160,192},{192,224},{224... | collective-permute-start | bytes 589832 | tf_op jit(solution)/shard_map/ppermute | solution.py:66
  64.7 11.5 %copy-start.10 = (f32[384,128]{1,0:T(8,128)S(1)}, f32[384,128]{1,0:T(8,128)}, u32[]{:S(2)}) copy-start(f32[384,128]{1,0:T(8,128)} %copy-done.9) | copy-start | bytes 589828
  66.7 11.8 %copy-start.2 = (f32[384,128]{1,0:T(8,128)}, f32[384,128]{1,0:T(8,128)S(1)}, u32[]{:S(2)}) copy-start(f32[384,128]{1,0:T(8,128)S(1)} %get-tuple-element.24.s_ref) | copy-start | bytes 589828
  66.7 6.9 %collective-permute-start.5 = (f32[128,128]{1,0:T(8,128)S(1)}, f32[128,128]{1,0:T(8,128)S(1)}, u32[]{:S(2)}, u32[]{:S(2)}) collective-permute-start(f32[128,128]{1,0:T(8,128)S(1)} %get-tuple-element.25), channel_id=1, source_target_pairs={{0,4},{4,8},{8,12},{12,16},{16,20},{20,24},{24,28},{28,32},{32,36}... | collective-permute-start | bytes 196616 | tf_op jit(solution)/shard_map/ppermute | solution.py:71
  70.7 5.6 %collective-permute-start.6 = (f32[128,128]{1,0:T(8,128)S(1)}, f32[128,128]{1,0:T(8,128)S(1)}, u32[]{:S(2)}, u32[]{:S(2)}) collective-permute-start(f32[128,128]{1,0:T(8,128)S(1)} %get-tuple-element.25), channel_id=1, source_target_pairs={{4,0},{8,4},{12,8},{16,12},{20,16},{24,20},{28,24},{32,28},{36,32}... | collective-permute-start | bytes 196616 | tf_op jit(solution)/shard_map/ppermute | solution.py:72
  78.6 0.7 copy-start.8
  79.2 0.7 copy-start.11
  79.9 15.5 %all-to-all-start.1 = ((f32[8,56,128]{2,1,0:T(8,128)}), f32[8,56,128]{2,1,0:T(8,128)S(1)}, u32[]{:S(2)}, u32[]{:S(2)}) async-start(f32[8,56,128]{2,1,0:T(8,128)} %copy-done.8), calls=%async_computation.1 | async-start | bytes 458752 | tf_op jit(solution)/shard_map/all_to_all | solution.py:61
  89.3 18.6 %collective-permute-start.18 = (f32[384,128]{1,0:T(8,128)}, f32[384,128]{1,0:T(8,128)S(1)}, u32[]{:S(2)}, u32[]{:S(2)}) collective-permute-start(f32[384,128]{1,0:T(8,128)} %get-tuple-element.32.a0), channel_id=1, source_target_pairs={{0,224},{32,0},{64,32},{96,64},{128,96},{160,128},{192,160},{224,1... | collective-permute-start | bytes 589832 | tf_op jit(solution)/shard_map/ppermute | solution.py:66
  90.7 20.6 %collective-permute-start.15 = (f32[384,128]{1,0:T(8,128)}, f32[384,128]{1,0:T(8,128)}, u32[]{:S(2)}, u32[]{:S(2)}) collective-permute-start(f32[384,128]{1,0:T(8,128)} %collective-permute-done.14.a1), channel_id=1, source_target_pairs={{0,32},{32,64},{64,96},{96,128},{128,160},{160,192},{192,224},{224... | collective-permute-start | bytes 589832 | tf_op jit(solution)/shard_map/ppermute | solution.py:66
  95.5 1.2 copy-start.1
  100.6 21.5 %all-to-all-start.2 = ((f32[8,72,128]{2,1,0:T(8,128)}), f32[8,72,128]{2,1,0:T(8,128)S(1)}, u32[]{:S(2)}, u32[]{:S(2)}) async-start(f32[8,72,128]{2,1,0:T(8,128)} %get-tuple-element.31), calls=%async_computation.2 | async-start | bytes 589824 | tf_op jit(solution)/shard_map/all_to_all | solution.py:61
  107.9 12.2 %collective-permute-start.19 = (f32[384,128]{1,0:T(8,128)S(1)}, f32[384,128]{1,0:T(8,128)}, u32[]{:S(2)}, u32[]{:S(2)}) collective-permute-start(f32[384,128]{1,0:T(8,128)S(1)} %collective-permute-done.18.b1), channel_id=1, source_target_pairs={{0,224},{32,0},{64,32},{96,64},{128,96},{160,128},{192,160},{224,1... | collective-permute-start | bytes 589832 | tf_op jit(solution)/shard_map/ppermute | solution.py:66
  110.6 0.7 copy-start.13
  111.3 10.8 %collective-permute-start.16 = (f32[384,128]{1,0:T(8,128)}, f32[384,128]{1,0:T(8,128)}, u32[]{:S(2)}, u32[]{:S(2)}) collective-permute-start(f32[384,128]{1,0:T(8,128)} %collective-permute-done.15.a2), channel_id=1, source_target_pairs={{0,32},{32,64},{64,96},{96,128},{128,160},{160,192},{192,224},{224... | collective-permute-start | bytes 589832 | tf_op jit(solution)/shard_map/ppermute | solution.py:66
  120.1 5.1 %collective-permute-start.20 = (f32[384,128]{1,0:T(8,128)}, f32[384,128]{1,0:T(8,128)S(1)}, u32[]{:S(2)}, u32[]{:S(2)}) collective-permute-start(f32[384,128]{1,0:T(8,128)} %collective-permute-done.19.b2), channel_id=1, source_target_pairs={{0,224},{32,0},{64,32},{96,64},{128,96},{160,128},{192,160},{224,1... | collective-permute-start | bytes 589832 | tf_op jit(solution)/shard_map/ppermute | solution.py:66
  122.1 6.5 %collective-permute-start.17 = (f32[384,128]{1,0:T(8,128)}, f32[384,128]{1,0:T(8,128)}, u32[]{:S(2)}, u32[]{:S(2)}) collective-permute-start(f32[384,128]{1,0:T(8,128)} %collective-permute-done.16.a3), channel_id=1, source_target_pairs={{0,32},{32,64},{64,96},{96,128},{128,160},{160,192},{192,224},{224... | collective-permute-start | bytes 589832 | tf_op jit(solution)/shard_map/ppermute | solution.py:66
  125.2 0.7 copy-start.15
  128.6 0.9 copy-start.14
  129.5 0.9 copy-start.16
  130.4 0.8 copy-start.36
  131.3 9.9 %copy-start.45 = (f32[256]{0:T(256)S(1)}, f32[256]{0:T(256)}, u32[]{:S(2)}) copy-start(f32[256]{0:T(256)} %param.15) | copy-start | bytes 3076
  131.3 15.5 %copy-start.3 = (f32[384,128]{1,0:T(8,128)S(1)}, f32[384,128]{1,0:T(8,128)}, u32[]{:S(2)}) copy-start(f32[384,128]{1,0:T(8,128)} %copy-done.2) | copy-start | bytes 589828
  134.9 0.7 copy-start.17
  135.5 11.2 %all-to-all-start.3 = ((f32[8,40,128]{2,1,0:T(8,128)}), f32[8,40,128]{2,1,0:T(8,128)S(1)}, u32[]{:S(2)}, u32[]{:S(2)}) async-start(f32[8,40,128]{2,1,0:T(8,128)} %copy-done.17), calls=%async_computation.3 | async-start | bytes 327680 | tf_op jit(solution)/shard_map/all_to_all | solution.py:61
  146.8 0.9 copy-start.12
  147.7 9.9 %copy-start.5 = (f32[96,256]{1,0:T(8,128)S(1)}, f32[96,256]{1,0:T(8,128)}, u32[]{:S(2)}) copy-start(f32[96,256]{1,0:T(8,128)} %direction_ref.1) | copy-start | bytes 294916
  147.7 9.9 %copy-start.7 = (f32[96,256]{1,0:T(8,128)S(1)}, f32[96,256]{1,0:T(8,128)}, u32[]{:S(2)}) copy-start(f32[96,256]{1,0:T(8,128)} %residual_ref.1) | copy-start | bytes 294916
  147.7 9.9 %copy-start.41 = (f32[96,256]{1,0:T(8,128)S(1)}, f32[96,256]{1,0:T(8,128)}, u32[]{:S(2)}) copy-start(f32[96,256]{1,0:T(8,128)} %param.12) | copy-start | bytes 294916
  (7 other events, 4.5 us)
where the time goes:
time: 160 us; the launch traced here: 158 us
  starting transfers between devices  60.7 us (38%)
  waiting for transfers between devices  42.2 us (26%)
  local copies, waits for them, and re-layouts  26.9 us (17%)
  Pallas kernels  18.2 us (11%)
  blocking collectives  8.19 us (5%)
    all_to_all x4, starting transfers between devices, to_each(): return lax.all_to_all(pieces, axes, split_axis=0, concat_axis=0, tiled=True)  27.5 us
    unnamed x95, local copies, waits for them, and re-layouts  26.6 us
    all_to_all x4, waiting for transfers between devices, to_each(): return lax.all_to_all(pieces, axes, split_axis=0, concat_axis=0, tiled=True)  24.8 us
    ppermute x17, starting transfers between devices, ring(): lax.ppermute(x, axis, [(i, (i + step) % count) for i in range(count)])  21.4 us
    pallas_call x8, Pallas kernels, call(): pl.pallas_call(body, out_shape=outs, in_specs=[SMEM] * smem + [VMEM] * (l...  18.2 us
    ppermute x17, waiting for transfers between devices, ring(): lax.ppermute(x, axis, [(i, (i + step) % count) for i in range(count)])  14.7 us
    all_to_all x1, blocking collectives, to_each(): return lax.all_to_all(pieces, axes, split_axis=0, concat_axis=0, tiled=True)  8.19 us
    ppermute x2, starting transfers between devices, beside(): below = lax.ppermute(faces, SLAB, [(i, i + 1) for i in range(count - 1)])  6.78 us
  transfers between devices with their start and end apart: 25, of which 8 were waited for; matrix products, arithmetic and copies ran while one was open for 0% of the time, Pallas kernels for 7%

commit v1 on v0

--- a/solution.py
+++ b/solution.py
@@ -55,6 +55,10 @@
         scratch_shapes=list(scratch),
         compiler_params=pltpu.CompilerParams(vmem_limit_bytes=16 * 1024 * 1024),
     )(*args)
+
+
+def far(x):
+    return pltpu.with_memory_space_constraint(x, pltpu.HBM)
 
 
 def to_each(pieces, axes):
@@ -328,11 +332,20 @@
     def here(axes):
         return lax.axis_index(axes).astype(jnp.int32).reshape(1)
 
-    grp = here("grp")
     part = 64
+    grp, at_x, at_c, at_z, place = (here(axes) for axes in ("grp", "slab_1", "slab_2", "slab_0", PLANE))
+    own_rho = lax.dynamic_slice_in_dim(prior_rho, part * grp[0], part).reshape(1, part)
+    grp, at_x, at_c, at_z, place, own_rho, direction, residual = lax.optimization_barrier(
+        (grp, at_x, at_c, at_z, place, own_rho, direction, residual)
+    )
     operator = jnp.concatenate([diag_blocks, lower_coupling, upper_coupling, jacobi_inverse], axis=1)
     got = to_each(
-        call(pack, shaped(4, 96, 768), 0, direction, residual, slab_inverse, lower_factor, upper_factor),
+        call(
+            pack,
+            shaped(4, 96, 768),
+            0,
+            *(far(a) for a in (direction, residual, slab_inverse, lower_factor, upper_factor)),
+        ),
         "grp",
     ).reshape(384, 768)
     pieces = [operator] + [ring(operator, "grp", step) for step in (1, 2, 3)]
@@ -383,8 +396,8 @@
             shaped(384, 128),
         ),
         2,
-        here("slab_1"),
-        here("slab_2"),
+        at_x,
+        at_c,
         *along,
         *across,
         scratch=[pltpu.VMEM((8, 256, 128), jnp.float32), pltpu.VMEM((8, 128, 128), jnp.float32)],
@@ -395,14 +408,13 @@
     downs = [plane]
     for _ in range(1, 4):
         downs.append(ring(downs[-1], "slab_0", -1))
-    place = here(PLANE)
     own_f, own_b, sums = call(
         sweep_plane,
         (shaped(9, 16, 128), shaped(8, 16, 128), shaped(8, 72, 128)),
         1,
         place,
         to_each(sent, PLANE),
-        maps,
+        far(maps),
         states_f,
         states_b,
     )
@@ -410,22 +422,22 @@
         solve_planes,
         (shaped(8, 40, 128), shaped(8, 128)),
         2,
-        here("slab_0"),
+        at_z,
         place,
         to_each(sums, "slab_0"),
-        *ups,
+        *ups[:4],
+        far(ups[4]),
         *downs[1:],
         states_f,
         states_b,
-        own_f,
-        own_b,
+        far(own_f),
+        far(own_b),
         scratch=[
             pltpu.VMEM((8, 384, 128), jnp.float32),
             pltpu.VMEM((8, 16, 128), jnp.float32),
             pltpu.VMEM((8, 16, 128), jnp.float32),
         ],
     )
-    own_rho = lax.dynamic_slice_in_dim(prior_rho, part * grp[0], part).reshape(1, part)
     out = to_each(
         call(
             finish,

time: 160 us -> 144 us (0.900)
  local copies, waits for them, and re-layouts: 26.9 us -> 5.34 us
  blocking collectives: 8.19 us -> 19.9 us
  waiting for transfers between devices: 42.2 us -> 35.5 us
    unnamed x95 -> x35, local copies, waits for them, and re-layouts: 26.6 us -> 4.4 us
    all_to_all x1 -> x2, blocking collectives: 8.19 us -> 19.9 us  [to_each(): return lax.all_to_all(pieces, axes, split_axis=0, concat_axis=0, tiled=True)]
    all_to_all x4 -> x3, waiting for transfers between devices: 24.8 us -> 14.9 us  [to_each(): return lax.all_to_all(pieces, axes, split_axis=0, concat_axis=0, tiled=True)]
    ppermute x17, starting transfers between devices: 21.4 us -> 28.3 us  [ring(): lax.ppermute(x, axis, [(i, (i + step) % count) for i in range(count)])]
    all_to_all x4 -> x3, starting transfers between devices: 27.5 us -> 22.4 us  [to_each(): return lax.all_to_all(pieces, axes, split_axis=0, concat_axis=0, tiled=True)]
    ppermute x17, waiting for transfers between devices: 14.7 us -> 19.3 us  [ring(): lax.ppermute(x, axis, [(i, (i + step) % count) for i in range(count)])]
    ppermute x2, waiting for transfers between devices: 2.62 us -> 0.41 us  [beside(): above = lax.ppermute(faces, SLAB, [(i + 1, i) for i in range(count - 1)])]
  transfers between devices with their start and end apart: 25 -> 24, of which waited for: 8 -> 9; matrix products, arithmetic and copies ran while one was open for 0% -> 0% of each run, Pallas kernels for 7% -> 7%
where the time goes in v1:
time: 144 us; the launch traced here: 143 us
  starting transfers between devices  61.7 us (43%)
  waiting for transfers between devices  35.5 us (25%)
  blocking collectives  19.9 us (14%)
  Pallas kernels  18.2 us (13%)
  local copies, waits for them, and re-layouts  5.34 us (4%)
  other arithmetic  1.46 us (1%)
    ppermute x17, starting transfers between devices, ring(): lax.ppermute(x, axis, [(i, (i + step) % count) for i in range(count)])  28.3 us
    all_to_all x3, starting transfers between devices, to_each(): return lax.all_to_all(pieces, axes, split_axis=0, concat_axis=0, tiled=True)  22.4 us
    all_to_all x2, blocking collectives, to_each(): return lax.all_to_all(pieces, axes, split_axis=0, concat_axis=0, tiled=True)  19.9 us
    ppermute x17, waiting for transfers between devices, ring(): lax.ppermute(x, axis, [(i, (i + step) % count) for i in range(count)])  19.3 us
    pallas_call x8, Pallas kernels, call(): pl.pallas_call(body, out_shape=outs, in_specs=[SMEM] * smem + [VMEM] * (l...  18.2 us
    all_to_all x3, waiting for transfers between devices, to_each(): return lax.all_to_all(pieces, axes, split_axis=0, concat_axis=0, tiled=True)  14.9 us
    ppermute x2, starting transfers between devices, beside(): below = lax.ppermute(faces, SLAB, [(i, i + 1) for i in range(count - 1)])  6.45 us
    ppermute x2, starting transfers between devices, beside(): above = lax.ppermute(faces, SLAB, [(i + 1, i) for i in range(count - 1)])  4.66 us
  transfers between devices with their start and end apart: 24, of which 9 were waited for; matrix products, arithmetic and copies ran while one was open for 0% of the time, Pallas kernels for 7%

profile of v1, /device:TPU:1, one launch (start us, length us, event | category | flops | bytes accessed | tf_op | source)
XLA Modules:
  0.0 143.0 jit_solution(1213715820253677898)
XLA Ops:
  0.6 0.8 dynamic-slice_bitcast_fusion.rho_ref
  1.4 2.2 %shard_map.147 = f32[4,96,768]{2,1,0:T(8,128)} custom-call(f32[96,256]{1,0:T(8,128)} %direction_ref, f32[96,256]{1,0:T(8,128)} %residual_ref, f32[96,384]{1,0:T(8,128)} %inverse_ref.1, f32[96,128]{1,0:T(8,128)} %lower_ref.1, f32[96,128]{1,0:T(8,128)} %upper_ref.1), custom_call_target="tpu_custom_call" | custom-call | tf_op jit(solution)/shard_map/pallas_call | solution.py:50
  3.6 5.1 %all-to-all-start = ((f32[4,96,768]{2,1,0:T(8,128)}), f32[4,96,768]{2,1,0:T(8,128)S(1)}, u32[]{:S(2)}, u32[]{:S(2)}) async-start(f32[4,96,768]{2,1,0:T(8,128)} %shard_map.147), calls=%async_computation | async-start | bytes 2359296 | tf_op jit(solution)/shard_map/all_to_all | solution.py:65
  8.8 0.0 copy-start.14
  8.8 14.9 %all-to-all-done = f32[4,96,768]{2,1,0:T(8,128)S(1)} async-done(((f32[4,96,768]{2,1,0:T(8,128)}), f32[4,96,768]{2,1,0:T(8,128)S(1)}, u32[]{:S(2)}, u32[]{:S(2)}) %all-to-all-start) | async-done | bytes 1179680 | tf_op jit(solution)/shard_map/all_to_all | solution.py:65
  23.7 1.1 shard_map.148
  24.8 3.3 %collective-permute-start.9 = (f32[256,128]{1,0:T(8,128)S(1)}, f32[256,128]{1,0:T(8,128)S(1)}, u32[]{:S(2)}, u32[]{:S(2)}) collective-permute-start(f32[256,128]{1,0:T(8,128)S(1)} %get-tuple-element.42.m0), channel_id=1, source_target_pairs={{0,24},{8,0},{16,8},{24,16},{1,25},{9,1},{17,9},{25,17},{2,26},{10... | collective-permute-start | bytes 393224 | tf_op jit(solution)/shard_map/ppermute | solution.py:70
  28.1 2.2 %collective-permute-start.10 = (f32[256,128]{1,0:T(8,128)S(1)}, f32[256,128]{1,0:T(8,128)S(1)}, u32[]{:S(2)}, u32[]{:S(2)}) collective-permute-start(f32[256,128]{1,0:T(8,128)S(1)} %get-tuple-element.42.m0), channel_id=1, source_target_pairs={{0,4},{4,0},{1,5},{5,1},{2,6},{6,2},{3,7},{7,3},{8,12},{12,8},{9,1... | collective-permute-start | bytes 393224 | tf_op jit(solution)/shard_map/ppermute | solution.py:70
  30.3 0.5 collective-permute-start.8
  30.8 0.7 collective-permute-start.7
  31.5 0.0 collective-permute-done.9.m3
  31.5 4.0 %collective-permute-start.13 = (f32[256,128]{1,0:T(8,128)S(1)}, f32[256,128]{1,0:T(8,128)S(1)}, u32[]{:S(2)}, u32[]{:S(2)}) collective-permute-start(f32[256,128]{1,0:T(8,128)S(1)} %collective-permute-done.9.m3), channel_id=1, source_target_pairs={{0,4},{4,0},{1,5},{5,1},{2,6},{6,2},{3,7},{7,3},{8,12},{12,8},{9,1... | collective-permute-start | bytes 393224 | tf_op jit(solution)/shard_map/ppermute | solution.py:70
  35.5 1.0 collective-permute-start.2
  36.5 0.0 collective-permute-done.10.n0
  36.5 1.2 collective-permute-start.1
  37.6 0.0 collective-permute-done.8.m2
  37.7 0.0 collective-permute-start
  37.7 2.3 %collective-permute-done.7.m1 = f32[256,128]{1,0:T(8,128)S(1)} collective-permute-done((f32[256,128]{1,0:T(8,128)S(1)}, f32[256,128]{1,0:T(8,128)S(1)}, u32[]{:S(2)}, u32[]{:S(2)}) %collective-permute-start.7) | collective-permute-done | bytes 131104 | tf_op jit(solution)/shard_map/ppermute | solution.py:70
  40.0 0.5 collective-permute-start.12
  40.5 0.0 collective-permute-start.11
  40.5 0.9 collective-permute-done.12.n2
  41.5 2.3 %collective-permute-start.4 = (f32[64,128]{1,0:T(8,128)S(1)}, f32[64,128]{1,0:T(8,128)S(1)}, u32[]{:S(2)}, u32[]{:S(2)}) collective-permute-start(f32[64,128]{1,0:T(8,128)S(1)} %get-tuple-element.35), channel_id=1, source_target_pairs={{4,0},{8,4},{12,8},{16,12},{20,16},{24,20},{28,24},{32,28},{36,32}... | collective-permute-start | bytes 98312 | tf_op jit(solution)/shard_map/ppermute | solution.py:76
  43.7 3.3 %collective-permute-start.3 = (f32[64,128]{1,0:T(8,128)S(1)}, f32[64,128]{1,0:T(8,128)S(1)}, u32[]{:S(2)}, u32[]{:S(2)}) collective-permute-start(f32[64,128]{1,0:T(8,128)S(1)} %get-tuple-element.35), channel_id=1, source_target_pairs={{0,4},{4,8},{8,12},{12,16},{16,20},{20,24},{24,28},{28,32},{32,36}... | collective-permute-start | bytes 98312 | tf_op jit(solution)/shard_map/ppermute | solution.py:75
  47.0 3.3 %shard_map.151 = (bf16[2,8,256,128]{3,2,1,0:T(8,128)(2,1)S(1)}, bf16[2,8,128,128]{3,2,1,0:T(8,128)(2,1)S(1)}, bf16[2,8,256,128]{3,2,1,0:T(8,128)(2,1)S(1)}, f32[384,128]{1,0:T(8,128)}) custom-call(s32[1]{0:T(128)} %bitcast.1.x_ref, s32[1]{0:T(128)} %bitcast.2.c_ref, f32[256,128]{1,0:T(8,128)S(1)} %get-tuple-element.42.m0, ...), custom_call_target="tpu_custom_call" | custom-call | tf_op jit(solution)/shard_map/pallas_call | solution.py:50
  50.4 1.0 copy-done
  51.4 0.0 collective-permute-done.2.p3
  51.4 1.6 %collective-permute-start.14 = (f32[384,128]{1,0:T(8,128)}, f32[384,128]{1,0:T(8,128)}, u32[]{:S(2)}, u32[]{:S(2)}) collective-permute-start(f32[384,128]{1,0:T(8,128)} %get-tuple-element.47.a0), channel_id=1, source_target_pairs={{0,32},{32,64},{64,96},{96,128},{128,160},{160,192},{192,224},{224... | collective-permute-start | bytes 589832 | tf_op jit(solution)/shard_map/ppermute | solution.py:70
  53.0 0.0 collective-permute-done.1.p2
  53.0 0.2 collective-permute-done.p1
  53.2 0.0 collective-permute-done.4.above_ref
  53.2 1.4 shard_map.149
  54.7 2.4 %collective-permute-start.6 = (f32[128,128]{1,0:T(8,128)S(1)}, f32[128,128]{1,0:T(8,128)S(1)}, u32[]{:S(2)}, u32[]{:S(2)}) collective-permute-start(f32[128,128]{1,0:T(8,128)S(1)} %get-tuple-element.38), channel_id=1, source_target_pairs={{4,0},{8,4},{12,8},{16,12},{20,16},{24,20},{28,24},{32,28},{36,32}... | collective-permute-start | bytes 196616 | tf_op jit(solution)/shard_map/ppermute | solution.py:76
  57.1 3.2 %collective-permute-start.5 = (f32[128,128]{1,0:T(8,128)S(1)}, f32[128,128]{1,0:T(8,128)S(1)}, u32[]{:S(2)}, u32[]{:S(2)}) collective-permute-start(f32[128,128]{1,0:T(8,128)S(1)} %get-tuple-element.38), channel_id=1, source_target_pairs={{0,4},{4,8},{8,12},{12,16},{16,20},{20,24},{24,28},{28,32},{32,36}... | collective-permute-start | bytes 196616 | tf_op jit(solution)/shard_map/ppermute | solution.py:75
  60.2 0.4 collective-permute-done.6.above_ref
  60.6 0.9 collective-permute-done.5.below_ref
  61.6 1.8 %shard_map.150 = (f32[384,128]{1,0:T(8,128)S(1)}, f32[8,56,128]{2,1,0:T(8,128)S(1)}) custom-call(s32[1,128]{1,0:T(1,128)S(1)} %copy-done.7, s32[1]{0:T(128)} %bitcast.grp_ref, f32[384,768]{1,0:T(8,128)S(1)} %bitcast.42, f32[96,736]{1,0:T(8,128)S(1)} %constant_dynamic-update-slice_fusion.p0, f32[96,736]{1,0:T(8,128)S(1)} %collective-permute-done.p1, ...), custom_call_target="tpu_custom_call" | custom-call | tf_op jit(solution)/shard_map/pallas_call | solution.py:50
  63.3 0.7 copy-done.2
  64.0 0.7 copy-done.3
  64.7 7.2 %all-to-all-start.1 = ((f32[8,56,128]{2,1,0:T(8,128)}), f32[8,56,128]{2,1,0:T(8,128)S(1)}, u32[]{:S(2)}, u32[]{:S(2)}) async-start(f32[8,56,128]{2,1,0:T(8,128)} %copy-done.2), calls=%async_computation.1 | async-start | bytes 458752 | tf_op jit(solution)/shard_map/all_to_all | solution.py:65
  71.9 8.7 %collective-permute-start.18 = (f32[384,128]{1,0:T(8,128)}, f32[384,128]{1,0:T(8,128)}, u32[]{:S(2)}, u32[]{:S(2)}) collective-permute-start(f32[384,128]{1,0:T(8,128)} %get-tuple-element.47.a0), channel_id=1, source_target_pairs={{0,224},{32,0},{64,32},{96,64},{128,96},{160,128},{192,160},{224,1... | collective-permute-start | bytes 589832 | tf_op jit(solution)/shard_map/ppermute | solution.py:70
  80.5 0.0 collective-permute-done.14.a1
  80.5 0.0 collective-permute-start.15
  80.5 0.0 all-to-all-done.1.got_ref
  80.5 3.8 %shard_map.152 = (f32[9,16,128]{2,1,0:T(8,128)S(1)}, f32[8,16,128]{2,1,0:T(8,128)S(1)}, f32[8,72,128]{2,1,0:T(8,128)S(1)}) custom-call(s32[1]{0:T(128)} %bitcast.4.place_ref, f32[8,56,128]{2,1,0:T(8,128)S(1)} %all-to-all-done.1.got_ref, bf16[2,8,256,128]{3,2,1,0:T(8,128)(2,1)} %copy-done, bf16[2,8,128,128]{3,2,1,0:T(8,128)(2,1)S(1)} %get-tuple-element.44.states_f_ref, ...), custom_call_target="tpu_custom_call" | custom-call | tf_op jit(solution)/shard_map/pallas_call | solution.py:50
  84.3 0.0 copy-start.1
  84.3 0.7 copy-done.1
  85.0 0.6 copy-done.5
  85.7 0.6 copy-done.6
  86.3 10.1 %all-to-all-start.2 = ((f32[8,72,128]{2,1,0:T(8,128)}), f32[8,72,128]{2,1,0:T(8,128)S(1)}, u32[]{:S(2)}, u32[]{:S(2)}) async-start(f32[8,72,128]{2,1,0:T(8,128)} %copy-done.1), calls=%async_computation.2 | async-start | bytes 589824 | tf_op jit(solution)/shard_map/all_to_all | solution.py:65
  96.4 2.7 %collective-permute-start.19 = (f32[384,128]{1,0:T(8,128)}, f32[384,128]{1,0:T(8,128)}, u32[]{:S(2)}, u32[]{:S(2)}) collective-permute-start(f32[384,128]{1,0:T(8,128)} %collective-permute-done.18.b1), channel_id=1, source_target_pairs={{0,224},{32,0},{64,32},{96,64},{128,96},{160,128},{192,160},{224,1... | collective-permute-start | bytes 589832 | tf_op jit(solution)/shard_map/ppermute | solution.py:70
  99.1 0.0 collective-permute-done.15.a2
  99.1 9.5 %collective-permute-done.19.b2 = f32[384,128]{1,0:T(8,128)} collective-permute-done((f32[384,128]{1,0:T(8,128)}, f32[384,128]{1,0:T(8,128)}, u32[]{:S(2)}, u32[]{:S(2)}) %collective-permute-start.19) | collective-permute-done | bytes 196640 | tf_op jit(solution)/shard_map/ppermute | solution.py:70
  108.5 1.9 %collective-permute-start.20 = (f32[384,128]{1,0:T(8,128)}, f32[384,128]{1,0:T(8,128)}, u32[]{:S(2)}, u32[]{:S(2)}) collective-permute-start(f32[384,128]{1,0:T(8,128)} %collective-permute-done.19.b2), channel_id=1, source_target_pairs={{0,224},{32,0},{64,32},{96,64},{128,96},{160,128},{192,160},{224,1... | collective-permute-start | bytes 589832 | tf_op jit(solution)/shard_map/ppermute | solution.py:70
  110.5 3.2 %collective-permute-done.20.b3 = f32[384,128]{1,0:T(8,128)} collective-permute-done((f32[384,128]{1,0:T(8,128)}, f32[384,128]{1,0:T(8,128)}, u32[]{:S(2)}, u32[]{:S(2)}) %collective-permute-start.20) | collective-permute-done | bytes 196640 | tf_op jit(solution)/shard_map/ppermute | solution.py:70
  113.7 3.1 %collective-permute-done.17.a4 = f32[384,128]{1,0:T(8,128)} collective-permute-done((f32[384,128]{1,0:T(8,128)}, f32[384,128]{1,0:T(8,128)}, u32[]{:S(2)}, u32[]{:S(2)}) %collective-permute-start.17) | collective-permute-done | bytes 196640 | tf_op jit(solution)/shard_map/ppermute | solution.py:70
  116.8 3.7 %shard_map.153 = (f32[8,40,128]{2,1,0:T(8,128)S(1)}, f32[8,128]{1,0:T(8,128)S(1)}) custom-call(s32[1]{0:T(128)} %bitcast.3.z_ref, s32[1]{0:T(128)} %bitcast.4.place_ref, f32[8,72,128]{2,1,0:T(8,128)S(1)} %all-to-all-done.2.sums_ref, f32[384,128]{1,0:T(8,128)} %get-tuple-element.47.a0, f32[384,128]{1,0:T(8,128)} %collective-permute-done.14.a1, ...), custom_call_target="tpu_custom_call" | custom-call | tf_op jit(solution)/shard_map/pallas_call | solution.py:50
  120.5 10.4 %all_to_all.25.back_ref = f32[8,40,128]{2,1,0:T(8,128)S(1)} all-to-all(f32[8,40,128]{2,1,0:T(8,128)S(1)} %get-tuple-element.50), channel_id=1, replica_groups=mesh['slab_0'=8,'slab_1'=4,'slab_2'=2,'grp'=4] {'slab_1','slab_2'}, dimensions={0} | all-to-all | bytes 327680 | tf_op jit(solution)/shard_map/all_to_all | solution.py:65
  131.0 0.0 copy-start.11
  131.0 0.9 shard_map.154
  131.9 9.5 %all_to_all.26 = f32[4,104,128]{2,1,0:T(8,128)S(1)} all-to-all(f32[4,104,128]{2,1,0:T(8,128)S(1)} %shard_map.154), channel_id=1, replica_groups=mesh['slab_0'=8,'slab_1'=4,'slab_2'=2,'grp'=4] {'grp'}, dimensions={0} | all-to-all | bytes 425984 | tf_op jit(solution)/shard_map/all_to_all | solution.py:65
  141.3 0.1 slice_bitcast_fusion.11
  141.4 0.6 fusion.1
  142.1 0.1 slice_bitcast_fusion.3
  142.2 0.8 maximum_add_fusion
  (35 shorter events, 0.1 us)
Async XLA Ops:
  3.6 5.1 %copy-start.10 = (f32[96,384]{1,0:T(8,128)S(1)}, f32[96,384]{1,0:T(8,128)}, u32[]{:S(2)}) copy-start(f32[96,384]{1,0:T(8,128)} %param.16) | copy-start | bytes 442372
  3.6 20.0 %copy-start.7 = (s32[1,128]{1,0:T(1,128)S(1)}, s32[1,128]{1,0:T(1,128)}, u32[]{:S(2)}) copy-start(s32[1,128]{1,0:T(1,128)} %index_ref.5) | copy-start | bytes 1540
  3.6 20.0 %all-to-all-start = ((f32[4,96,768]{2,1,0:T(8,128)}), f32[4,96,768]{2,1,0:T(8,128)S(1)}, u32[]{:S(2)}, u32[]{:S(2)}) async-start(f32[4,96,768]{2,1,0:T(8,128)} %shard_map.147), calls=%async_computation | async-start | bytes 2359296 | tf_op jit(solution)/shard_map/all_to_all | solution.py:65
  8.8 19.3 %copy-start.12 = (f32[96,128]{1,0:T(8,128)S(1)}, f32[96,128]{1,0:T(8,128)}, u32[]{:S(2)}) copy-start(f32[96,128]{1,0:T(8,128)} %param.17) | copy-start | bytes 147460
  8.8 22.0 %copy-start.13 = (f32[96,128]{1,0:T(8,128)S(1)}, f32[96,128]{1,0:T(8,128)}, u32[]{:S(2)}) copy-start(f32[96,128]{1,0:T(8,128)} %param.18) | copy-start | bytes 147460
  8.8 26.7 %copy-start.14 = (f32[96,96]{1,0:T(8,128)S(1)}, f32[96,96]{1,0:T(8,128)}, u32[]{:S(2)}) copy-start(f32[96,96]{1,0:T(8,128)} %param.20) | copy-start | bytes 110596
  24.8 6.7 %collective-permute-start.9 = (f32[256,128]{1,0:T(8,128)S(1)}, f32[256,128]{1,0:T(8,128)S(1)}, u32[]{:S(2)}, u32[]{:S(2)}) collective-permute-start(f32[256,128]{1,0:T(8,128)S(1)} %get-tuple-element.42.m0), channel_id=1, source_target_pairs={{0,24},{8,0},{16,8},{24,16},{1,25},{9,1},{17,9},{25,17},{2,26},{10... | collective-permute-start | bytes 393224 | tf_op jit(solution)/shard_map/ppermute | solution.py:70
  28.1 8.4 %collective-permute-start.10 = (f32[256,128]{1,0:T(8,128)S(1)}, f32[256,128]{1,0:T(8,128)S(1)}, u32[]{:S(2)}, u32[]{:S(2)}) collective-permute-start(f32[256,128]{1,0:T(8,128)S(1)} %get-tuple-element.42.m0), channel_id=1, source_target_pairs={{0,4},{4,0},{1,5},{5,1},{2,6},{6,2},{3,7},{7,3},{8,12},{12,8},{9,1... | collective-permute-start | bytes 393224 | tf_op jit(solution)/shard_map/ppermute | solution.py:70
  30.3 7.4 %collective-permute-start.8 = (f32[256,128]{1,0:T(8,128)S(1)}, f32[256,128]{1,0:T(8,128)S(1)}, u32[]{:S(2)}, u32[]{:S(2)}) collective-permute-start(f32[256,128]{1,0:T(8,128)S(1)} %get-tuple-element.42.m0), channel_id=1, source_target_pairs={{0,16},{8,24},{16,0},{24,8},{1,17},{9,25},{17,1},{25,9},{2,18},{10... | collective-permute-start | bytes 393224 | tf_op jit(solution)/shard_map/ppermute | solution.py:70
  30.8 9.2 %collective-permute-start.7 = (f32[256,128]{1,0:T(8,128)S(1)}, f32[256,128]{1,0:T(8,128)S(1)}, u32[]{:S(2)}, u32[]{:S(2)}) collective-permute-start(f32[256,128]{1,0:T(8,128)S(1)} %get-tuple-element.42.m0), channel_id=1, source_target_pairs={{0,8},{8,16},{16,24},{24,0},{1,9},{9,17},{17,25},{25,1},{2,10},{10... | collective-permute-start | bytes 393224 | tf_op jit(solution)/shard_map/ppermute | solution.py:70
  31.5 9.0 %collective-permute-start.13 = (f32[256,128]{1,0:T(8,128)S(1)}, f32[256,128]{1,0:T(8,128)S(1)}, u32[]{:S(2)}, u32[]{:S(2)}) collective-permute-start(f32[256,128]{1,0:T(8,128)S(1)} %collective-permute-done.9.m3), channel_id=1, source_target_pairs={{0,4},{4,0},{1,5},{5,1},{2,6},{6,2},{3,7},{7,3},{8,12},{12,8},{9,1... | collective-permute-start | bytes 393224 | tf_op jit(solution)/shard_map/ppermute | solution.py:70
  35.5 15.9 %collective-permute-start.2 = (f32[96,736]{1,0:T(8,128)S(1)}, f32[96,736]{1,0:T(8,128)S(1)}, u32[]{:S(2)}, u32[]{:S(2)}) collective-permute-start(f32[96,736]{1,0:T(8,128)S(1)} %constant_dynamic-update-slice_fusion.p0), channel_id=1, source_target_pairs={{0,3},{1,0},{2,1},{3,2},{4,7},{5,4},{6,5},{7,6},{8,11},{9,8},{10,9... | collective-permute-start | bytes 847880 | tf_op jit(solution)/shard_map/ppermute | solution.py:70
  36.5 16.6 %collective-permute-start.1 = (f32[96,736]{1,0:T(8,128)S(1)}, f32[96,736]{1,0:T(8,128)S(1)}, u32[]{:S(2)}, u32[]{:S(2)}) collective-permute-start(f32[96,736]{1,0:T(8,128)S(1)} %constant_dynamic-update-slice_fusion.p0), channel_id=1, source_target_pairs={{0,2},{1,3},{2,0},{3,1},{4,6},{5,7},{6,4},{7,5},{8,10},{9,11},{10,... | collective-permute-start | bytes 847880 | tf_op jit(solution)/shard_map/ppermute | solution.py:70
  37.7 15.6 %collective-permute-start = (f32[96,736]{1,0:T(8,128)S(1)}, f32[96,736]{1,0:T(8,128)S(1)}, u32[]{:S(2)}, u32[]{:S(2)}) collective-permute-start(f32[96,736]{1,0:T(8,128)S(1)} %constant_dynamic-update-slice_fusion.p0), channel_id=1, source_target_pairs={{0,1},{1,2},{2,3},{3,0},{4,5},{5,6},{6,7},{7,4},{8,9},{9,10},{10,1... | collective-permute-start | bytes 847880 | tf_op jit(solution)/shard_map/ppermute | solution.py:70
  40.0 1.5 %collective-permute-start.12 = (f32[256,128]{1,0:T(8,128)S(1)}, f32[256,128]{1,0:T(8,128)S(1)}, u32[]{:S(2)}, u32[]{:S(2)}) collective-permute-start(f32[256,128]{1,0:T(8,128)S(1)} %collective-permute-done.8.m2), channel_id=1, source_target_pairs={{0,4},{4,0},{1,5},{5,1},{2,6},{6,2},{3,7},{7,3},{8,12},{12,8},{9,1... | collective-permute-start | bytes 393224 | tf_op jit(solution)/shard_map/ppermute | solution.py:70
  40.5 3.3 %collective-permute-start.11 = (f32[256,128]{1,0:T(8,128)S(1)}, f32[256,128]{1,0:T(8,128)S(1)}, u32[]{:S(2)}, u32[]{:S(2)}) collective-permute-start(f32[256,128]{1,0:T(8,128)S(1)} %collective-permute-done.7.m1), channel_id=1, source_target_pairs={{0,4},{4,0},{1,5},{5,1},{2,6},{6,2},{3,7},{7,3},{8,12},{12,8},{9,1... | collective-permute-start | bytes 393224 | tf_op jit(solution)/shard_map/ppermute | solution.py:70
  41.5 11.8 %collective-permute-start.4 = (f32[64,128]{1,0:T(8,128)S(1)}, f32[64,128]{1,0:T(8,128)S(1)}, u32[]{:S(2)}, u32[]{:S(2)}) collective-permute-start(f32[64,128]{1,0:T(8,128)S(1)} %get-tuple-element.35), channel_id=1, source_target_pairs={{4,0},{8,4},{12,8},{16,12},{20,16},{24,20},{28,24},{32,28},{36,32}... | collective-permute-start | bytes 98312 | tf_op jit(solution)/shard_map/ppermute | solution.py:76
  43.7 9.5 %collective-permute-start.3 = (f32[64,128]{1,0:T(8,128)S(1)}, f32[64,128]{1,0:T(8,128)S(1)}, u32[]{:S(2)}, u32[]{:S(2)}) collective-permute-start(f32[64,128]{1,0:T(8,128)S(1)} %get-tuple-element.35), channel_id=1, source_target_pairs={{0,4},{4,8},{8,12},{12,16},{16,20},{20,24},{24,28},{28,32},{32,36}... | collective-permute-start | bytes 98312 | tf_op jit(solution)/shard_map/ppermute | solution.py:75
  50.4 1.0 copy-start
  51.4 29.1 %collective-permute-start.14 = (f32[384,128]{1,0:T(8,128)}, f32[384,128]{1,0:T(8,128)}, u32[]{:S(2)}, u32[]{:S(2)}) collective-permute-start(f32[384,128]{1,0:T(8,128)} %get-tuple-element.47.a0), channel_id=1, source_target_pairs={{0,32},{32,64},{64,96},{96,128},{128,160},{160,192},{192,224},{224... | collective-permute-start | bytes 589832 | tf_op jit(solution)/shard_map/ppermute | solution.py:70
  54.7 6.0 %collective-permute-start.6 = (f32[128,128]{1,0:T(8,128)S(1)}, f32[128,128]{1,0:T(8,128)S(1)}, u32[]{:S(2)}, u32[]{:S(2)}) collective-permute-start(f32[128,128]{1,0:T(8,128)S(1)} %get-tuple-element.38), channel_id=1, source_target_pairs={{4,0},{8,4},{12,8},{16,12},{20,16},{24,20},{28,24},{32,28},{36,32}... | collective-permute-start | bytes 196616 | tf_op jit(solution)/shard_map/ppermute | solution.py:76
  57.1 4.5 %collective-permute-start.5 = (f32[128,128]{1,0:T(8,128)S(1)}, f32[128,128]{1,0:T(8,128)S(1)}, u32[]{:S(2)}, u32[]{:S(2)}) collective-permute-start(f32[128,128]{1,0:T(8,128)S(1)} %get-tuple-element.38), channel_id=1, source_target_pairs={{0,4},{4,8},{8,12},{12,16},{16,20},{20,24},{24,28},{28,32},{32,36}... | collective-permute-start | bytes 196616 | tf_op jit(solution)/shard_map/ppermute | solution.py:75
  63.3 0.7 copy-start.2
  64.0 0.7 copy-start.3
  64.7 15.8 %all-to-all-start.1 = ((f32[8,56,128]{2,1,0:T(8,128)}), f32[8,56,128]{2,1,0:T(8,128)S(1)}, u32[]{:S(2)}, u32[]{:S(2)}) async-start(f32[8,56,128]{2,1,0:T(8,128)} %copy-done.2), calls=%async_computation.1 | async-start | bytes 458752 | tf_op jit(solution)/shard_map/all_to_all | solution.py:65
  71.9 24.5 %collective-permute-start.18 = (f32[384,128]{1,0:T(8,128)}, f32[384,128]{1,0:T(8,128)}, u32[]{:S(2)}, u32[]{:S(2)}) collective-permute-start(f32[384,128]{1,0:T(8,128)} %get-tuple-element.47.a0), channel_id=1, source_target_pairs={{0,224},{32,0},{64,32},{96,64},{128,96},{160,128},{192,160},{224,1... | collective-permute-start | bytes 589832 | tf_op jit(solution)/shard_map/ppermute | solution.py:70
  80.5 18.5 %collective-permute-start.15 = (f32[384,128]{1,0:T(8,128)}, f32[384,128]{1,0:T(8,128)}, u32[]{:S(2)}, u32[]{:S(2)}) collective-permute-start(f32[384,128]{1,0:T(8,128)} %collective-permute-done.14.a1), channel_id=1, source_target_pairs={{0,32},{32,64},{64,96},{96,128},{128,160},{160,192},{192,224},{224... | collective-permute-start | bytes 589832 | tf_op jit(solution)/shard_map/ppermute | solution.py:70
  84.3 0.7 copy-start.1
  85.0 0.6 copy-start.5
  85.7 0.6 copy-start.6
  86.3 24.2 %all-to-all-start.2 = ((f32[8,72,128]{2,1,0:T(8,128)}), f32[8,72,128]{2,1,0:T(8,128)S(1)}, u32[]{:S(2)}, u32[]{:S(2)}) async-start(f32[8,72,128]{2,1,0:T(8,128)} %copy-done.1), calls=%async_computation.2 | async-start | bytes 589824 | tf_op jit(solution)/shard_map/all_to_all | solution.py:65
  96.4 12.2 %collective-permute-start.19 = (f32[384,128]{1,0:T(8,128)}, f32[384,128]{1,0:T(8,128)}, u32[]{:S(2)}, u32[]{:S(2)}) collective-permute-start(f32[384,128]{1,0:T(8,128)} %collective-permute-done.18.b1), channel_id=1, source_target_pairs={{0,224},{32,0},{64,32},{96,64},{128,96},{160,128},{192,160},{224,1... | collective-permute-start | bytes 589832 | tf_op jit(solution)/shard_map/ppermute | solution.py:70
  99.1 11.4 %collective-permute-start.16 = (f32[384,128]{1,0:T(8,128)}, f32[384,128]{1,0:T(8,128)}, u32[]{:S(2)}, u32[]{:S(2)}) collective-permute-start(f32[384,128]{1,0:T(8,128)} %collective-permute-done.15.a2), channel_id=1, source_target_pairs={{0,32},{32,64},{64,96},{96,128},{128,160},{160,192},{192,224},{224... | collective-permute-start | bytes 589832 | tf_op jit(solution)/shard_map/ppermute | solution.py:70
  108.5 5.1 %collective-permute-start.20 = (f32[384,128]{1,0:T(8,128)}, f32[384,128]{1,0:T(8,128)}, u32[]{:S(2)}, u32[]{:S(2)}) collective-permute-start(f32[384,128]{1,0:T(8,128)} %collective-permute-done.19.b2), channel_id=1, source_target_pairs={{0,224},{32,0},{64,32},{96,64},{128,96},{160,128},{192,160},{224,1... | collective-permute-start | bytes 589832 | tf_op jit(solution)/shard_map/ppermute | solution.py:70
  110.5 6.4 %collective-permute-start.17 = (f32[384,128]{1,0:T(8,128)}, f32[384,128]{1,0:T(8,128)}, u32[]{:S(2)}, u32[]{:S(2)}) collective-permute-start(f32[384,128]{1,0:T(8,128)} %collective-permute-done.16.a3), channel_id=1, source_target_pairs={{0,32},{32,64},{64,96},{96,128},{128,160},{160,192},{192,224},{224... | collective-permute-start | bytes 589832 | tf_op jit(solution)/shard_map/ppermute | solution.py:70
  116.8 14.1 %copy-start.4 = (f32[384,128]{1,0:T(8,128)S(1)}, f32[384,128]{1,0:T(8,128)}, u32[]{:S(2)}) copy-start(f32[384,128]{1,0:T(8,128)} %copy-done.3) | copy-start | bytes 589828
  131.0 10.5 %copy-start.15 = (f32[256]{0:T(256)S(1)}, f32[256]{0:T(256)}, u32[]{:S(2)}) copy-start(f32[256]{0:T(256)} %param.15) | copy-start | bytes 3076
  131.0 11.2 %copy-start.8 = (f32[96,256]{1,0:T(8,128)S(1)}, f32[96,256]{1,0:T(8,128)}, u32[]{:S(2)}) copy-start(f32[96,256]{1,0:T(8,128)} %direction_ref) | copy-start | bytes 294916
  131.0 11.2 %copy-start.9 = (f32[96,256]{1,0:T(8,128)S(1)}, f32[96,256]{1,0:T(8,128)}, u32[]{:S(2)}) copy-start(f32[96,256]{1,0:T(8,128)} %residual_ref) | copy-start | bytes 294916
  131.0 11.2 %copy-start.11 = (f32[96,256]{1,0:T(8,128)S(1)}, f32[96,256]{1,0:T(8,128)}, u32[]{:S(2)}) copy-start(f32[96,256]{1,0:T(8,128)} %param.12) | copy-start | bytes 294916

commit v2 on v1

--- a/solution.py
+++ b/solution.py
@@ -44,6 +44,10 @@
 
 def shaped(*shape, dtype=jnp.float32):
     return jax.ShapeDtypeStruct(shape, dtype)
+
+
+def stored(*shape, dtype=jnp.float32):
+    return pltpu.HBM(shape, dtype)
 
 
 def call(body, outs, smem, *args, scratch=()):
@@ -374,7 +378,7 @@
     below, above = beside(faces)
     defect, sent = call(
         solve_slab,
-        (shaped(384, 128), shaped(8, 56, 128)),
+        (stored(384, 128), stored(8, 56, 128)),
         2,
         interface,
         grp,
@@ -390,7 +394,7 @@
     maps, states_f, states_b, plane = call(
         map_plane,
         (
-            shaped(2, 8, 256, 128, dtype=jnp.bfloat16),
+            stored(2, 8, 256, 128, dtype=jnp.bfloat16),
             shaped(2, 8, 128, 128, dtype=jnp.bfloat16),
             shaped(2, 8, 256, 128, dtype=jnp.bfloat16),
             shaped(384, 128),
@@ -398,8 +402,8 @@
         2,
         at_x,
         at_c,
-        *along,
-        *across,
+        *map(far, along),
+        *map(far, across),
         scratch=[pltpu.VMEM((8, 256, 128), jnp.float32), pltpu.VMEM((8, 128, 128), jnp.float32)],
     )
     ups = [plane]
@@ -410,7 +414,7 @@
         downs.append(ring(downs[-1], "slab_0", -1))
     own_f, own_b, sums = call(
         sweep_plane,
-        (shaped(9, 16, 128), shaped(8, 16, 128), shaped(8, 72, 128)),
+        (stored(9, 16, 128), stored(8, 16, 128), stored(8, 72, 128)),
         1,
         place,
         to_each(sent, PLANE),
@@ -425,9 +429,8 @@
         at_z,
         place,
         to_each(sums, "slab_0"),
-        *ups[:4],
-        far(ups[4]),
-        *downs[1:],
+        *map(far, ups),
+        *map(far, downs[1:]),
         states_f,
         states_b,
         far(own_f),

time: 144 us -> 143 us (level)
  local copies, waits for them, and re-layouts: 5.34 us -> 1.03 us
  Pallas kernels: 18.2 us -> 21.3 us
    unnamed x35 -> x39, local copies, waits for them, and re-layouts: 4.4 us -> 0.09 us
    pallas_call x8, Pallas kernels: 18.2 us -> 21.3 us  [call(): pl.pallas_call(body, out_shape=outs, in_specs=[SMEM] * smem + [VMEM] * (l...]
  transfers between devices with their start and end apart: 24 -> 24, of which waited for: 9 -> 8; matrix products, arithmetic and copies ran while one was open for 0% -> 0% of each run, Pallas kernels for 7% -> 9%
where the time goes in v2:
time: 143 us; the launch traced here: 142 us
  starting transfers between devices  62 us (43%)
  waiting for transfers between devices  35.2 us (25%)
  Pallas kernels  21.3 us (15%)
  blocking collectives  19.9 us (14%)
  other arithmetic  1.46 us (1%)
    ppermute x17, starting transfers between devices, ring(): lax.ppermute(x, axis, [(i, (i + step) % count) for i in range(count)])  27.9 us
    all_to_all x3, starting transfers between devices, to_each(): return lax.all_to_all(pieces, axes, split_axis=0, concat_axis=0, tiled=True)  23 us
    pallas_call x8, Pallas kernels, call(): pl.pallas_call(body, out_shape=outs, in_specs=[SMEM] * smem + [VMEM] * (l...  21.3 us
    all_to_all x2, blocking collectives, to_each(): return lax.all_to_all(pieces, axes, split_axis=0, concat_axis=0, tiled=True)  19.9 us
    ppermute x17, waiting for transfers between devices, ring(): lax.ppermute(x, axis, [(i, (i + step) % count) for i in range(count)])  19.1 us
    all_to_all x3, waiting for transfers between devices, to_each(): return lax.all_to_all(pieces, axes, split_axis=0, concat_axis=0, tiled=True)  14.9 us
    ppermute x2, starting transfers between devices, beside(): below = lax.ppermute(faces, SLAB, [(i, i + 1) for i in range(count - 1)])  6.93 us
    ppermute x2, starting transfers between devices, beside(): above = lax.ppermute(faces, SLAB, [(i + 1, i) for i in range(count - 1)])  4.18 us
  transfers between devices with their start and end apart: 24, of which 8 were waited for; matrix products, arithmetic and copies ran while one was open for 0% of the time, Pallas kernels for 9%

profile of v2, /device:TPU:1, one launch (start us, length us, event | category | flops | bytes accessed | tf_op | source)
XLA Modules:
  0.0 141.9 jit_solution(16919762049608600824)
XLA Ops:
  0.6 0.8 dynamic-slice_bitcast_fusion.rho_ref
  1.4 2.2 %shard_map.147 = f32[4,96,768]{2,1,0:T(8,128)} custom-call(f32[96,256]{1,0:T(8,128)} %direction_ref, f32[96,256]{1,0:T(8,128)} %residual_ref, f32[96,384]{1,0:T(8,128)} %inverse_ref.1, f32[96,128]{1,0:T(8,128)} %lower_ref.1, f32[96,128]{1,0:T(8,128)} %upper_ref.1), custom_call_target="tpu_custom_call" | custom-call | tf_op jit(solution)/shard_map/pallas_call | solution.py:54
  3.6 5.1 %all-to-all-start = ((f32[4,96,768]{2,1,0:T(8,128)}), f32[4,96,768]{2,1,0:T(8,128)S(1)}, u32[]{:S(2)}, u32[]{:S(2)}) async-start(f32[4,96,768]{2,1,0:T(8,128)} %shard_map.147), calls=%async_computation | async-start | bytes 2359296 | tf_op jit(solution)/shard_map/all_to_all | solution.py:69
  8.8 0.0 copy-start.16
  8.8 14.9 %all-to-all-done = f32[4,96,768]{2,1,0:T(8,128)S(1)} async-done(((f32[4,96,768]{2,1,0:T(8,128)}), f32[4,96,768]{2,1,0:T(8,128)S(1)}, u32[]{:S(2)}, u32[]{:S(2)}) %all-to-all-start) | async-done | bytes 1179680 | tf_op jit(solution)/shard_map/all_to_all | solution.py:69
  23.7 1.1 shard_map.148
  24.8 3.3 %collective-permute-start.9 = (f32[256,128]{1,0:T(8,128)S(1)}, f32[256,128]{1,0:T(8,128)S(1)}, u32[]{:S(2)}, u32[]{:S(2)}) collective-permute-start(f32[256,128]{1,0:T(8,128)S(1)} %get-tuple-element.42.m0), channel_id=1, source_target_pairs={{0,24},{8,0},{16,8},{24,16},{1,25},{9,1},{17,9},{25,17},{2,26},{10... | collective-permute-start | bytes 393224 | tf_op jit(solution)/shard_map/ppermute | solution.py:74
  28.1 2.2 %collective-permute-start.10 = (f32[256,128]{1,0:T(8,128)S(1)}, f32[256,128]{1,0:T(8,128)S(1)}, u32[]{:S(2)}, u32[]{:S(2)}) collective-permute-start(f32[256,128]{1,0:T(8,128)S(1)} %get-tuple-element.42.m0), channel_id=1, source_target_pairs={{0,4},{4,0},{1,5},{5,1},{2,6},{6,2},{3,7},{7,3},{8,12},{12,8},{9,1... | collective-permute-start | bytes 393224 | tf_op jit(solution)/shard_map/ppermute | solution.py:74
  30.3 0.5 collective-permute-start.8
  30.8 0.7 collective-permute-start.7
  31.5 0.0 collective-permute-done.9.m3
  31.5 4.0 %collective-permute-start.13 = (f32[256,128]{1,0:T(8,128)S(1)}, f32[256,128]{1,0:T(8,128)S(1)}, u32[]{:S(2)}, u32[]{:S(2)}) collective-permute-start(f32[256,128]{1,0:T(8,128)S(1)} %collective-permute-done.9.m3), channel_id=1, source_target_pairs={{0,4},{4,0},{1,5},{5,1},{2,6},{6,2},{3,7},{7,3},{8,12},{12,8},{9,1... | collective-permute-start | bytes 393224 | tf_op jit(solution)/shard_map/ppermute | solution.py:74
  35.5 1.0 collective-permute-start.2
  36.5 0.0 collective-permute-done.10.n0
  36.5 1.2 collective-permute-start.1
  37.7 0.0 collective-permute-done.8.m2
  37.7 0.0 collective-permute-start
  37.7 2.3 %collective-permute-done.7.m1 = f32[256,128]{1,0:T(8,128)S(1)} collective-permute-done((f32[256,128]{1,0:T(8,128)S(1)}, f32[256,128]{1,0:T(8,128)S(1)}, u32[]{:S(2)}, u32[]{:S(2)}) %collective-permute-start.7) | collective-permute-done | bytes 131104 | tf_op jit(solution)/shard_map/ppermute | solution.py:74
  40.0 0.5 collective-permute-start.12
  40.5 0.0 collective-permute-done.13.n3
  40.5 0.1 collective-permute-start.11
  40.6 0.9 collective-permute-done.12.n2
  41.5 2.3 %collective-permute-start.4 = (f32[64,128]{1,0:T(8,128)S(1)}, f32[64,128]{1,0:T(8,128)S(1)}, u32[]{:S(2)}, u32[]{:S(2)}) collective-permute-start(f32[64,128]{1,0:T(8,128)S(1)} %get-tuple-element.35), channel_id=1, source_target_pairs={{4,0},{8,4},{12,8},{16,12},{20,16},{24,20},{28,24},{32,28},{36,32}... | collective-permute-start | bytes 98312 | tf_op jit(solution)/shard_map/ppermute | solution.py:80
  43.8 0.0 collective-permute-done.11.n1
  43.8 3.3 %collective-permute-start.3 = (f32[64,128]{1,0:T(8,128)S(1)}, f32[64,128]{1,0:T(8,128)S(1)}, u32[]{:S(2)}, u32[]{:S(2)}) collective-permute-start(f32[64,128]{1,0:T(8,128)S(1)} %get-tuple-element.35), channel_id=1, source_target_pairs={{0,4},{4,8},{8,12},{12,16},{16,20},{20,24},{24,28},{28,32},{32,36}... | collective-permute-start | bytes 98312 | tf_op jit(solution)/shard_map/ppermute | solution.py:79
  47.2 4.9 %shard_map.151 = (bf16[2,8,256,128]{3,2,1,0:T(8,128)(2,1)}, bf16[2,8,128,128]{3,2,1,0:T(8,128)(2,1)S(1)}, bf16[2,8,256,128]{3,2,1,0:T(8,128)(2,1)S(1)}, f32[384,128]{1,0:T(8,128)}) custom-call(s32[1]{0:T(128)} %bitcast.1.x_ref, s32[1]{0:T(128)} %bitcast.2.c_ref, f32[256,128]{1,0:T(8,128)} %copy-done.1, f32[256,128]{1,0:T(8,128)} %copy-done.9, ...), custom_call_target="tpu_custom_call" | custom-call | tf_op jit(solution)/shard_map/pallas_call | solution.py:54
  52.1 0.0 collective-permute-done.2.p3
  52.1 1.6 %collective-permute-start.14 = (f32[384,128]{1,0:T(8,128)}, f32[384,128]{1,0:T(8,128)}, u32[]{:S(2)}, u32[]{:S(2)}) collective-permute-start(f32[384,128]{1,0:T(8,128)} %get-tuple-element.47.a0), channel_id=1, source_target_pairs={{0,32},{32,64},{64,96},{96,128},{128,160},{160,192},{192,224},{224... | collective-permute-start | bytes 589832 | tf_op jit(solution)/shard_map/ppermute | solution.py:74
  53.7 0.0 collective-permute-done.1.p2
  53.7 0.0 collective-permute-done.p1
  53.7 0.0 collective-permute-done.4.above_ref
  53.7 0.0 collective-permute-done.3.below_ref
  53.8 1.4 %shard_map.149 = (f32[384,128]{1,0:T(8,128)S(1)}, f32[384,128]{1,0:T(8,128)S(1)}, f32[128,128]{1,0:T(8,128)S(1)}) custom-call(s32[1,128]{1,0:T(1,128)S(1)} %copy-done.2, s32[1]{0:T(128)} %bitcast.grp_ref, f32[384,768]{1,0:T(8,128)S(1)} %bitcast.41, f32[96,736]{1,0:T(8,128)S(1)} %constant_dynamic-update-slice_fusion.p0, ...), custom_call_target="tpu_custom_call" | custom-call | tf_op jit(solution)/shard_map/pallas_call | solution.py:54
  55.2 1.9 %collective-permute-start.6 = (f32[128,128]{1,0:T(8,128)S(1)}, f32[128,128]{1,0:T(8,128)S(1)}, u32[]{:S(2)}, u32[]{:S(2)}) collective-permute-start(f32[128,128]{1,0:T(8,128)S(1)} %get-tuple-element.38), channel_id=1, source_target_pairs={{4,0},{8,4},{12,8},{16,12},{20,16},{24,20},{28,24},{32,28},{36,32}... | collective-permute-start | bytes 196616 | tf_op jit(solution)/shard_map/ppermute | solution.py:80
  57.1 3.6 %collective-permute-start.5 = (f32[128,128]{1,0:T(8,128)S(1)}, f32[128,128]{1,0:T(8,128)S(1)}, u32[]{:S(2)}, u32[]{:S(2)}) collective-permute-start(f32[128,128]{1,0:T(8,128)S(1)} %get-tuple-element.38), channel_id=1, source_target_pairs={{0,4},{4,8},{8,12},{12,16},{16,20},{20,24},{24,28},{28,32},{32,36}... | collective-permute-start | bytes 196616 | tf_op jit(solution)/shard_map/ppermute | solution.py:79
  60.8 0.4 collective-permute-done.6.above_ref
  61.2 0.9 collective-permute-done.5.below_ref
  62.1 2.5 %shard_map.150 = (f32[384,128]{1,0:T(8,128)}, f32[8,56,128]{2,1,0:T(8,128)}) custom-call(s32[1,128]{1,0:T(1,128)S(1)} %copy-done.2, s32[1]{0:T(128)} %bitcast.grp_ref, f32[384,768]{1,0:T(8,128)S(1)} %bitcast.42, f32[96,736]{1,0:T(8,128)S(1)} %constant_dynamic-update-slice_fusion.p0, f32[96,736]{1,0:T(8,128)S(1)} %collective-permute-done.p1, ...), custom_call_target="tpu_custom_call" | custom-call | tf_op jit(solution)/shard_map/pallas_call | solution.py:54
  64.6 7.1 %all-to-all-start.1 = ((f32[8,56,128]{2,1,0:T(8,128)}), f32[8,56,128]{2,1,0:T(8,128)S(1)}, u32[]{:S(2)}, u32[]{:S(2)}) async-start(f32[8,56,128]{2,1,0:T(8,128)} %get-tuple-element.39), calls=%async_computation.1 | async-start | bytes 458752 | tf_op jit(solution)/shard_map/all_to_all | solution.py:69
  71.7 8.2 %collective-permute-start.18 = (f32[384,128]{1,0:T(8,128)}, f32[384,128]{1,0:T(8,128)}, u32[]{:S(2)}, u32[]{:S(2)}) collective-permute-start(f32[384,128]{1,0:T(8,128)} %get-tuple-element.47.a0), channel_id=1, source_target_pairs={{0,224},{32,0},{64,32},{96,64},{128,96},{160,128},{192,160},{224,1... | collective-permute-start | bytes 589832 | tf_op jit(solution)/shard_map/ppermute | solution.py:74
  79.9 0.0 collective-permute-done.14.a1
  79.9 0.0 collective-permute-start.15
  79.9 0.0 all-to-all-done.1.got_ref
  79.9 4.5 %shard_map.152 = (f32[9,16,128]{2,1,0:T(8,128)}, f32[8,16,128]{2,1,0:T(8,128)}, f32[8,72,128]{2,1,0:T(8,128)}) custom-call(s32[1]{0:T(128)} %bitcast.4.place_ref, f32[8,56,128]{2,1,0:T(8,128)S(1)} %all-to-all-done.1.got_ref, bf16[2,8,256,128]{3,2,1,0:T(8,128)(2,1)} %get-tuple-element.43.maps_ref, ...), custom_call_target="tpu_custom_call" | custom-call | tf_op jit(solution)/shard_map/pallas_call | solution.py:54
  84.4 10.8 %all-to-all-start.2 = ((f32[8,72,128]{2,1,0:T(8,128)}), f32[8,72,128]{2,1,0:T(8,128)S(1)}, u32[]{:S(2)}, u32[]{:S(2)}) async-start(f32[8,72,128]{2,1,0:T(8,128)} %get-tuple-element.46), calls=%async_computation.2 | async-start | bytes 589824 | tf_op jit(solution)/shard_map/all_to_all | solution.py:69
  95.2 2.7 %collective-permute-start.19 = (f32[384,128]{1,0:T(8,128)}, f32[384,128]{1,0:T(8,128)}, u32[]{:S(2)}, u32[]{:S(2)}) collective-permute-start(f32[384,128]{1,0:T(8,128)} %collective-permute-done.18.b1), channel_id=1, source_target_pairs={{0,224},{32,0},{64,32},{96,64},{128,96},{160,128},{192,160},{224,1... | collective-permute-start | bytes 589832 | tf_op jit(solution)/shard_map/ppermute | solution.py:74
  97.9 0.0 collective-permute-done.15.a2
  97.9 0.0 collective-permute-start.16
  97.9 9.5 %collective-permute-done.19.b2 = f32[384,128]{1,0:T(8,128)} collective-permute-done((f32[384,128]{1,0:T(8,128)}, f32[384,128]{1,0:T(8,128)}, u32[]{:S(2)}, u32[]{:S(2)}) %collective-permute-start.19) | collective-permute-done | bytes 196640 | tf_op jit(solution)/shard_map/ppermute | solution.py:74
  107.4 1.9 %collective-permute-start.20 = (f32[384,128]{1,0:T(8,128)}, f32[384,128]{1,0:T(8,128)}, u32[]{:S(2)}, u32[]{:S(2)}) collective-permute-start(f32[384,128]{1,0:T(8,128)} %collective-permute-done.19.b2), channel_id=1, source_target_pairs={{0,224},{32,0},{64,32},{96,64},{128,96},{160,128},{192,160},{224,1... | collective-permute-start | bytes 589832 | tf_op jit(solution)/shard_map/ppermute | solution.py:74
  109.3 0.0 collective-permute-done.16.a3
  109.3 0.0 collective-permute-start.17
  109.3 0.0 all-to-all-done.2.sums_ref
  109.3 3.2 %collective-permute-done.20.b3 = f32[384,128]{1,0:T(8,128)} collective-permute-done((f32[384,128]{1,0:T(8,128)}, f32[384,128]{1,0:T(8,128)}, u32[]{:S(2)}, u32[]{:S(2)}) %collective-permute-start.20) | collective-permute-done | bytes 196640 | tf_op jit(solution)/shard_map/ppermute | solution.py:74
  112.5 3.1 %collective-permute-done.17.a4 = f32[384,128]{1,0:T(8,128)} collective-permute-done((f32[384,128]{1,0:T(8,128)}, f32[384,128]{1,0:T(8,128)}, u32[]{:S(2)}, u32[]{:S(2)}) %collective-permute-start.17) | collective-permute-done | bytes 196640 | tf_op jit(solution)/shard_map/ppermute | solution.py:74
  115.6 3.7 %shard_map.153 = (f32[8,40,128]{2,1,0:T(8,128)S(1)}, f32[8,128]{1,0:T(8,128)S(1)}) custom-call(s32[1]{0:T(128)} %bitcast.3.z_ref, s32[1]{0:T(128)} %bitcast.4.place_ref, f32[8,72,128]{2,1,0:T(8,128)S(1)} %all-to-all-done.2.sums_ref, f32[384,128]{1,0:T(8,128)} %get-tuple-element.47.a0, f32[384,128]{1,0:T(8,128)} %collective-permute-done.14.a1, ...), custom_call_target="tpu_custom_call" | custom-call | tf_op jit(solution)/shard_map/pallas_call | solution.py:54
  119.4 10.4 %all_to_all.25.back_ref = f32[8,40,128]{2,1,0:T(8,128)S(1)} all-to-all(f32[8,40,128]{2,1,0:T(8,128)S(1)} %get-tuple-element.50), channel_id=1, replica_groups=mesh['slab_0'=8,'slab_1'=4,'slab_2'=2,'grp'=4] {'slab_1','slab_2'}, dimensions={0} | all-to-all | bytes 327680 | tf_op jit(solution)/shard_map/all_to_all | solution.py:69
  129.8 0.0 copy-start.13
  129.8 0.9 shard_map.154
  130.7 9.5 %all_to_all.26 = f32[4,104,128]{2,1,0:T(8,128)S(1)} all-to-all(f32[4,104,128]{2,1,0:T(8,128)S(1)} %shard_map.154), channel_id=1, replica_groups=mesh['slab_0'=8,'slab_1'=4,'slab_2'=2,'grp'=4] {'grp'}, dimensions={0} | all-to-all | bytes 425984 | tf_op jit(solution)/shard_map/all_to_all | solution.py:69
  140.2 0.1 slice_bitcast_fusion.11
  140.3 0.6 fusion.1
  140.9 0.1 slice_bitcast_fusion.3
  141.0 0.8 maximum_add_fusion
  (39 shorter events, 0.1 us)
Async XLA Ops:
  3.6 5.1 %copy-start.5 = (f32[96,384]{1,0:T(8,128)S(1)}, f32[96,384]{1,0:T(8,128)}, u32[]{:S(2)}) copy-start(f32[96,384]{1,0:T(8,128)} %param.16) | copy-start | bytes 442372
  3.6 20.0 %copy-start.2 = (s32[1,128]{1,0:T(1,128)S(1)}, s32[1,128]{1,0:T(1,128)}, u32[]{:S(2)}) copy-start(s32[1,128]{1,0:T(1,128)} %index_ref.5) | copy-start | bytes 1540
  3.6 20.0 %all-to-all-start = ((f32[4,96,768]{2,1,0:T(8,128)}), f32[4,96,768]{2,1,0:T(8,128)S(1)}, u32[]{:S(2)}, u32[]{:S(2)}) async-start(f32[4,96,768]{2,1,0:T(8,128)} %shard_map.147), calls=%async_computation | async-start | bytes 2359296 | tf_op jit(solution)/shard_map/all_to_all | solution.py:69
  8.8 19.3 %copy-start.14 = (f32[96,128]{1,0:T(8,128)S(1)}, f32[96,128]{1,0:T(8,128)}, u32[]{:S(2)}) copy-start(f32[96,128]{1,0:T(8,128)} %param.17) | copy-start | bytes 147460
  8.8 22.0 %copy-start.15 = (f32[96,128]{1,0:T(8,128)S(1)}, f32[96,128]{1,0:T(8,128)}, u32[]{:S(2)}) copy-start(f32[96,128]{1,0:T(8,128)} %param.18) | copy-start | bytes 147460
  8.8 26.7 %copy-start.16 = (f32[96,96]{1,0:T(8,128)S(1)}, f32[96,96]{1,0:T(8,128)}, u32[]{:S(2)}) copy-start(f32[96,96]{1,0:T(8,128)} %param.20) | copy-start | bytes 110596
  24.8 22.3 %copy-start.1 = (f32[256,128]{1,0:T(8,128)}, f32[256,128]{1,0:T(8,128)S(1)}, u32[]{:S(2)}) copy-start(f32[256,128]{1,0:T(8,128)S(1)} %get-tuple-element.42.m0) | copy-start | bytes 393220
  24.8 6.7 %collective-permute-start.9 = (f32[256,128]{1,0:T(8,128)S(1)}, f32[256,128]{1,0:T(8,128)S(1)}, u32[]{:S(2)}, u32[]{:S(2)}) collective-permute-start(f32[256,128]{1,0:T(8,128)S(1)} %get-tuple-element.42.m0), channel_id=1, source_target_pairs={{0,24},{8,0},{16,8},{24,16},{1,25},{9,1},{17,9},{25,17},{2,26},{10... | collective-permute-start | bytes 393224 | tf_op jit(solution)/shard_map/ppermute | solution.py:74
  28.1 8.4 %collective-permute-start.10 = (f32[256,128]{1,0:T(8,128)S(1)}, f32[256,128]{1,0:T(8,128)S(1)}, u32[]{:S(2)}, u32[]{:S(2)}) collective-permute-start(f32[256,128]{1,0:T(8,128)S(1)} %get-tuple-element.42.m0), channel_id=1, source_target_pairs={{0,4},{4,0},{1,5},{5,1},{2,6},{6,2},{3,7},{7,3},{8,12},{12,8},{9,1... | collective-permute-start | bytes 393224 | tf_op jit(solution)/shard_map/ppermute | solution.py:74
  30.3 7.4 %collective-permute-start.8 = (f32[256,128]{1,0:T(8,128)S(1)}, f32[256,128]{1,0:T(8,128)S(1)}, u32[]{:S(2)}, u32[]{:S(2)}) collective-permute-start(f32[256,128]{1,0:T(8,128)S(1)} %get-tuple-element.42.m0), channel_id=1, source_target_pairs={{0,16},{8,24},{16,0},{24,8},{1,17},{9,25},{17,1},{25,9},{2,18},{10... | collective-permute-start | bytes 393224 | tf_op jit(solution)/shard_map/ppermute | solution.py:74
  30.8 9.2 %collective-permute-start.7 = (f32[256,128]{1,0:T(8,128)S(1)}, f32[256,128]{1,0:T(8,128)S(1)}, u32[]{:S(2)}, u32[]{:S(2)}) collective-permute-start(f32[256,128]{1,0:T(8,128)S(1)} %get-tuple-element.42.m0), channel_id=1, source_target_pairs={{0,8},{8,16},{16,24},{24,0},{1,9},{9,17},{17,25},{25,1},{2,10},{10... | collective-permute-start | bytes 393224 | tf_op jit(solution)/shard_map/ppermute | solution.py:74
  31.5 15.6 %copy-start.6 = (f32[256,128]{1,0:T(8,128)}, f32[256,128]{1,0:T(8,128)S(1)}, u32[]{:S(2)}) copy-start(f32[256,128]{1,0:T(8,128)S(1)} %collective-permute-done.9.m3) | copy-start | bytes 393220
  31.5 9.0 %collective-permute-start.13 = (f32[256,128]{1,0:T(8,128)S(1)}, f32[256,128]{1,0:T(8,128)S(1)}, u32[]{:S(2)}, u32[]{:S(2)}) collective-permute-start(f32[256,128]{1,0:T(8,128)S(1)} %collective-permute-done.9.m3), channel_id=1, source_target_pairs={{0,4},{4,0},{1,5},{5,1},{2,6},{6,2},{3,7},{7,3},{8,12},{12,8},{9,1... | collective-permute-start | bytes 393224 | tf_op jit(solution)/shard_map/ppermute | solution.py:74
  35.5 16.6 %collective-permute-start.2 = (f32[96,736]{1,0:T(8,128)S(1)}, f32[96,736]{1,0:T(8,128)S(1)}, u32[]{:S(2)}, u32[]{:S(2)}) collective-permute-start(f32[96,736]{1,0:T(8,128)S(1)} %constant_dynamic-update-slice_fusion.p0), channel_id=1, source_target_pairs={{0,3},{1,0},{2,1},{3,2},{4,7},{5,4},{6,5},{7,6},{8,11},{9,8},{10,9... | collective-permute-start | bytes 847880 | tf_op jit(solution)/shard_map/ppermute | solution.py:74
  36.5 10.6 %copy-start.7 = (f32[256,128]{1,0:T(8,128)}, f32[256,128]{1,0:T(8,128)S(1)}, u32[]{:S(2)}) copy-start(f32[256,128]{1,0:T(8,128)S(1)} %collective-permute-done.10.n0) | copy-start | bytes 393220
  36.5 17.2 %collective-permute-start.1 = (f32[96,736]{1,0:T(8,128)S(1)}, f32[96,736]{1,0:T(8,128)S(1)}, u32[]{:S(2)}, u32[]{:S(2)}) collective-permute-start(f32[96,736]{1,0:T(8,128)S(1)} %constant_dynamic-update-slice_fusion.p0), channel_id=1, source_target_pairs={{0,2},{1,3},{2,0},{3,1},{4,6},{5,7},{6,4},{7,5},{8,10},{9,11},{10,... | collective-permute-start | bytes 847880 | tf_op jit(solution)/shard_map/ppermute | solution.py:74
  37.7 9.4 %copy-start.8 = (f32[256,128]{1,0:T(8,128)}, f32[256,128]{1,0:T(8,128)S(1)}, u32[]{:S(2)}) copy-start(f32[256,128]{1,0:T(8,128)S(1)} %collective-permute-done.8.m2) | copy-start | bytes 393220
  37.7 16.0 %collective-permute-start = (f32[96,736]{1,0:T(8,128)S(1)}, f32[96,736]{1,0:T(8,128)S(1)}, u32[]{:S(2)}, u32[]{:S(2)}) collective-permute-start(f32[96,736]{1,0:T(8,128)S(1)} %constant_dynamic-update-slice_fusion.p0), channel_id=1, source_target_pairs={{0,1},{1,2},{2,3},{3,0},{4,5},{5,6},{6,7},{7,4},{8,9},{9,10},{10,1... | collective-permute-start | bytes 847880 | tf_op jit(solution)/shard_map/ppermute | solution.py:74
  40.0 7.1 %copy-start.9 = (f32[256,128]{1,0:T(8,128)}, f32[256,128]{1,0:T(8,128)S(1)}, u32[]{:S(2)}) copy-start(f32[256,128]{1,0:T(8,128)S(1)} %collective-permute-done.7.m1) | copy-start | bytes 393220
  40.0 1.5 %collective-permute-start.12 = (f32[256,128]{1,0:T(8,128)S(1)}, f32[256,128]{1,0:T(8,128)S(1)}, u32[]{:S(2)}, u32[]{:S(2)}) collective-permute-start(f32[256,128]{1,0:T(8,128)S(1)} %collective-permute-done.8.m2), channel_id=1, source_target_pairs={{0,4},{4,0},{1,5},{5,1},{2,6},{6,2},{3,7},{7,3},{8,12},{12,8},{9,1... | collective-permute-start | bytes 393224 | tf_op jit(solution)/shard_map/ppermute | solution.py:74
  40.5 6.6 %copy-start.10 = (f32[256,128]{1,0:T(8,128)}, f32[256,128]{1,0:T(8,128)S(1)}, u32[]{:S(2)}) copy-start(f32[256,128]{1,0:T(8,128)S(1)} %collective-permute-done.13.n3) | copy-start | bytes 393220
  40.5 3.3 %collective-permute-start.11 = (f32[256,128]{1,0:T(8,128)S(1)}, f32[256,128]{1,0:T(8,128)S(1)}, u32[]{:S(2)}, u32[]{:S(2)}) collective-permute-start(f32[256,128]{1,0:T(8,128)S(1)} %collective-permute-done.7.m1), channel_id=1, source_target_pairs={{0,4},{4,0},{1,5},{5,1},{2,6},{6,2},{3,7},{7,3},{8,12},{12,8},{9,1... | collective-permute-start | bytes 393224 | tf_op jit(solution)/shard_map/ppermute | solution.py:74
  41.5 5.7 %copy-start.11 = (f32[256,128]{1,0:T(8,128)}, f32[256,128]{1,0:T(8,128)S(1)}, u32[]{:S(2)}) copy-start(f32[256,128]{1,0:T(8,128)S(1)} %collective-permute-done.12.n2) | copy-start | bytes 393220
  41.5 12.2 %collective-permute-start.4 = (f32[64,128]{1,0:T(8,128)S(1)}, f32[64,128]{1,0:T(8,128)S(1)}, u32[]{:S(2)}, u32[]{:S(2)}) collective-permute-start(f32[64,128]{1,0:T(8,128)S(1)} %get-tuple-element.35), channel_id=1, source_target_pairs={{4,0},{8,4},{12,8},{16,12},{20,16},{24,20},{28,24},{32,28},{36,32}... | collective-permute-start | bytes 98312 | tf_op jit(solution)/shard_map/ppermute | solution.py:80
  43.8 3.4 %copy-start.12 = (f32[256,128]{1,0:T(8,128)}, f32[256,128]{1,0:T(8,128)S(1)}, u32[]{:S(2)}) copy-start(f32[256,128]{1,0:T(8,128)S(1)} %collective-permute-done.11.n1) | copy-start | bytes 393220
  43.8 10.0 %collective-permute-start.3 = (f32[64,128]{1,0:T(8,128)S(1)}, f32[64,128]{1,0:T(8,128)S(1)}, u32[]{:S(2)}, u32[]{:S(2)}) collective-permute-start(f32[64,128]{1,0:T(8,128)S(1)} %get-tuple-element.35), channel_id=1, source_target_pairs={{0,4},{4,8},{8,12},{12,16},{16,20},{20,24},{24,28},{28,32},{32,36}... | collective-permute-start | bytes 98312 | tf_op jit(solution)/shard_map/ppermute | solution.py:79
  52.1 27.8 %collective-permute-start.14 = (f32[384,128]{1,0:T(8,128)}, f32[384,128]{1,0:T(8,128)}, u32[]{:S(2)}, u32[]{:S(2)}) collective-permute-start(f32[384,128]{1,0:T(8,128)} %get-tuple-element.47.a0), channel_id=1, source_target_pairs={{0,32},{32,64},{64,96},{96,128},{128,160},{160,192},{192,224},{224... | collective-permute-start | bytes 589832 | tf_op jit(solution)/shard_map/ppermute | solution.py:74
  55.2 6.0 %collective-permute-start.6 = (f32[128,128]{1,0:T(8,128)S(1)}, f32[128,128]{1,0:T(8,128)S(1)}, u32[]{:S(2)}, u32[]{:S(2)}) collective-permute-start(f32[128,128]{1,0:T(8,128)S(1)} %get-tuple-element.38), channel_id=1, source_target_pairs={{4,0},{8,4},{12,8},{16,12},{20,16},{24,20},{28,24},{32,28},{36,32}... | collective-permute-start | bytes 196616 | tf_op jit(solution)/shard_map/ppermute | solution.py:80
  57.1 5.0 %collective-permute-start.5 = (f32[128,128]{1,0:T(8,128)S(1)}, f32[128,128]{1,0:T(8,128)S(1)}, u32[]{:S(2)}, u32[]{:S(2)}) collective-permute-start(f32[128,128]{1,0:T(8,128)S(1)} %get-tuple-element.38), channel_id=1, source_target_pairs={{0,4},{4,8},{8,12},{12,16},{16,20},{20,24},{24,28},{28,32},{32,36}... | collective-permute-start | bytes 196616 | tf_op jit(solution)/shard_map/ppermute | solution.py:79
  64.6 15.3 %all-to-all-start.1 = ((f32[8,56,128]{2,1,0:T(8,128)}), f32[8,56,128]{2,1,0:T(8,128)S(1)}, u32[]{:S(2)}, u32[]{:S(2)}) async-start(f32[8,56,128]{2,1,0:T(8,128)} %get-tuple-element.39), calls=%async_computation.1 | async-start | bytes 458752 | tf_op jit(solution)/shard_map/all_to_all | solution.py:69
  71.7 23.5 %collective-permute-start.18 = (f32[384,128]{1,0:T(8,128)}, f32[384,128]{1,0:T(8,128)}, u32[]{:S(2)}, u32[]{:S(2)}) collective-permute-start(f32[384,128]{1,0:T(8,128)} %get-tuple-element.47.a0), channel_id=1, source_target_pairs={{0,224},{32,0},{64,32},{96,64},{128,96},{160,128},{192,160},{224,1... | collective-permute-start | bytes 589832 | tf_op jit(solution)/shard_map/ppermute | solution.py:74
  79.9 18.0 %collective-permute-start.15 = (f32[384,128]{1,0:T(8,128)}, f32[384,128]{1,0:T(8,128)}, u32[]{:S(2)}, u32[]{:S(2)}) collective-permute-start(f32[384,128]{1,0:T(8,128)} %collective-permute-done.14.a1), channel_id=1, source_target_pairs={{0,32},{32,64},{64,96},{96,128},{128,160},{160,192},{192,224},{224... | collective-permute-start | bytes 589832 | tf_op jit(solution)/shard_map/ppermute | solution.py:74
  84.4 24.9 %all-to-all-start.2 = ((f32[8,72,128]{2,1,0:T(8,128)}), f32[8,72,128]{2,1,0:T(8,128)S(1)}, u32[]{:S(2)}, u32[]{:S(2)}) async-start(f32[8,72,128]{2,1,0:T(8,128)} %get-tuple-element.46), calls=%async_computation.2 | async-start | bytes 589824 | tf_op jit(solution)/shard_map/all_to_all | solution.py:69
  95.2 12.2 %collective-permute-start.19 = (f32[384,128]{1,0:T(8,128)}, f32[384,128]{1,0:T(8,128)}, u32[]{:S(2)}, u32[]{:S(2)}) collective-permute-start(f32[384,128]{1,0:T(8,128)} %collective-permute-done.18.b1), channel_id=1, source_target_pairs={{0,224},{32,0},{64,32},{96,64},{128,96},{160,128},{192,160},{224,1... | collective-permute-start | bytes 589832 | tf_op jit(solution)/shard_map/ppermute | solution.py:74
  97.9 11.4 %collective-permute-start.16 = (f32[384,128]{1,0:T(8,128)}, f32[384,128]{1,0:T(8,128)}, u32[]{:S(2)}, u32[]{:S(2)}) collective-permute-start(f32[384,128]{1,0:T(8,128)} %collective-permute-done.15.a2), channel_id=1, source_target_pairs={{0,32},{32,64},{64,96},{96,128},{128,160},{160,192},{192,224},{224... | collective-permute-start | bytes 589832 | tf_op jit(solution)/shard_map/ppermute | solution.py:74
  107.4 5.1 %collective-permute-start.20 = (f32[384,128]{1,0:T(8,128)}, f32[384,128]{1,0:T(8,128)}, u32[]{:S(2)}, u32[]{:S(2)}) collective-permute-start(f32[384,128]{1,0:T(8,128)} %collective-permute-done.19.b2), channel_id=1, source_target_pairs={{0,224},{32,0},{64,32},{96,64},{128,96},{160,128},{192,160},{224,1... | collective-permute-start | bytes 589832 | tf_op jit(solution)/shard_map/ppermute | solution.py:74
  109.3 6.4 %collective-permute-start.17 = (f32[384,128]{1,0:T(8,128)}, f32[384,128]{1,0:T(8,128)}, u32[]{:S(2)}, u32[]{:S(2)}) collective-permute-start(f32[384,128]{1,0:T(8,128)} %collective-permute-done.16.a3), channel_id=1, source_target_pairs={{0,32},{32,64},{64,96},{96,128},{128,160},{160,192},{192,224},{224... | collective-permute-start | bytes 589832 | tf_op jit(solution)/shard_map/ppermute | solution.py:74
  115.6 14.1 %copy-start = (f32[384,128]{1,0:T(8,128)S(1)}, f32[384,128]{1,0:T(8,128)}, u32[]{:S(2)}) copy-start(f32[384,128]{1,0:T(8,128)} %get-tuple-element.53.defect_ref) | copy-start | bytes 589828
  129.8 10.5 %copy-start.17 = (f32[256]{0:T(256)S(1)}, f32[256]{0:T(256)}, u32[]{:S(2)}) copy-start(f32[256]{0:T(256)} %param.15) | copy-start | bytes 3076
  129.8 11.2 %copy-start.3 = (f32[96,256]{1,0:T(8,128)S(1)}, f32[96,256]{1,0:T(8,128)}, u32[]{:S(2)}) copy-start(f32[96,256]{1,0:T(8,128)} %direction_ref) | copy-start | bytes 294916
  129.8 11.2 %copy-start.4 = (f32[96,256]{1,0:T(8,128)S(1)}, f32[96,256]{1,0:T(8,128)}, u32[]{:S(2)}) copy-start(f32[96,256]{1,0:T(8,128)} %residual_ref) | copy-start | bytes 294916
  129.8 11.2 %copy-start.13 = (f32[96,256]{1,0:T(8,128)S(1)}, f32[96,256]{1,0:T(8,128)}, u32[]{:S(2)}) copy-start(f32[96,256]{1,0:T(8,128)} %param.12) | copy-start | bytes 294916

commit v3 on v2

--- a/solution.py
+++ b/solution.py
@@ -167,8 +167,8 @@
 
 
 def map_plane(
-    x_ref, c_ref, m0, m1, m2, m3, n0, n1, n2, n3, maps_ref, states_f_ref, states_b_ref, plane_ref,
-    all_scr, f_scr
+    x_ref, c_ref, m0, m1, m2, m3, n0, n1, n2, n3, maps_ref, states_f_ref, states_b_ref, half_ref,
+    all_scr, f_scr, plane_ref
 ):
     for step, (mine, other) in enumerate(((m0, n0), (m1, n1), (m2, n2), (m3, n3))):
         at = 2 * ((x_ref[0] + 4 - step) % 4)
@@ -193,6 +193,9 @@
         b = mm(plane_ref[128:384], kept(maps_ref, i, slice(128, 256)), 1)
         plane_ref[128:256] = b[0:128]
         plane_ref[256:384] = b[128:256] + f_scr[i]
+    for m in range(3):
+        own = pl.ds(pl.multiple_of(128 * m + 64 * c_ref[0], 8), 64)
+        half_ref[64 * m : 64 * m + 64] = plane_ref[own]
 
 
 def in_lanes(values, place):
@@ -248,11 +251,18 @@
 
 
 def solve_planes(
-    z_ref, place_ref, sums_ref, a0, a1, a2, a3, a4, b1, b2, b3,
+    c_ref, z_ref, place_ref, sums_ref, p0, p1, p2, p3, p4, p5, p6, p7, q0, q1, q2, q3, q4, q5, q6, q7,
     states_f_ref, states_b_ref, own_f_ref, own_b_ref, out_ref, total_ref, maps_scr, f_scr, b_scr
 ):
-    for step, piece in ((0, a0), (1, a1), (2, a2), (3, a3), (4, a4), (-1, b1), (-2, b2), (-3, b3)):
-        maps_scr[(z_ref[0] + 8 - step) % 8] = piece[...]
+    mine = (p0, p1, p2, p3, p4, p5, p6, p7)
+    theirs = (q0, q1, q2, q3, q4, q5, q6, q7)
+    for step, own, other in zip((0, 1, -1, 2, -2, 3, -3, 4), mine, theirs):
+        z = (z_ref[0] + 8 - step) % 8
+        for m in range(3):
+            own_rows = pl.ds(pl.multiple_of(128 * m + 64 * c_ref[0], 8), 64)
+            other_rows = pl.ds(pl.multiple_of(128 * m + 64 - 64 * c_ref[0], 8), 64)
+            maps_scr[z, own_rows] = own[64 * m : 64 * m + 64]
+            maps_scr[z, other_rows] = other[64 * m : 64 * m + 64]
     f_scr[0] = jnp.zeros((16, 128), jnp.float32)
     f_scr[1] = sums_ref[0, 0:16]
     for z in range(1, 7):
@@ -293,7 +303,7 @@
         out_ref[i, 32:40] = dots
 
 
-def finish(got_ref, back_ref, total_ref, rho_ref, defect_ref, x_ref, s_ref, out_ref):
+def finish(grp_ref, got_ref, back_ref, total_ref, rho_ref, defect_ref, x_ref, s_ref, out_ref):
     def rows(start):
         return jnp.concatenate(
             [back_ref[p, start : start + 8] for p in range(8)]
@@ -307,7 +317,10 @@
     rest = defect_ref[...] - mm(got_ref[:, 512:640], rows(0), 1)
     precond = s_ref[...] + mm(got_ref[:, 128:512], rest) - mm(got_ref[:, 640:768], rows(16), 1)
     total = total_ref[...]
-    step = rho_ref[...] / total[2:3, 0:64]
+    own_rho = rho_ref[:, 0:64]
+    for q in range(1, 4):
+        own_rho = jnp.where(grp_ref[0] == q, rho_ref[:, 64 * q : 64 * q + 64], own_rho)
+    step = own_rho / total[2:3, 0:64]
     same = total[0:1] + dots[0:1]
     cross = total[1:2] + dots[1:2]
     rho = same[:, 0:64] - step * (cross[:, 0:64] + cross[:, 64:128]) + step * (step * same[:, 64:128])
@@ -338,9 +351,8 @@
 
     part = 64
     grp, at_x, at_c, at_z, place = (here(axes) for axes in ("grp", "slab_1", "slab_2", "slab_0", PLANE))
-    own_rho = lax.dynamic_slice_in_dim(prior_rho, part * grp[0], part).reshape(1, part)
-    grp, at_x, at_c, at_z, place, own_rho, direction, residual = lax.optimization_barrier(
-        (grp, at_x, at_c, at_z, place, own_rho, direction, residual)
+    grp, at_x, at_c, at_z, place, direction, residual = lax.optimization_barrier(
+        (grp, at_x, at_c, at_z, place, direction, residual)
     )
     operator = jnp.concatenate([diag_blocks, lower_coupling, upper_coupling, jacobi_inverse], axis=1)
     got = to_each(
@@ -352,7 +364,9 @@
         ),
         "grp",
     ).reshape(384, 768)
-    pieces = [operator] + [ring(operator, "grp", step) for step in (1, 2, 3)]
+    bulk_up = ring(operator, "grp", 1)
+    bulk_down = ring(operator, "grp", 3)
+    bulk = [operator, bulk_up, ring(bulk_down, "grp", 3), bulk_down]
     factor, maps, faces = call(
         make_maps,
         (shaped(384, 128), shaped(256, 128), shaped(64, 128)),
@@ -371,7 +385,7 @@
         interface,
         grp,
         got,
-        *pieces,
+        *bulk,
         below,
         above,
     )
@@ -383,7 +397,7 @@
         interface,
         grp,
         got,
-        *pieces,
+        *bulk,
         factor,
         x,
         s,
@@ -391,27 +405,33 @@
         above,
         scratch=[pltpu.VMEM((384, 128), jnp.float32), pltpu.VMEM((128, 128), jnp.float32)],
     )
-    maps, states_f, states_b, plane = call(
+    maps, states_f, states_b, half = call(
         map_plane,
         (
             stored(2, 8, 256, 128, dtype=jnp.bfloat16),
             shaped(2, 8, 128, 128, dtype=jnp.bfloat16),
             shaped(2, 8, 256, 128, dtype=jnp.bfloat16),
-            shaped(384, 128),
+            shaped(192, 128),
         ),
         2,
         at_x,
         at_c,
-        *map(far, along),
-        *map(far, across),
-        scratch=[pltpu.VMEM((8, 256, 128), jnp.float32), pltpu.VMEM((8, 128, 128), jnp.float32)],
-    )
-    ups = [plane]
+        *along,
+        *across,
+        scratch=[
+            pltpu.VMEM((8, 256, 128), jnp.float32),
+            pltpu.VMEM((8, 128, 128), jnp.float32),
+            pltpu.VMEM((384, 128), jnp.float32),
+        ],
+    )
+    ups = [half]
     for _ in range(1, 5):
         ups.append(ring(ups[-1], "slab_0", 1))
-    downs = [plane]
+    downs = [half]
     for _ in range(1, 4):
         downs.append(ring(downs[-1], "slab_0", -1))
+    pieces = [half, ups[1], downs[1], ups[2], downs[2], ups[3], downs[3], ups[4]]
+    others = [ring(piece, "slab_2", 1) for piece in pieces]
     own_f, own_b, sums = call(
         sweep_plane,
         (stored(9, 16, 128), stored(8, 16, 128), stored(8, 72, 128)),
@@ -425,12 +445,13 @@
     entering, total = call(
         solve_planes,
         (shaped(8, 40, 128), shaped(8, 128)),
-        2,
+        3,
+        at_c,
         at_z,
         place,
         to_each(sums, "slab_0"),
-        *map(far, ups),
-        *map(far, downs[1:]),
+        *map(far, pieces),
+        *map(far, others),
         states_f,
         states_b,
         far(own_f),
@@ -445,11 +466,12 @@
         call(
             finish,
             shaped(4, 104, 128),
-            0,
+            1,
+            grp,
             got,
             to_each(entering, PLANE),
             total,
-            own_rho,
+            prior_rho.reshape(1, 4 * part),
             defect,
             x,
             s,

time: 143 us -> 143 us (level)
  waiting for transfers between devices: 35.2 us -> 30.4 us
  local copies, waits for them, and re-layouts: 1.03 us -> 5.54 us
  starting transfers between devices: 62 us -> 64.7 us
  blocking collectives: 19.9 us -> 18 us
    all_to_all x3, waiting for transfers between devices: 14.9 us -> 0.01 us  [to_each(): return lax.all_to_all(pieces, axes, split_axis=0, concat_axis=0, tiled=True)]
    ppermute x17 -> x25, waiting for transfers between devices: 19.1 us -> 29.4 us  [ring(): lax.ppermute(x, axis, [(i, (i + step) % count) for i in range(count)])]
    unnamed x39 -> x65, local copies, waits for them, and re-layouts: 0.09 us -> 5.35 us
    ppermute x17 -> x25, starting transfers between devices: 27.9 us -> 30.1 us  [ring(): lax.ppermute(x, axis, [(i, (i + step) % count) for i in range(count)])]
    ppermute x2, starting transfers between devices: 4.18 us -> 6.4 us  [beside(): above = lax.ppermute(faces, SLAB, [(i + 1, i) for i in range(count - 1)])]
    all_to_all x3, starting transfers between devices: 23 us -> 21 us  [to_each(): return lax.all_to_all(pieces, axes, split_axis=0, concat_axis=0, tiled=True)]
    all_to_all x2, blocking collectives: 19.9 us -> 18 us  [to_each(): return lax.all_to_all(pieces, axes, split_axis=0, concat_axis=0, tiled=True)]
  transfers between devices with their start and end apart: 24 -> 32, of which waited for: 8 -> 7; matrix products, arithmetic and copies ran while one was open for 0% -> 0% of each run, Pallas kernels for 9% -> 6%
where the time goes in v3:
time: 143 us; the launch traced here: 142 us
  starting transfers between devices  64.7 us (45%)
  waiting for transfers between devices  30.4 us (21%)
  Pallas kernels  20.9 us (15%)
  blocking collectives  18 us (13%)
  local copies, waits for them, and re-layouts  5.54 us (4%)
  other arithmetic  1.46 us (1%)
    ppermute x25, starting transfers between devices, ring(): lax.ppermute(x, axis, [(i, (i + step) % count) for i in range(count)])  30.1 us
    ppermute x25, waiting for transfers between devices, ring(): lax.ppermute(x, axis, [(i, (i + step) % count) for i in range(count)])  29.4 us
    all_to_all x3, starting transfers between devices, to_each(): return lax.all_to_all(pieces, axes, split_axis=0, concat_axis=0, tiled=True)  21 us
    pallas_call x8, Pallas kernels, call(): pl.pallas_call(body, out_shape=outs, in_specs=[SMEM] * smem + [VMEM] * (l...  20.9 us
    all_to_all x2, blocking collectives, to_each(): return lax.all_to_all(pieces, axes, split_axis=0, concat_axis=0, tiled=True)  18 us
    ppermute x2, starting transfers between devices, beside(): below = lax.ppermute(faces, SLAB, [(i, i + 1) for i in range(count - 1)])  7.25 us
    ppermute x2, starting transfers between devices, beside(): above = lax.ppermute(faces, SLAB, [(i + 1, i) for i in range(count - 1)])  6.4 us
    unnamed x65, local copies, waits for them, and re-layouts  5.35 us
  transfers between devices with their start and end apart: 32, of which 7 were waited for; matrix products, arithmetic and copies ran while one was open for 0% of the time, Pallas kernels for 6%

profile of v3, /device:TPU:1, one launch (start us, length us, event | category | flops | bytes accessed | tf_op | source)
XLA Modules:
  0.0 142.0 jit_solution(9258743017995043110)
XLA Ops:
  0.6 2.2 %shard_map.147 = f32[4,96,768]{2,1,0:T(8,128)} custom-call(f32[96,256]{1,0:T(8,128)} %direction_ref, f32[96,256]{1,0:T(8,128)} %residual_ref, f32[96,384]{1,0:T(8,128)} %inverse_ref.1, f32[96,128]{1,0:T(8,128)} %lower_ref.1, f32[96,128]{1,0:T(8,128)} %upper_ref.1), custom_call_target="tpu_custom_call" | custom-call | tf_op jit(solution)/shard_map/pallas_call | solution.py:54
  2.8 0.0 copy-start.8
  2.8 5.1 %all-to-all-start = ((f32[4,96,768]{2,1,0:T(8,128)}), f32[4,96,768]{2,1,0:T(8,128)S(1)}, u32[]{:S(2)}, u32[]{:S(2)}) async-start(f32[4,96,768]{2,1,0:T(8,128)} %shard_map.147), calls=%async_computation | async-start | bytes 2359296 | tf_op jit(solution)/shard_map/all_to_all | solution.py:69
  8.1 2.8 %collective-permute-start.1 = (f32[96,736]{1,0:T(8,128)S(1)}, f32[96,736]{1,0:T(8,128)S(1)}, u32[]{:S(2)}, u32[]{:S(2)}) collective-permute-start(f32[96,736]{1,0:T(8,128)S(1)} %constant_dynamic-update-slice_fusion.p0), channel_id=1, source_target_pairs={{0,3},{1,0},{2,1},{3,2},{4,7},{5,4},{6,5},{7,6},{8,11},{9,8},{10,9... | collective-permute-start | bytes 847880 | tf_op jit(solution)/shard_map/ppermute | solution.py:74
  10.8 0.0 collective-permute-start
  10.8 16.9 %collective-permute-done.1.p3 = f32[96,736]{1,0:T(8,128)S(1)} collective-permute-done((f32[96,736]{1,0:T(8,128)S(1)}, f32[96,736]{1,0:T(8,128)S(1)}, u32[]{:S(2)}, u32[]{:S(2)}) %collective-permute-start.1) | collective-permute-done | bytes 282656 | tf_op jit(solution)/shard_map/ppermute | solution.py:74
  27.7 1.4 %collective-permute-start.2 = (f32[96,736]{1,0:T(8,128)S(1)}, f32[96,736]{1,0:T(8,128)S(1)}, u32[]{:S(2)}, u32[]{:S(2)}) collective-permute-start(f32[96,736]{1,0:T(8,128)S(1)} %collective-permute-done.1.p3), channel_id=1, source_target_pairs={{0,3},{1,0},{2,1},{3,2},{4,7},{5,4},{6,5},{7,6},{8,11},{9,8},{10,9... | collective-permute-start | bytes 847880 | tf_op jit(solution)/shard_map/ppermute | solution.py:74
  29.2 0.0 all-to-all-done
  29.2 1.1 shard_map.148
  30.3 4.5 %collective-permute-start.4 = (f32[64,128]{1,0:T(8,128)S(1)}, f32[64,128]{1,0:T(8,128)S(1)}, u32[]{:S(2)}, u32[]{:S(2)}) collective-permute-start(f32[64,128]{1,0:T(8,128)S(1)} %get-tuple-element.35), channel_id=1, source_target_pairs={{4,0},{8,4},{12,8},{16,12},{20,16},{24,20},{28,24},{32,28},{36,32}... | collective-permute-start | bytes 98312 | tf_op jit(solution)/shard_map/ppermute | solution.py:80
  34.8 3.0 %collective-permute-start.3 = (f32[64,128]{1,0:T(8,128)S(1)}, f32[64,128]{1,0:T(8,128)S(1)}, u32[]{:S(2)}, u32[]{:S(2)}) collective-permute-start(f32[64,128]{1,0:T(8,128)S(1)} %get-tuple-element.35), channel_id=1, source_target_pairs={{0,4},{4,8},{8,12},{12,16},{16,20},{20,24},{24,28},{28,32},{32,36}... | collective-permute-start | bytes 98312 | tf_op jit(solution)/shard_map/ppermute | solution.py:79
  37.8 0.0 collective-permute-done.2.p2
  37.9 1.0 collective-permute-done.3.below_ref
  38.8 1.4 %shard_map.149 = (f32[384,128]{1,0:T(8,128)S(1)}, f32[384,128]{1,0:T(8,128)S(1)}, f32[128,128]{1,0:T(8,128)S(1)}) custom-call(s32[1,128]{1,0:T(1,128)S(1)} %copy-done.8, s32[1]{0:T(128)} %bitcast.grp_ref, f32[384,768]{1,0:T(8,128)S(1)} %bitcast.40, f32[96,736]{1,0:T(8,128)S(1)} %constant_dynamic-update-slice_fusion.p0, ...), custom_call_target="tpu_custom_call" | custom-call | tf_op jit(solution)/shard_map/pallas_call | solution.py:54
  40.3 1.9 %collective-permute-start.6 = (f32[128,128]{1,0:T(8,128)S(1)}, f32[128,128]{1,0:T(8,128)S(1)}, u32[]{:S(2)}, u32[]{:S(2)}) collective-permute-start(f32[128,128]{1,0:T(8,128)S(1)} %get-tuple-element.38), channel_id=1, source_target_pairs={{4,0},{8,4},{12,8},{16,12},{20,16},{24,20},{28,24},{32,28},{36,32}... | collective-permute-start | bytes 196616 | tf_op jit(solution)/shard_map/ppermute | solution.py:80
  42.2 4.2 %collective-permute-start.5 = (f32[128,128]{1,0:T(8,128)S(1)}, f32[128,128]{1,0:T(8,128)S(1)}, u32[]{:S(2)}, u32[]{:S(2)}) collective-permute-start(f32[128,128]{1,0:T(8,128)S(1)} %get-tuple-element.38), channel_id=1, source_target_pairs={{0,4},{4,8},{8,12},{12,16},{16,20},{20,24},{24,28},{28,32},{32,36}... | collective-permute-start | bytes 196616 | tf_op jit(solution)/shard_map/ppermute | solution.py:79
  46.4 5.6 %collective-permute-start.9 = (f32[256,128]{1,0:T(8,128)S(1)}, f32[256,128]{1,0:T(8,128)S(1)}, u32[]{:S(2)}, u32[]{:S(2)}) collective-permute-start(f32[256,128]{1,0:T(8,128)S(1)} %get-tuple-element.41.m0), channel_id=1, source_target_pairs={{0,24},{8,0},{16,8},{24,16},{1,25},{9,1},{17,9},{25,17},{2,26},{10... | collective-permute-start | bytes 393224 | tf_op jit(solution)/shard_map/ppermute | solution.py:74
  52.0 0.7 collective-permute-start.7
  52.7 0.0 collective-permute-done.5.below_ref
  52.7 2.5 %shard_map.150 = (f32[384,128]{1,0:T(8,128)}, f32[8,56,128]{2,1,0:T(8,128)}) custom-call(s32[1,128]{1,0:T(1,128)S(1)} %copy-done.8, s32[1]{0:T(128)} %bitcast.grp_ref, f32[384,768]{1,0:T(8,128)S(1)} %bitcast.41, f32[96,736]{1,0:T(8,128)S(1)} %constant_dynamic-update-slice_fusion.p0, f32[96,736]{1,0:T(8,128)S(1)} %collective-permute-done.p1, ...), custom_call_target="tpu_custom_call" | custom-call | tf_op jit(solution)/shard_map/pallas_call | solution.py:54
  55.2 4.0 %all-to-all-start.1 = ((f32[8,56,128]{2,1,0:T(8,128)}), f32[8,56,128]{2,1,0:T(8,128)S(1)}, u32[]{:S(2)}, u32[]{:S(2)}) async-start(f32[8,56,128]{2,1,0:T(8,128)} %get-tuple-element.39), calls=%async_computation.1 | async-start | bytes 458752 | tf_op jit(solution)/shard_map/all_to_all | solution.py:69
  59.2 0.1 collective-permute-start.10
  59.3 0.4 collective-permute-start.13
  59.7 0.7 copy-done.3
  60.3 0.1 collective-permute-start.12
  60.4 0.7 copy-done.5
  61.1 0.4 collective-permute-start.11
  61.5 0.2 collective-permute-done.12.n2
  61.7 1.0 collective-permute-done.11.n1
  62.7 0.9 copy-done.2
  63.6 0.9 copy-done.4
  64.5 0.9 copy-done.6
  65.4 4.5 %shard_map.151 = (bf16[2,8,256,128]{3,2,1,0:T(8,128)(2,1)}, bf16[2,8,128,128]{3,2,1,0:T(8,128)(2,1)S(1)}, bf16[2,8,256,128]{3,2,1,0:T(8,128)(2,1)S(1)}, f32[192,128]{1,0:T(8,128)S(1)}) custom-call(s32[1]{0:T(128)} %bitcast.1.x_ref, s32[1]{0:T(128)} %bitcast.2.c_ref, f32[256,128]{1,0:T(8,128)S(1)} %copy-done.2, f32[256,128]{1,0:T(8,128)} %collective-permute-done.7.m1, ...), custom_call_target="tpu_custom_call" | custom-call | tf_op jit(solution)/shard_map/pallas_call | solution.py:54
  69.9 4.6 %shard_map.152 = (f32[9,16,128]{2,1,0:T(8,128)}, f32[8,16,128]{2,1,0:T(8,128)}, f32[8,72,128]{2,1,0:T(8,128)}) custom-call(s32[1]{0:T(128)} %bitcast.4.place_ref, f32[8,56,128]{2,1,0:T(8,128)S(1)} %all-to-all-done.1.got_ref, bf16[2,8,256,128]{3,2,1,0:T(8,128)(2,1)} %get-tuple-element.42.maps_ref, ...), custom_call_target="tpu_custom_call" | custom-call | tf_op jit(solution)/shard_map/pallas_call | solution.py:54
  74.5 11.9 %all-to-all-start.2 = ((f32[8,72,128]{2,1,0:T(8,128)}), f32[8,72,128]{2,1,0:T(8,128)S(1)}, u32[]{:S(2)}, u32[]{:S(2)}) async-start(f32[8,72,128]{2,1,0:T(8,128)} %get-tuple-element.45), calls=%async_computation.2 | async-start | bytes 589824 | tf_op jit(solution)/shard_map/all_to_all | solution.py:69
  86.4 1.5 %collective-permute-start.14 = (f32[192,128]{1,0:T(8,128)S(1)}, f32[192,128]{1,0:T(8,128)S(1)}, u32[]{:S(2)}, u32[]{:S(2)}) collective-permute-start(f32[192,128]{1,0:T(8,128)S(1)} %get-tuple-element.46.p0), channel_id=1, source_target_pairs={{0,32},{32,64},{64,96},{96,128},{128,160},{160,192},{192,224},{224... | collective-permute-start | bytes 294920 | tf_op jit(solution)/shard_map/ppermute | solution.py:74
  87.8 1.2 collective-permute-start.15
  89.0 7.7 %collective-permute-done.14.p1 = f32[192,128]{1,0:T(8,128)S(1)} collective-permute-done((f32[192,128]{1,0:T(8,128)S(1)}, f32[192,128]{1,0:T(8,128)S(1)}, u32[]{:S(2)}, u32[]{:S(2)}) %collective-permute-start.14) | collective-permute-done | bytes 98336 | tf_op jit(solution)/shard_map/ppermute | solution.py:74
  96.7 0.0 copy-start.14
  96.7 2.7 %collective-permute-start.17 = (f32[192,128]{1,0:T(8,128)S(1)}, f32[192,128]{1,0:T(8,128)S(1)}, u32[]{:S(2)}, u32[]{:S(2)}) collective-permute-start(f32[192,128]{1,0:T(8,128)S(1)} %collective-permute-done.15.p2), channel_id=1, source_target_pairs={{0,224},{32,0},{64,32},{96,64},{128,96},{160,128},{192,160},{224,1... | collective-permute-start | bytes 294920 | tf_op jit(solution)/shard_map/ppermute | solution.py:74
  99.4 2.0 %collective-permute-done.16.p3 = f32[192,128]{1,0:T(8,128)S(1)} collective-permute-done((f32[192,128]{1,0:T(8,128)S(1)}, f32[192,128]{1,0:T(8,128)S(1)}, u32[]{:S(2)}, u32[]{:S(2)}) %collective-permute-start.16) | collective-permute-done | bytes 98336 | tf_op jit(solution)/shard_map/ppermute | solution.py:74
  101.4 3.3 %collective-permute-start.21 = (f32[192,128]{1,0:T(8,128)S(1)}, f32[192,128]{1,0:T(8,128)S(1)}, u32[]{:S(2)}, u32[]{:S(2)}) collective-permute-start(f32[192,128]{1,0:T(8,128)S(1)} %get-tuple-element.46.p0), channel_id=1, source_target_pairs={{0,4},{4,0},{1,5},{5,1},{2,6},{6,2},{3,7},{7,3},{8,12},{12,8},{9,1... | collective-permute-start | bytes 294920 | tf_op jit(solution)/shard_map/ppermute | solution.py:74
  104.8 0.1 collective-permute-start.23
  104.9 0.4 collective-permute-start.22
  105.3 2.9 %collective-permute-start.19 = (f32[192,128]{1,0:T(8,128)S(1)}, f32[192,128]{1,0:T(8,128)S(1)}, u32[]{:S(2)}, u32[]{:S(2)}) collective-permute-start(f32[192,128]{1,0:T(8,128)S(1)} %collective-permute-done.17.p4), channel_id=1, source_target_pairs={{0,224},{32,0},{64,32},{96,64},{128,96},{160,128},{192,160},{224,1... | collective-permute-start | bytes 294920 | tf_op jit(solution)/shard_map/ppermute | solution.py:74
  108.2 2.4 %collective-permute-start.25 = (f32[192,128]{1,0:T(8,128)S(1)}, f32[192,128]{1,0:T(8,128)S(1)}, u32[]{:S(2)}, u32[]{:S(2)}) collective-permute-start(f32[192,128]{1,0:T(8,128)S(1)} %collective-permute-done.17.p4), channel_id=1, source_target_pairs={{0,4},{4,0},{1,5},{5,1},{2,6},{6,2},{3,7},{7,3},{8,12},{12,8},{9,1... | collective-permute-start | bytes 294920 | tf_op jit(solution)/shard_map/ppermute | solution.py:74
  110.6 0.1 collective-permute-start.24
  110.7 0.4 collective-permute-start.26
  111.1 0.1 collective-permute-start.27
  111.2 1.6 %collective-permute-done.20.p7 = f32[192,128]{1,0:T(8,128)S(1)} collective-permute-done((f32[192,128]{1,0:T(8,128)S(1)}, f32[192,128]{1,0:T(8,128)S(1)}, u32[]{:S(2)}, u32[]{:S(2)}) %collective-permute-start.20) | collective-permute-done | bytes 98336 | tf_op jit(solution)/shard_map/ppermute | solution.py:74
  112.8 3.5 %collective-permute-start.28 = (f32[192,128]{1,0:T(8,128)S(1)}, f32[192,128]{1,0:T(8,128)}, u32[]{:S(2)}, u32[]{:S(2)}) collective-permute-start(f32[192,128]{1,0:T(8,128)S(1)} %collective-permute-done.20.p7), channel_id=1, source_target_pairs={{0,4},{4,0},{1,5},{5,1},{2,6},{6,2},{3,7},{7,3},{8,12},{12,8},{9,1... | collective-permute-start | bytes 294920 | tf_op jit(solution)/shard_map/ppermute | solution.py:74
  116.5 0.5 copy-done.24
  117.0 0.0 copy-done.26
  117.0 0.6 copy-done.25
  117.7 0.0 copy-start.9
  117.7 3.8 %shard_map.153 = (f32[8,40,128]{2,1,0:T(8,128)S(1)}, f32[8,128]{1,0:T(8,128)S(1)}) custom-call(s32[1]{0:T(128)} %bitcast.2.c_ref, s32[1]{0:T(128)} %bitcast.3.z_ref, s32[1]{0:T(128)} %bitcast.4.place_ref, f32[8,72,128]{2,1,0:T(8,128)S(1)} %all-to-all-done.2.sums_ref, f32[192,128]{1,0:T(8,128)} %copy-done.7, f32[192,128]{1,0:T(8,128)} %copy-done.13, ...), custom_call_target="tpu_custom_call" | custom-call | tf_op jit(solution)/shard_map/pallas_call | solution.py:54
  121.5 10.1 %all_to_all.25.back_ref = f32[8,40,128]{2,1,0:T(8,128)S(1)} all-to-all(f32[8,40,128]{2,1,0:T(8,128)S(1)} %get-tuple-element.49), channel_id=1, replica_groups=mesh['slab_0'=8,'slab_1'=4,'slab_2'=2,'grp'=4] {'slab_1','slab_2'}, dimensions={0} | all-to-all | bytes 327680 | tf_op jit(solution)/shard_map/all_to_all | solution.py:69
  131.6 0.0 copy-start.27
  131.6 0.9 shard_map.154
  132.5 7.8 %all_to_all.26 = f32[4,104,128]{2,1,0:T(8,128)S(1)} all-to-all(f32[4,104,128]{2,1,0:T(8,128)S(1)} %shard_map.154), channel_id=1, replica_groups=mesh['slab_0'=8,'slab_1'=4,'slab_2'=2,'grp'=4] {'grp'}, dimensions={0} | all-to-all | bytes 425984 | tf_op jit(solution)/shard_map/all_to_all | solution.py:69
  140.3 0.1 slice_bitcast_fusion.11
  140.4 0.6 fusion.1
  141.0 0.1 slice_bitcast_fusion.3
  141.2 0.8 maximum_add_fusion
  (80 shorter events, 0.2 us)
Async XLA Ops:
  2.8 5.2 %copy-start.12 = (f32[96,384]{1,0:T(8,128)S(1)}, f32[96,384]{1,0:T(8,128)}, u32[]{:S(2)}) copy-start(f32[96,384]{1,0:T(8,128)} %param.16) | copy-start | bytes 442372
  2.8 5.2 %copy-start.28 = (f32[96,128]{1,0:T(8,128)S(1)}, f32[96,128]{1,0:T(8,128)}, u32[]{:S(2)}) copy-start(f32[96,128]{1,0:T(8,128)} %param.17) | copy-start | bytes 147460
  2.8 5.2 %copy-start.29 = (f32[96,128]{1,0:T(8,128)S(1)}, f32[96,128]{1,0:T(8,128)}, u32[]{:S(2)}) copy-start(f32[96,128]{1,0:T(8,128)} %param.18) | copy-start | bytes 147460
  2.8 5.2 %copy-start.30 = (f32[96,96]{1,0:T(8,128)S(1)}, f32[96,96]{1,0:T(8,128)}, u32[]{:S(2)}) copy-start(f32[96,96]{1,0:T(8,128)} %param.20) | copy-start | bytes 110596
  2.8 26.3 %copy-start.8 = (s32[1,128]{1,0:T(1,128)S(1)}, s32[1,128]{1,0:T(1,128)}, u32[]{:S(2)}) copy-start(s32[1,128]{1,0:T(1,128)} %index_ref.5) | copy-start | bytes 1540
  2.8 26.3 %all-to-all-start = ((f32[4,96,768]{2,1,0:T(8,128)}), f32[4,96,768]{2,1,0:T(8,128)S(1)}, u32[]{:S(2)}, u32[]{:S(2)}) async-start(f32[4,96,768]{2,1,0:T(8,128)} %shard_map.147), calls=%async_computation | async-start | bytes 2359296 | tf_op jit(solution)/shard_map/all_to_all | solution.py:69
  8.1 19.7 %collective-permute-start.1 = (f32[96,736]{1,0:T(8,128)S(1)}, f32[96,736]{1,0:T(8,128)S(1)}, u32[]{:S(2)}, u32[]{:S(2)}) collective-permute-start(f32[96,736]{1,0:T(8,128)S(1)} %constant_dynamic-update-slice_fusion.p0), channel_id=1, source_target_pairs={{0,3},{1,0},{2,1},{3,2},{4,7},{5,4},{6,5},{7,6},{8,11},{9,8},{10,9... | collective-permute-start | bytes 847880 | tf_op jit(solution)/shard_map/ppermute | solution.py:74
  10.8 27.0 %collective-permute-start = (f32[96,736]{1,0:T(8,128)S(1)}, f32[96,736]{1,0:T(8,128)S(1)}, u32[]{:S(2)}, u32[]{:S(2)}) collective-permute-start(f32[96,736]{1,0:T(8,128)S(1)} %constant_dynamic-update-slice_fusion.p0), channel_id=1, source_target_pairs={{0,1},{1,2},{2,3},{3,0},{4,5},{5,6},{6,7},{7,4},{8,9},{9,10},{10,1... | collective-permute-start | bytes 847880 | tf_op jit(solution)/shard_map/ppermute | solution.py:74
  27.7 10.1 %collective-permute-start.2 = (f32[96,736]{1,0:T(8,128)S(1)}, f32[96,736]{1,0:T(8,128)S(1)}, u32[]{:S(2)}, u32[]{:S(2)}) collective-permute-start(f32[96,736]{1,0:T(8,128)S(1)} %collective-permute-done.1.p3), channel_id=1, source_target_pairs={{0,3},{1,0},{2,1},{3,2},{4,7},{5,4},{6,5},{7,6},{8,11},{9,8},{10,9... | collective-permute-start | bytes 847880 | tf_op jit(solution)/shard_map/ppermute | solution.py:74
  30.3 28.9 %copy-start.1 = (f32[256,128]{1,0:T(8,128)}, f32[256,128]{1,0:T(8,128)S(1)}, u32[]{:S(2)}) copy-start(f32[256,128]{1,0:T(8,128)S(1)} %get-tuple-element.41.m0) | copy-start | bytes 393220
  30.3 7.5 %collective-permute-start.4 = (f32[64,128]{1,0:T(8,128)S(1)}, f32[64,128]{1,0:T(8,128)S(1)}, u32[]{:S(2)}, u32[]{:S(2)}) collective-permute-start(f32[64,128]{1,0:T(8,128)S(1)} %get-tuple-element.35), channel_id=1, source_target_pairs={{4,0},{8,4},{12,8},{16,12},{20,16},{24,20},{28,24},{32,28},{36,32}... | collective-permute-start | bytes 98312 | tf_op jit(solution)/shard_map/ppermute | solution.py:80
  34.8 4.0 %collective-permute-start.3 = (f32[64,128]{1,0:T(8,128)S(1)}, f32[64,128]{1,0:T(8,128)S(1)}, u32[]{:S(2)}, u32[]{:S(2)}) collective-permute-start(f32[64,128]{1,0:T(8,128)S(1)} %get-tuple-element.35), channel_id=1, source_target_pairs={{0,4},{4,8},{8,12},{12,16},{16,20},{20,24},{24,28},{28,32},{32,36}... | collective-permute-start | bytes 98312 | tf_op jit(solution)/shard_map/ppermute | solution.py:79
  40.3 12.4 %collective-permute-start.6 = (f32[128,128]{1,0:T(8,128)S(1)}, f32[128,128]{1,0:T(8,128)S(1)}, u32[]{:S(2)}, u32[]{:S(2)}) collective-permute-start(f32[128,128]{1,0:T(8,128)S(1)} %get-tuple-element.38), channel_id=1, source_target_pairs={{4,0},{8,4},{12,8},{16,12},{20,16},{24,20},{28,24},{32,28},{36,32}... | collective-permute-start | bytes 196616 | tf_op jit(solution)/shard_map/ppermute | solution.py:80
  42.2 10.5 %collective-permute-start.5 = (f32[128,128]{1,0:T(8,128)S(1)}, f32[128,128]{1,0:T(8,128)S(1)}, u32[]{:S(2)}, u32[]{:S(2)}) collective-permute-start(f32[128,128]{1,0:T(8,128)S(1)} %get-tuple-element.38), channel_id=1, source_target_pairs={{0,4},{4,8},{8,12},{12,16},{16,20},{20,24},{24,28},{28,32},{32,36}... | collective-permute-start | bytes 196616 | tf_op jit(solution)/shard_map/ppermute | solution.py:79
  46.4 12.8 %collective-permute-start.9 = (f32[256,128]{1,0:T(8,128)S(1)}, f32[256,128]{1,0:T(8,128)S(1)}, u32[]{:S(2)}, u32[]{:S(2)}) collective-permute-start(f32[256,128]{1,0:T(8,128)S(1)} %get-tuple-element.41.m0), channel_id=1, source_target_pairs={{0,24},{8,0},{16,8},{24,16},{1,25},{9,1},{17,9},{25,17},{2,26},{10... | collective-permute-start | bytes 393224 | tf_op jit(solution)/shard_map/ppermute | solution.py:74
  52.0 8.3 %collective-permute-start.8 = (f32[256,128]{1,0:T(8,128)S(1)}, f32[256,128]{1,0:T(8,128)S(1)}, u32[]{:S(2)}, u32[]{:S(2)}) collective-permute-start(f32[256,128]{1,0:T(8,128)S(1)} %get-tuple-element.41.m0), channel_id=1, source_target_pairs={{0,16},{8,24},{16,0},{24,8},{1,17},{9,25},{17,1},{25,9},{2,18},{10... | collective-permute-start | bytes 393224 | tf_op jit(solution)/shard_map/ppermute | solution.py:74
  52.0 9.1 %collective-permute-start.7 = (f32[256,128]{1,0:T(8,128)S(1)}, f32[256,128]{1,0:T(8,128)}, u32[]{:S(2)}, u32[]{:S(2)}) collective-permute-start(f32[256,128]{1,0:T(8,128)S(1)} %get-tuple-element.41.m0), channel_id=1, source_target_pairs={{0,8},{8,16},{16,24},{24,0},{1,9},{9,17},{17,25},{25,1},{2,10},{10... | collective-permute-start | bytes 393224 | tf_op jit(solution)/shard_map/ppermute | solution.py:74
  55.2 14.7 %all-to-all-start.1 = ((f32[8,56,128]{2,1,0:T(8,128)}), f32[8,56,128]{2,1,0:T(8,128)S(1)}, u32[]{:S(2)}, u32[]{:S(2)}) async-start(f32[8,56,128]{2,1,0:T(8,128)} %get-tuple-element.39), calls=%async_computation.1 | async-start | bytes 458752 | tf_op jit(solution)/shard_map/all_to_all | solution.py:69
  59.2 2.4 %collective-permute-start.10 = (f32[256,128]{1,0:T(8,128)S(1)}, f32[256,128]{1,0:T(8,128)S(1)}, u32[]{:S(2)}, u32[]{:S(2)}) collective-permute-start(f32[256,128]{1,0:T(8,128)S(1)} %get-tuple-element.41.m0), channel_id=1, source_target_pairs={{0,4},{4,0},{1,5},{5,1},{2,6},{6,2},{3,7},{7,3},{8,12},{12,8},{9,1... | collective-permute-start | bytes 393224 | tf_op jit(solution)/shard_map/ppermute | solution.py:74
  59.3 2.3 %collective-permute-start.13 = (f32[256,128]{1,0:T(8,128)S(1)}, f32[256,128]{1,0:T(8,128)S(1)}, u32[]{:S(2)}, u32[]{:S(2)}) collective-permute-start(f32[256,128]{1,0:T(8,128)S(1)} %collective-permute-done.9.m3), channel_id=1, source_target_pairs={{0,4},{4,0},{1,5},{5,1},{2,6},{6,2},{3,7},{7,3},{8,12},{12,8},{9,1... | collective-permute-start | bytes 393224 | tf_op jit(solution)/shard_map/ppermute | solution.py:74
  59.7 0.7 copy-start.3
  60.3 1.3 collective-permute-start.12
  60.4 0.7 copy-start.5
  61.1 1.6 %collective-permute-start.11 = (f32[256,128]{1,0:T(8,128)}, f32[256,128]{1,0:T(8,128)S(1)}, u32[]{:S(2)}, u32[]{:S(2)}) collective-permute-start(f32[256,128]{1,0:T(8,128)} %collective-permute-done.7.m1), channel_id=1, source_target_pairs={{0,4},{4,0},{1,5},{5,1},{2,6},{6,2},{3,7},{7,3},{8,12},{12,8},{9,1... | collective-permute-start | bytes 393224 | tf_op jit(solution)/shard_map/ppermute | solution.py:74
  62.7 0.9 copy-start.2
  63.6 0.9 copy-start.4
  64.5 0.9 copy-start.6
  69.9 31.5 %copy-start.7 = (f32[192,128]{1,0:T(8,128)}, f32[192,128]{1,0:T(8,128)S(1)}, u32[]{:S(2)}) copy-start(f32[192,128]{1,0:T(8,128)S(1)} %get-tuple-element.46.p0) | copy-start | bytes 294916
  74.5 43.2 %all-to-all-start.2 = ((f32[8,72,128]{2,1,0:T(8,128)}), f32[8,72,128]{2,1,0:T(8,128)S(1)}, u32[]{:S(2)}, u32[]{:S(2)}) async-start(f32[8,72,128]{2,1,0:T(8,128)} %get-tuple-element.45), calls=%async_computation.2 | async-start | bytes 589824 | tf_op jit(solution)/shard_map/all_to_all | solution.py:69
  86.4 10.4 %collective-permute-start.14 = (f32[192,128]{1,0:T(8,128)S(1)}, f32[192,128]{1,0:T(8,128)S(1)}, u32[]{:S(2)}, u32[]{:S(2)}) collective-permute-start(f32[192,128]{1,0:T(8,128)S(1)} %get-tuple-element.46.p0), channel_id=1, source_target_pairs={{0,32},{32,64},{64,96},{96,128},{128,160},{160,192},{192,224},{224... | collective-permute-start | bytes 294920 | tf_op jit(solution)/shard_map/ppermute | solution.py:74
  87.8 8.9 %collective-permute-start.15 = (f32[192,128]{1,0:T(8,128)S(1)}, f32[192,128]{1,0:T(8,128)S(1)}, u32[]{:S(2)}, u32[]{:S(2)}) collective-permute-start(f32[192,128]{1,0:T(8,128)S(1)} %get-tuple-element.46.p0), channel_id=1, source_target_pairs={{0,224},{32,0},{64,32},{96,64},{128,96},{160,128},{192,160},{224,1... | collective-permute-start | bytes 294920 | tf_op jit(solution)/shard_map/ppermute | solution.py:74
  96.7 19.6 %copy-start.13 = (f32[192,128]{1,0:T(8,128)}, f32[192,128]{1,0:T(8,128)S(1)}, u32[]{:S(2)}) copy-start(f32[192,128]{1,0:T(8,128)S(1)} %collective-permute-done.14.p1) | copy-start | bytes 294916
  96.7 4.7 %collective-permute-start.16 = (f32[192,128]{1,0:T(8,128)S(1)}, f32[192,128]{1,0:T(8,128)S(1)}, u32[]{:S(2)}, u32[]{:S(2)}) collective-permute-start(f32[192,128]{1,0:T(8,128)S(1)} %collective-permute-done.14.p1), channel_id=1, source_target_pairs={{0,32},{32,64},{64,96},{96,128},{128,160},{160,192},{192,224},{224... | collective-permute-start | bytes 294920 | tf_op jit(solution)/shard_map/ppermute | solution.py:74
  96.7 19.6 %copy-start.14 = (f32[192,128]{1,0:T(8,128)}, f32[192,128]{1,0:T(8,128)S(1)}, u32[]{:S(2)}) copy-start(f32[192,128]{1,0:T(8,128)S(1)} %collective-permute-done.15.p2) | copy-start | bytes 294916
  96.7 8.5 %collective-permute-start.17 = (f32[192,128]{1,0:T(8,128)S(1)}, f32[192,128]{1,0:T(8,128)S(1)}, u32[]{:S(2)}, u32[]{:S(2)}) collective-permute-start(f32[192,128]{1,0:T(8,128)S(1)} %collective-permute-done.15.p2), channel_id=1, source_target_pairs={{0,224},{32,0},{64,32},{96,64},{128,96},{160,128},{192,160},{224,1... | collective-permute-start | bytes 294920 | tf_op jit(solution)/shard_map/ppermute | solution.py:74
  101.4 15.0 %copy-start.15 = (f32[192,128]{1,0:T(8,128)}, f32[192,128]{1,0:T(8,128)S(1)}, u32[]{:S(2)}) copy-start(f32[192,128]{1,0:T(8,128)S(1)} %collective-permute-done.16.p3) | copy-start | bytes 294916
  101.4 6.7 %collective-permute-start.18 = (f32[192,128]{1,0:T(8,128)S(1)}, f32[192,128]{1,0:T(8,128)S(1)}, u32[]{:S(2)}, u32[]{:S(2)}) collective-permute-start(f32[192,128]{1,0:T(8,128)S(1)} %collective-permute-done.16.p3), channel_id=1, source_target_pairs={{0,32},{32,64},{64,96},{96,128},{128,160},{160,192},{192,224},{224... | collective-permute-start | bytes 294920 | tf_op jit(solution)/shard_map/ppermute | solution.py:74
  101.4 6.7 %collective-permute-start.21 = (f32[192,128]{1,0:T(8,128)S(1)}, f32[192,128]{1,0:T(8,128)S(1)}, u32[]{:S(2)}, u32[]{:S(2)}) collective-permute-start(f32[192,128]{1,0:T(8,128)S(1)} %get-tuple-element.46.p0), channel_id=1, source_target_pairs={{0,4},{4,0},{1,5},{5,1},{2,6},{6,2},{3,7},{7,3},{8,12},{12,8},{9,1... | collective-permute-start | bytes 294920 | tf_op jit(solution)/shard_map/ppermute | solution.py:74
  104.8 5.8 %collective-permute-start.23 = (f32[192,128]{1,0:T(8,128)S(1)}, f32[192,128]{1,0:T(8,128)S(1)}, u32[]{:S(2)}, u32[]{:S(2)}) collective-permute-start(f32[192,128]{1,0:T(8,128)S(1)} %collective-permute-done.15.p2), channel_id=1, source_target_pairs={{0,4},{4,0},{1,5},{5,1},{2,6},{6,2},{3,7},{7,3},{8,12},{12,8},{9,1... | collective-permute-start | bytes 294920 | tf_op jit(solution)/shard_map/ppermute | solution.py:74
  104.9 5.9 %collective-permute-start.22 = (f32[192,128]{1,0:T(8,128)S(1)}, f32[192,128]{1,0:T(8,128)S(1)}, u32[]{:S(2)}, u32[]{:S(2)}) collective-permute-start(f32[192,128]{1,0:T(8,128)S(1)} %collective-permute-done.14.p1), channel_id=1, source_target_pairs={{0,4},{4,0},{1,5},{5,1},{2,6},{6,2},{3,7},{7,3},{8,12},{12,8},{9,1... | collective-permute-start | bytes 294920 | tf_op jit(solution)/shard_map/ppermute | solution.py:74
  105.3 11.1 %copy-start.16 = (f32[192,128]{1,0:T(8,128)}, f32[192,128]{1,0:T(8,128)S(1)}, u32[]{:S(2)}) copy-start(f32[192,128]{1,0:T(8,128)S(1)} %collective-permute-done.17.p4) | copy-start | bytes 294916
  105.3 5.8 %collective-permute-start.19 = (f32[192,128]{1,0:T(8,128)S(1)}, f32[192,128]{1,0:T(8,128)S(1)}, u32[]{:S(2)}, u32[]{:S(2)}) collective-permute-start(f32[192,128]{1,0:T(8,128)S(1)} %collective-permute-done.17.p4), channel_id=1, source_target_pairs={{0,224},{32,0},{64,32},{96,64},{128,96},{160,128},{192,160},{224,1... | collective-permute-start | bytes 294920 | tf_op jit(solution)/shard_map/ppermute | solution.py:74
  108.1 8.3 %copy-start.17 = (f32[192,128]{1,0:T(8,128)}, f32[192,128]{1,0:T(8,128)S(1)}, u32[]{:S(2)}) copy-start(f32[192,128]{1,0:T(8,128)S(1)} %collective-permute-done.18.p5) | copy-start | bytes 294916
  108.1 4.7 %collective-permute-start.20 = (f32[192,128]{1,0:T(8,128)S(1)}, f32[192,128]{1,0:T(8,128)S(1)}, u32[]{:S(2)}, u32[]{:S(2)}) collective-permute-start(f32[192,128]{1,0:T(8,128)S(1)} %collective-permute-done.18.p5), channel_id=1, source_target_pairs={{0,32},{32,64},{64,96},{96,128},{128,160},{160,192},{192,224},{224... | collective-permute-start | bytes 294920 | tf_op jit(solution)/shard_map/ppermute | solution.py:74
  108.2 8.3 %copy-start.18 = (f32[192,128]{1,0:T(8,128)}, f32[192,128]{1,0:T(8,128)S(1)}, u32[]{:S(2)}) copy-start(f32[192,128]{1,0:T(8,128)S(1)} %collective-permute-done.21.q0) | copy-start | bytes 294916
  108.2 8.2 %collective-permute-start.25 = (f32[192,128]{1,0:T(8,128)S(1)}, f32[192,128]{1,0:T(8,128)S(1)}, u32[]{:S(2)}, u32[]{:S(2)}) collective-permute-start(f32[192,128]{1,0:T(8,128)S(1)} %collective-permute-done.17.p4), channel_id=1, source_target_pairs={{0,4},{4,0},{1,5},{5,1},{2,6},{6,2},{3,7},{7,3},{8,12},{12,8},{9,1... | collective-permute-start | bytes 294920 | tf_op jit(solution)/shard_map/ppermute | solution.py:74
  110.6 5.8 %copy-start.19 = (f32[192,128]{1,0:T(8,128)}, f32[192,128]{1,0:T(8,128)S(1)}, u32[]{:S(2)}) copy-start(f32[192,128]{1,0:T(8,128)S(1)} %collective-permute-done.23.q2) | copy-start | bytes 294916
  110.6 5.7 %collective-permute-start.24 = (f32[192,128]{1,0:T(8,128)S(1)}, f32[192,128]{1,0:T(8,128)S(1)}, u32[]{:S(2)}, u32[]{:S(2)}) collective-permute-start(f32[192,128]{1,0:T(8,128)S(1)} %collective-permute-done.16.p3), channel_id=1, source_target_pairs={{0,4},{4,0},{1,5},{5,1},{2,6},{6,2},{3,7},{7,3},{8,12},{12,8},{9,1... | collective-permute-start | bytes 294920 | tf_op jit(solution)/shard_map/ppermute | solution.py:74
  110.7 5.7 %copy-start.20 = (f32[192,128]{1,0:T(8,128)}, f32[192,128]{1,0:T(8,128)S(1)}, u32[]{:S(2)}) copy-start(f32[192,128]{1,0:T(8,128)S(1)} %collective-permute-done.22.q1) | copy-start | bytes 294916
  110.7 5.6 %collective-permute-start.26 = (f32[192,128]{1,0:T(8,128)S(1)}, f32[192,128]{1,0:T(8,128)S(1)}, u32[]{:S(2)}, u32[]{:S(2)}) collective-permute-start(f32[192,128]{1,0:T(8,128)S(1)} %collective-permute-done.18.p5), channel_id=1, source_target_pairs={{0,4},{4,0},{1,5},{5,1},{2,6},{6,2},{3,7},{7,3},{8,12},{12,8},{9,1... | collective-permute-start | bytes 294920 | tf_op jit(solution)/shard_map/ppermute | solution.py:74
  111.1 5.3 %copy-start.21 = (f32[192,128]{1,0:T(8,128)}, f32[192,128]{1,0:T(8,128)S(1)}, u32[]{:S(2)}) copy-start(f32[192,128]{1,0:T(8,128)S(1)} %collective-permute-done.19.p6) | copy-start | bytes 294916
  111.1 5.2 %collective-permute-start.27 = (f32[192,128]{1,0:T(8,128)S(1)}, f32[192,128]{1,0:T(8,128)S(1)}, u32[]{:S(2)}, u32[]{:S(2)}) collective-permute-start(f32[192,128]{1,0:T(8,128)S(1)} %collective-permute-done.19.p6), channel_id=1, source_target_pairs={{0,4},{4,0},{1,5},{5,1},{2,6},{6,2},{3,7},{7,3},{8,12},{12,8},{9,1... | collective-permute-start | bytes 294920 | tf_op jit(solution)/shard_map/ppermute | solution.py:74
  112.8 3.6 %copy-start.22 = (f32[192,128]{1,0:T(8,128)}, f32[192,128]{1,0:T(8,128)S(1)}, u32[]{:S(2)}) copy-start(f32[192,128]{1,0:T(8,128)S(1)} %collective-permute-done.20.p7) | copy-start | bytes 294916
  112.8 4.9 %collective-permute-start.28 = (f32[192,128]{1,0:T(8,128)S(1)}, f32[192,128]{1,0:T(8,128)}, u32[]{:S(2)}, u32[]{:S(2)}) collective-permute-start(f32[192,128]{1,0:T(8,128)S(1)} %collective-permute-done.20.p7), channel_id=1, source_target_pairs={{0,4},{4,0},{1,5},{5,1},{2,6},{6,2},{3,7},{7,3},{8,12},{12,8},{9,1... | collective-permute-start | bytes 294920 | tf_op jit(solution)/shard_map/ppermute | solution.py:74
  116.3 1.4 copy-start.23
  116.3 0.7 copy-start.24
  116.3 0.7 copy-start.26
  117.0 0.6 copy-start.25
  117.7 13.9 %copy-start = (f32[384,128]{1,0:T(8,128)S(1)}, f32[384,128]{1,0:T(8,128)}, u32[]{:S(2)}) copy-start(f32[384,128]{1,0:T(8,128)} %get-tuple-element.51.defect_ref) | copy-start | bytes 589828
  117.7 13.9 %copy-start.9 = (f32[256]{0:T(256)S(1)}, f32[256]{0:T(256)}, u32[]{:S(2)}) copy-start(f32[256]{0:T(256)} %param.15) | copy-start | bytes 3076
  131.6 9.5 %copy-start.10 = (f32[96,256]{1,0:T(8,128)S(1)}, f32[96,256]{1,0:T(8,128)}, u32[]{:S(2)}) copy-start(f32[96,256]{1,0:T(8,128)} %direction_ref) | copy-start | bytes 294916
  131.6 9.6 %copy-start.11 = (f32[96,256]{1,0:T(8,128)S(1)}, f32[96,256]{1,0:T(8,128)}, u32[]{:S(2)}) copy-start(f32[96,256]{1,0:T(8,128)} %residual_ref) | copy-start | bytes 294916
  131.6 9.6 %copy-start.27 = (f32[96,256]{1,0:T(8,128)S(1)}, f32[96,256]{1,0:T(8,128)}, u32[]{:S(2)}) copy-start(f32[96,256]{1,0:T(8,128)} %param.12) | copy-start | bytes 294916

commit v4 on v3

--- a/solution.py
+++ b/solution.py
@@ -96,17 +96,23 @@
         out_ref[j : j + 1, :] = source_ref[pl.ds(index_ref[0, j], 1), :]
 
 
-def pack(direction_ref, residual_ref, inverse_ref, lower_ref, upper_ref, out_ref):
+def pack(direction_ref, residual_ref, inverse_ref, lower_ref, upper_ref, out_ref, coarse_ref):
+    coarse_ref[:, 0:384] = inverse_ref[...]
+    coarse_ref[:, 384:512] = lower_ref[...]
+    coarse_ref[:, 512:640] = upper_ref[...]
     d = direction_ref[...]
     r = residual_ref[...]
     for q in range(4):
-        out_ref[q, :, 0:128] = jnp.concatenate([d[:, 64 * q : 64 * q + 64], r[:, 64 * q : 64 * q + 64]], axis=1)
-        out_ref[q, :, 128:512] = inverse_ref[...]
-        out_ref[q, :, 512:640] = lower_ref[...]
-        out_ref[q, :, 640:768] = upper_ref[...]
-
-
-def make_maps(index_ref, got_ref, factor_ref, maps_ref, faces_ref, all_scr, face_scr):
+        out_ref[q] = jnp.concatenate([d[:, 64 * q : 64 * q + 64], r[:, 64 * q : 64 * q + 64]], axis=1)
+
+
+def make_maps(
+    index_ref, grp_ref, fields_ref, c0, c1, c2, c3, got_ref, factor_ref, maps_ref, faces_ref, all_scr, face_scr
+):
+    for step, piece in enumerate((c0, c1, c2, c3)):
+        rows = pl.ds(pl.multiple_of(96 * ((grp_ref[0] + 4 - step) % 4), 8), 96)
+        got_ref[rows, 128:768] = piece[...]
+    got_ref[:, 0:128] = fields_ref[...]
     factor = mm(got_ref[:, 128:512], got_ref[:, 512:640])
     factor_ref[...] = factor
     all_scr[:, 0:128] = got_ref[:, 0:128]
@@ -355,24 +361,28 @@
         (grp, at_x, at_c, at_z, place, direction, residual)
     )
     operator = jnp.concatenate([diag_blocks, lower_coupling, upper_coupling, jacobi_inverse], axis=1)
-    got = to_each(
-        call(
-            pack,
-            shaped(4, 96, 768),
-            0,
-            *(far(a) for a in (direction, residual, slab_inverse, lower_factor, upper_factor)),
-        ),
-        "grp",
-    ).reshape(384, 768)
+    sent, coarse = call(
+        pack,
+        (shaped(4, 96, 128), shaped(96, 640)),
+        0,
+        *(far(a) for a in (direction, residual, slab_inverse, lower_factor, upper_factor)),
+    )
+    fields = to_each(sent, "grp").reshape(384, 128)
+    coarse_up = ring(coarse, "grp", 1)
+    coarse_down = ring(coarse, "grp", 3)
+    coarse = [coarse, coarse_up, ring(coarse_up, "grp", 1), coarse_down]
     bulk_up = ring(operator, "grp", 1)
     bulk_down = ring(operator, "grp", 3)
     bulk = [operator, bulk_up, ring(bulk_down, "grp", 3), bulk_down]
-    factor, maps, faces = call(
+    got, factor, maps, faces = call(
         make_maps,
-        (shaped(384, 128), shaped(256, 128), shaped(64, 128)),
-        1,
+        (shaped(384, 768), shaped(384, 128), shaped(256, 128), shaped(64, 128)),
+        2,
         interface,
-        got,
+        grp,
+        fields,
+        far(coarse[0]),
+        *coarse[1:],
         scratch=[pltpu.VMEM((384, 384), jnp.float32), pltpu.VMEM((128, 384), jnp.float32)],
     )
     along = [maps] + [ring(maps, "slab_1", step) for step in (1, 2, 3)]

time: 143 us -> 144 us (level)
  waiting for transfers between devices: 30.4 us -> 17 us
  blocking collectives: 18 us -> 30.6 us
  local copies, waits for them, and re-layouts: 5.54 us -> 10.4 us
  Pallas kernels: 20.9 us -> 19.4 us
    ppermute x25 -> x28, waiting for transfers between devices: 29.4 us -> 16 us  [ring(): lax.ppermute(x, axis, [(i, (i + step) % count) for i in range(count)])]
    all_to_all x2 -> x3, blocking collectives: 18 us -> 30.6 us  [to_each(): return lax.all_to_all(pieces, axes, split_axis=0, concat_axis=0, tiled=True)]
    all_to_all x3 -> x2, starting transfers between devices: 21 us -> 15.9 us  [to_each(): return lax.all_to_all(pieces, axes, split_axis=0, concat_axis=0, tiled=True)]
    unnamed x65 -> x63, local copies, waits for them, and re-layouts: 5.35 us -> 9.4 us
    ppermute x25 -> x28, starting transfers between devices: 30.1 us -> 34 us  [ring(): lax.ppermute(x, axis, [(i, (i + step) % count) for i in range(count)])]
    pallas_call x8, Pallas kernels: 20.9 us -> 19.4 us  [call(): pl.pallas_call(body, out_shape=outs, in_specs=[SMEM] * smem + [VMEM] * (l...]
  transfers between devices with their start and end apart: 32 -> 34, of which waited for: 7 -> 6; matrix products, arithmetic and copies ran while one was open for 0% -> 0% of each run, Pallas kernels for 6% -> 6%
where the time goes in v4:
time: 144 us; the launch traced here: 143 us
  starting transfers between devices  63.3 us (44%)
  blocking collectives  30.6 us (21%)
  Pallas kernels  19.4 us (13%)
  waiting for transfers between devices  17 us (12%)
  local copies, waits for them, and re-layouts  10.4 us (7%)
  other arithmetic  1.46 us (1%)
    ppermute x28, starting transfers between devices, ring(): lax.ppermute(x, axis, [(i, (i + step) % count) for i in range(count)])  34 us
    all_to_all x3, blocking collectives, to_each(): return lax.all_to_all(pieces, axes, split_axis=0, concat_axis=0, tiled=True)  30.6 us
    pallas_call x8, Pallas kernels, call(): pl.pallas_call(body, out_shape=outs, in_specs=[SMEM] * smem + [VMEM] * (l...  19.4 us
    ppermute x28, waiting for transfers between devices, ring(): lax.ppermute(x, axis, [(i, (i + step) % count) for i in range(count)])  16 us
    all_to_all x2, starting transfers between devices, to_each(): return lax.all_to_all(pieces, axes, split_axis=0, concat_axis=0, tiled=True)  15.9 us
    unnamed x63, local copies, waits for them, and re-layouts  9.4 us
    ppermute x2, starting transfers between devices, beside(): below = lax.ppermute(faces, SLAB, [(i, i + 1) for i in range(count - 1)])  7.24 us
    ppermute x2, starting transfers between devices, beside(): above = lax.ppermute(faces, SLAB, [(i + 1, i) for i in range(count - 1)])  6.17 us
  transfers between devices with their start and end apart: 34, of which 6 were waited for; matrix products, arithmetic and copies ran while one was open for 0% of the time, Pallas kernels for 6%

profile of v4, /device:TPU:1, one launch (start us, length us, event | category | flops | bytes accessed | tf_op | source)
XLA Modules:
  0.0 143.1 jit_solution(4527869808932754345)
XLA Ops:
  0.6 0.9 constant_dynamic-update-slice_fusion.3
  1.6 0.8 constant_dynamic-update-slice_fusion.2
  2.4 0.8 constant_dynamic-update-slice_fusion.1
  3.2 0.8 constant_dynamic-update-slice_fusion.p0
  4.0 3.6 %collective-permute-start.4 = (f32[96,736]{1,0:T(8,128)S(1)}, f32[96,736]{1,0:T(8,128)S(1)}, u32[]{:S(2)}, u32[]{:S(2)}) collective-permute-start(f32[96,736]{1,0:T(8,128)S(1)} %constant_dynamic-update-slice_fusion.p0), channel_id=1, source_target_pairs={{0,3},{1,0},{2,1},{3,2},{4,7},{5,4},{6,5},{7,6},{8,11},{9,8},{10,9... | collective-permute-start | bytes 847880 | tf_op jit(solution)/shard_map/ppermute | solution.py:74
  7.5 1.2 shard_map.147
  8.7 0.1 collective-permute-start
  8.8 0.1 collective-permute-start.3
  8.9 4.3 %collective-permute-done.4.p3 = f32[96,736]{1,0:T(8,128)S(1)} collective-permute-done((f32[96,736]{1,0:T(8,128)S(1)}, f32[96,736]{1,0:T(8,128)S(1)}, u32[]{:S(2)}, u32[]{:S(2)}) %collective-permute-start.4) | collective-permute-done | bytes 282656 | tf_op jit(solution)/shard_map/ppermute | solution.py:74
  13.2 3.4 %collective-permute-start.5 = (f32[96,736]{1,0:T(8,128)S(1)}, f32[96,736]{1,0:T(8,128)S(1)}, u32[]{:S(2)}, u32[]{:S(2)}) collective-permute-start(f32[96,736]{1,0:T(8,128)S(1)} %collective-permute-done.4.p3), channel_id=1, source_target_pairs={{0,3},{1,0},{2,1},{3,2},{4,7},{5,4},{6,5},{7,6},{8,11},{9,8},{10,9... | collective-permute-start | bytes 847880 | tf_op jit(solution)/shard_map/ppermute | solution.py:74
  16.7 1.4 %collective-permute-start.1 = (f32[96,640]{1,0:T(8,128)S(1)}, f32[96,640]{1,0:T(8,128)S(1)}, u32[]{:S(2)}, u32[]{:S(2)}) collective-permute-start(f32[96,640]{1,0:T(8,128)S(1)} %collective-permute-done.c1), channel_id=1, source_target_pairs={{0,1},{1,2},{2,3},{3,0},{4,5},{5,6},{6,7},{7,4},{8,9},{9,10},{10,1... | collective-permute-start | bytes 737288 | tf_op jit(solution)/shard_map/ppermute | solution.py:74
  18.1 11.6 %all_to_all.25 = f32[4,96,128]{2,1,0:T(8,128)S(1)} all-to-all(f32[4,96,128]{2,1,0:T(8,128)S(1)} %get-tuple-element.34), channel_id=1, replica_groups=mesh['slab_0'=8,'slab_1'=4,'slab_2'=2,'grp'=4] {'grp'}, dimensions={0} | all-to-all | bytes 393216 | tf_op jit(solution)/shard_map/all_to_all | solution.py:69
  29.8 1.6 %shard_map.148 = (f32[384,768]{1,0:T(8,128)S(1)}, f32[384,128]{1,0:T(8,128)S(1)}, f32[256,128]{1,0:T(8,128)S(1)}, f32[64,128]{1,0:T(8,128)S(1)}) custom-call(s32[1,128]{1,0:T(1,128)S(1)} %copy-done.11, s32[1]{0:T(128)} %bitcast.grp_ref, f32[384,128]{1,0:T(8,128)S(1)} %bitcast.39, f32[96,640]{1,0:T(8,128)} %copy-done, f32[96,640]{1,0:T(8,128)S(1)} %collective-permute-done.c1, ...), custom_call_target="tpu_custom_call" | custom-call | tf_op jit(solution)/shard_map/pallas_call | solution.py:54
  31.4 4.2 %collective-permute-start.7 = (f32[64,128]{1,0:T(8,128)S(1)}, f32[64,128]{1,0:T(8,128)S(1)}, u32[]{:S(2)}, u32[]{:S(2)}) collective-permute-start(f32[64,128]{1,0:T(8,128)S(1)} %get-tuple-element.41), channel_id=1, source_target_pairs={{4,0},{8,4},{12,8},{16,12},{20,16},{24,20},{28,24},{32,28},{36,32}... | collective-permute-start | bytes 98312 | tf_op jit(solution)/shard_map/ppermute | solution.py:80
  35.6 3.0 %collective-permute-start.6 = (f32[64,128]{1,0:T(8,128)S(1)}, f32[64,128]{1,0:T(8,128)S(1)}, u32[]{:S(2)}, u32[]{:S(2)}) collective-permute-start(f32[64,128]{1,0:T(8,128)S(1)} %get-tuple-element.41), channel_id=1, source_target_pairs={{0,4},{4,8},{8,12},{12,16},{16,20},{20,24},{24,28},{28,32},{32,36}... | collective-permute-start | bytes 98312 | tf_op jit(solution)/shard_map/ppermute | solution.py:79
  38.7 1.0 collective-permute-done.6.below_ref
  39.7 1.4 shard_map.149
  41.1 1.9 %collective-permute-start.9 = (f32[128,128]{1,0:T(8,128)S(1)}, f32[128,128]{1,0:T(8,128)S(1)}, u32[]{:S(2)}, u32[]{:S(2)}) collective-permute-start(f32[128,128]{1,0:T(8,128)S(1)} %get-tuple-element.44), channel_id=1, source_target_pairs={{4,0},{8,4},{12,8},{16,12},{20,16},{24,20},{28,24},{32,28},{36,32}... | collective-permute-start | bytes 196616 | tf_op jit(solution)/shard_map/ppermute | solution.py:80
  43.0 4.2 %collective-permute-start.8 = (f32[128,128]{1,0:T(8,128)S(1)}, f32[128,128]{1,0:T(8,128)S(1)}, u32[]{:S(2)}, u32[]{:S(2)}) collective-permute-start(f32[128,128]{1,0:T(8,128)S(1)} %get-tuple-element.44), channel_id=1, source_target_pairs={{0,4},{4,8},{8,12},{12,16},{16,20},{20,24},{24,28},{28,32},{32,36}... | collective-permute-start | bytes 196616 | tf_op jit(solution)/shard_map/ppermute | solution.py:79
  47.3 5.1 %collective-permute-start.12 = (f32[256,128]{1,0:T(8,128)S(1)}, f32[256,128]{1,0:T(8,128)S(1)}, u32[]{:S(2)}, u32[]{:S(2)}) collective-permute-start(f32[256,128]{1,0:T(8,128)S(1)} %get-tuple-element.47.m0), channel_id=1, source_target_pairs={{0,24},{8,0},{16,8},{24,16},{1,25},{9,1},{17,9},{25,17},{2,26},{10... | collective-permute-start | bytes 393224 | tf_op jit(solution)/shard_map/ppermute | solution.py:74
  52.3 0.7 collective-permute-start.10
  53.0 2.5 %shard_map.150 = (f32[384,128]{1,0:T(8,128)}, f32[8,56,128]{2,1,0:T(8,128)}) custom-call(s32[1,128]{1,0:T(1,128)S(1)} %copy-done.11, s32[1]{0:T(128)} %bitcast.grp_ref, f32[384,768]{1,0:T(8,128)S(1)} %get-tuple-element.36.got_ref, f32[96,736]{1,0:T(8,128)S(1)} %constant_dynamic-update-slice_fusion.p0, f32[96,736]{1,0:T(8,128)S(1)} %collective-permute-done.3.p1, ...), custom_call_target="tpu_custom_call" | custom-call | tf_op jit(solution)/shard_map/pallas_call | solution.py:54
  55.5 4.0 %all-to-all-start.1 = ((f32[8,56,128]{2,1,0:T(8,128)}), f32[8,56,128]{2,1,0:T(8,128)S(1)}, u32[]{:S(2)}, u32[]{:S(2)}) async-start(f32[8,56,128]{2,1,0:T(8,128)} %get-tuple-element.45), calls=%async_computation.1 | async-start | bytes 458752 | tf_op jit(solution)/shard_map/all_to_all | solution.py:69
  59.5 0.1 collective-permute-start.13
  59.6 0.4 collective-permute-start.16
  60.0 0.7 copy-done.4
  60.6 0.1 collective-permute-start.15
  60.7 0.6 copy-done.6
  61.4 0.4 collective-permute-start.14
  61.8 0.6 copy-done.8
  62.4 0.3 collective-permute-done.14.n1
  62.8 0.9 copy-done.3
  63.7 0.9 copy-done.5
  64.6 0.9 copy-done.7
  65.5 0.9 copy-done.9
  66.4 3.5 %shard_map.151 = (bf16[2,8,256,128]{3,2,1,0:T(8,128)(2,1)}, bf16[2,8,128,128]{3,2,1,0:T(8,128)(2,1)S(1)}, bf16[2,8,256,128]{3,2,1,0:T(8,128)(2,1)S(1)}, f32[192,128]{1,0:T(8,128)S(1)}) custom-call(s32[1]{0:T(128)} %bitcast.1.x_ref, s32[1]{0:T(128)} %bitcast.2.c_ref, f32[256,128]{1,0:T(8,128)S(1)} %copy-done.3, f32[256,128]{1,0:T(8,128)S(1)} %copy-done.9, ...), custom_call_target="tpu_custom_call" | custom-call | tf_op jit(solution)/shard_map/pallas_call | solution.py:54
  69.9 4.6 %shard_map.152 = (f32[9,16,128]{2,1,0:T(8,128)}, f32[8,16,128]{2,1,0:T(8,128)}, f32[8,72,128]{2,1,0:T(8,128)}) custom-call(s32[1]{0:T(128)} %bitcast.4.place_ref, f32[8,56,128]{2,1,0:T(8,128)S(1)} %all-to-all-done.1.got_ref, bf16[2,8,256,128]{3,2,1,0:T(8,128)(2,1)} %get-tuple-element.48.maps_ref, ...), custom_call_target="tpu_custom_call" | custom-call | tf_op jit(solution)/shard_map/pallas_call | solution.py:54
  74.5 11.9 %all-to-all-start.2 = ((f32[8,72,128]{2,1,0:T(8,128)}), f32[8,72,128]{2,1,0:T(8,128)S(1)}, u32[]{:S(2)}, u32[]{:S(2)}) async-start(f32[8,72,128]{2,1,0:T(8,128)} %get-tuple-element.51), calls=%async_computation.2 | async-start | bytes 589824 | tf_op jit(solution)/shard_map/all_to_all | solution.py:69
  86.4 1.5 %collective-permute-start.17 = (f32[192,128]{1,0:T(8,128)S(1)}, f32[192,128]{1,0:T(8,128)S(1)}, u32[]{:S(2)}, u32[]{:S(2)}) collective-permute-start(f32[192,128]{1,0:T(8,128)S(1)} %get-tuple-element.52.p0), channel_id=1, source_target_pairs={{0,32},{32,64},{64,96},{96,128},{128,160},{160,192},{192,224},{224... | collective-permute-start | bytes 294920 | tf_op jit(solution)/shard_map/ppermute | solution.py:74
  87.8 1.2 collective-permute-start.18
  89.1 7.7 %collective-permute-done.17.p1 = f32[192,128]{1,0:T(8,128)S(1)} collective-permute-done((f32[192,128]{1,0:T(8,128)S(1)}, f32[192,128]{1,0:T(8,128)S(1)}, u32[]{:S(2)}, u32[]{:S(2)}) %collective-permute-start.17) | collective-permute-done | bytes 98336 | tf_op jit(solution)/shard_map/ppermute | solution.py:74
  96.8 2.7 %collective-permute-start.20 = (f32[192,128]{1,0:T(8,128)S(1)}, f32[192,128]{1,0:T(8,128)S(1)}, u32[]{:S(2)}, u32[]{:S(2)}) collective-permute-start(f32[192,128]{1,0:T(8,128)S(1)} %collective-permute-done.18.p2), channel_id=1, source_target_pairs={{0,224},{32,0},{64,32},{96,64},{128,96},{160,128},{192,160},{224,1... | collective-permute-start | bytes 294920 | tf_op jit(solution)/shard_map/ppermute | solution.py:74
  99.4 2.0 %collective-permute-done.19.p3 = f32[192,128]{1,0:T(8,128)S(1)} collective-permute-done((f32[192,128]{1,0:T(8,128)S(1)}, f32[192,128]{1,0:T(8,128)S(1)}, u32[]{:S(2)}, u32[]{:S(2)}) %collective-permute-start.19) | collective-permute-done | bytes 98336 | tf_op jit(solution)/shard_map/ppermute | solution.py:74
  101.4 3.3 %collective-permute-start.24 = (f32[192,128]{1,0:T(8,128)S(1)}, f32[192,128]{1,0:T(8,128)S(1)}, u32[]{:S(2)}, u32[]{:S(2)}) collective-permute-start(f32[192,128]{1,0:T(8,128)S(1)} %get-tuple-element.52.p0), channel_id=1, source_target_pairs={{0,4},{4,0},{1,5},{5,1},{2,6},{6,2},{3,7},{7,3},{8,12},{12,8},{9,1... | collective-permute-start | bytes 294920 | tf_op jit(solution)/shard_map/ppermute | solution.py:74
  104.8 0.1 collective-permute-start.26
  104.9 0.4 collective-permute-start.25
  105.3 2.9 %collective-permute-start.22 = (f32[192,128]{1,0:T(8,128)S(1)}, f32[192,128]{1,0:T(8,128)S(1)}, u32[]{:S(2)}, u32[]{:S(2)}) collective-permute-start(f32[192,128]{1,0:T(8,128)S(1)} %collective-permute-done.20.p4), channel_id=1, source_target_pairs={{0,224},{32,0},{64,32},{96,64},{128,96},{160,128},{192,160},{224,1... | collective-permute-start | bytes 294920 | tf_op jit(solution)/shard_map/ppermute | solution.py:74
  108.2 2.4 %collective-permute-start.28 = (f32[192,128]{1,0:T(8,128)S(1)}, f32[192,128]{1,0:T(8,128)S(1)}, u32[]{:S(2)}, u32[]{:S(2)}) collective-permute-start(f32[192,128]{1,0:T(8,128)S(1)} %collective-permute-done.20.p4), channel_id=1, source_target_pairs={{0,4},{4,0},{1,5},{5,1},{2,6},{6,2},{3,7},{7,3},{8,12},{12,8},{9,1... | collective-permute-start | bytes 294920 | tf_op jit(solution)/shard_map/ppermute | solution.py:74
  110.6 0.1 collective-permute-start.27
  110.7 0.4 collective-permute-start.29
  111.1 0.1 collective-permute-start.30
  111.3 1.6 %collective-permute-done.23.p7 = f32[192,128]{1,0:T(8,128)S(1)} collective-permute-done((f32[192,128]{1,0:T(8,128)S(1)}, f32[192,128]{1,0:T(8,128)S(1)}, u32[]{:S(2)}, u32[]{:S(2)}) %collective-permute-start.23) | collective-permute-done | bytes 98336 | tf_op jit(solution)/shard_map/ppermute | solution.py:74
  112.8 3.5 %collective-permute-start.31 = (f32[192,128]{1,0:T(8,128)S(1)}, f32[192,128]{1,0:T(8,128)}, u32[]{:S(2)}, u32[]{:S(2)}) collective-permute-start(f32[192,128]{1,0:T(8,128)S(1)} %collective-permute-done.23.p7), channel_id=1, source_target_pairs={{0,4},{4,0},{1,5},{5,1},{2,6},{6,2},{3,7},{7,3},{8,12},{12,8},{9,1... | collective-permute-start | bytes 294920 | tf_op jit(solution)/shard_map/ppermute | solution.py:74
  116.5 0.5 copy-done.26
  117.0 0.0 copy-done.28
  117.1 0.6 copy-done.27
  117.8 3.8 %shard_map.153 = (f32[8,40,128]{2,1,0:T(8,128)S(1)}, f32[8,128]{1,0:T(8,128)S(1)}) custom-call(s32[1]{0:T(128)} %bitcast.2.c_ref, s32[1]{0:T(128)} %bitcast.3.z_ref, s32[1]{0:T(128)} %bitcast.4.place_ref, f32[8,72,128]{2,1,0:T(8,128)S(1)} %all-to-all-done.2.sums_ref, f32[192,128]{1,0:T(8,128)} %copy-done.10, f32[192,128]{1,0:T(8,128)} %copy-done.15, ...), custom_call_target="tpu_custom_call" | custom-call | tf_op jit(solution)/shard_map/pallas_call | solution.py:54
  121.5 10.1 %all_to_all.26.back_ref = f32[8,40,128]{2,1,0:T(8,128)S(1)} all-to-all(f32[8,40,128]{2,1,0:T(8,128)S(1)} %get-tuple-element.55), channel_id=1, replica_groups=mesh['slab_0'=8,'slab_1'=4,'slab_2'=2,'grp'=4] {'slab_1','slab_2'}, dimensions={0} | all-to-all | bytes 327680 | tf_op jit(solution)/shard_map/all_to_all | solution.py:69
  131.7 0.9 shard_map.154
  132.6 8.9 %all_to_all.27 = f32[4,104,128]{2,1,0:T(8,128)S(1)} all-to-all(f32[4,104,128]{2,1,0:T(8,128)S(1)} %shard_map.154), channel_id=1, replica_groups=mesh['slab_0'=8,'slab_1'=4,'slab_2'=2,'grp'=4] {'grp'}, dimensions={0} | all-to-all | bytes 425984 | tf_op jit(solution)/shard_map/all_to_all | solution.py:69
  141.4 0.1 slice_bitcast_fusion.11
  141.5 0.6 fusion.1
  142.2 0.1 slice_bitcast_fusion.3
  142.3 0.8 maximum_add_fusion
  (83 shorter events, 0.2 us)
Async XLA Ops:
  0.6 29.1 %copy-start.11 = (s32[1,128]{1,0:T(1,128)S(1)}, s32[1,128]{1,0:T(1,128)}, u32[]{:S(2)}) copy-start(s32[1,128]{1,0:T(1,128)} %index_ref.5) | copy-start | bytes 1540
  4.0 9.2 %collective-permute-start.4 = (f32[96,736]{1,0:T(8,128)S(1)}, f32[96,736]{1,0:T(8,128)S(1)}, u32[]{:S(2)}, u32[]{:S(2)}) collective-permute-start(f32[96,736]{1,0:T(8,128)S(1)} %constant_dynamic-update-slice_fusion.p0), channel_id=1, source_target_pairs={{0,3},{1,0},{2,1},{3,2},{4,7},{5,4},{6,5},{7,6},{8,11},{9,8},{10,9... | collective-permute-start | bytes 847880 | tf_op jit(solution)/shard_map/ppermute | solution.py:74
  8.7 21.0 %copy-start = (f32[96,640]{1,0:T(8,128)}, f32[96,640]{1,0:T(8,128)S(1)}, u32[]{:S(2)}) copy-start(f32[96,640]{1,0:T(8,128)S(1)} %get-tuple-element.35.c0) | copy-start | bytes 737284
  8.7 7.9 %collective-permute-start = (f32[96,640]{1,0:T(8,128)S(1)}, f32[96,640]{1,0:T(8,128)S(1)}, u32[]{:S(2)}, u32[]{:S(2)}) collective-permute-start(f32[96,640]{1,0:T(8,128)S(1)} %get-tuple-element.35.c0), channel_id=1, source_target_pairs={{0,1},{1,2},{2,3},{3,0},{4,5},{5,6},{6,7},{7,4},{8,9},{9,10},{10,1... | collective-permute-start | bytes 737288 | tf_op jit(solution)/shard_map/ppermute | solution.py:74
  8.8 29.9 %collective-permute-start.3 = (f32[96,736]{1,0:T(8,128)S(1)}, f32[96,736]{1,0:T(8,128)S(1)}, u32[]{:S(2)}, u32[]{:S(2)}) collective-permute-start(f32[96,736]{1,0:T(8,128)S(1)} %constant_dynamic-update-slice_fusion.p0), channel_id=1, source_target_pairs={{0,1},{1,2},{2,3},{3,0},{4,5},{5,6},{6,7},{7,4},{8,9},{9,10},{10,1... | collective-permute-start | bytes 847880 | tf_op jit(solution)/shard_map/ppermute | solution.py:74
  13.2 26.4 %collective-permute-start.5 = (f32[96,736]{1,0:T(8,128)S(1)}, f32[96,736]{1,0:T(8,128)S(1)}, u32[]{:S(2)}, u32[]{:S(2)}) collective-permute-start(f32[96,736]{1,0:T(8,128)S(1)} %collective-permute-done.4.p3), channel_id=1, source_target_pairs={{0,3},{1,0},{2,1},{3,2},{4,7},{5,4},{6,5},{7,6},{8,11},{9,8},{10,9... | collective-permute-start | bytes 847880 | tf_op jit(solution)/shard_map/ppermute | solution.py:74
  16.6 13.1 %collective-permute-start.2 = (f32[96,640]{1,0:T(8,128)S(1)}, f32[96,640]{1,0:T(8,128)S(1)}, u32[]{:S(2)}, u32[]{:S(2)}) collective-permute-start(f32[96,640]{1,0:T(8,128)S(1)} %get-tuple-element.35.c0), channel_id=1, source_target_pairs={{0,3},{1,0},{2,1},{3,2},{4,7},{5,4},{6,5},{7,6},{8,11},{9,8},{10,9... | collective-permute-start | bytes 737288 | tf_op jit(solution)/shard_map/ppermute | solution.py:74
  16.7 13.1 %collective-permute-start.1 = (f32[96,640]{1,0:T(8,128)S(1)}, f32[96,640]{1,0:T(8,128)S(1)}, u32[]{:S(2)}, u32[]{:S(2)}) collective-permute-start(f32[96,640]{1,0:T(8,128)S(1)} %collective-permute-done.c1), channel_id=1, source_target_pairs={{0,1},{1,2},{2,3},{3,0},{4,5},{5,6},{6,7},{7,4},{8,9},{9,10},{10,1... | collective-permute-start | bytes 737288 | tf_op jit(solution)/shard_map/ppermute | solution.py:74
  31.4 28.1 %copy-start.2 = (f32[256,128]{1,0:T(8,128)}, f32[256,128]{1,0:T(8,128)S(1)}, u32[]{:S(2)}) copy-start(f32[256,128]{1,0:T(8,128)S(1)} %get-tuple-element.47.m0) | copy-start | bytes 393220
  31.4 7.3 %collective-permute-start.7 = (f32[64,128]{1,0:T(8,128)S(1)}, f32[64,128]{1,0:T(8,128)S(1)}, u32[]{:S(2)}, u32[]{:S(2)}) collective-permute-start(f32[64,128]{1,0:T(8,128)S(1)} %get-tuple-element.41), channel_id=1, source_target_pairs={{4,0},{8,4},{12,8},{16,12},{20,16},{24,20},{28,24},{32,28},{36,32}... | collective-permute-start | bytes 98312 | tf_op jit(solution)/shard_map/ppermute | solution.py:80
  35.6 4.0 %collective-permute-start.6 = (f32[64,128]{1,0:T(8,128)S(1)}, f32[64,128]{1,0:T(8,128)S(1)}, u32[]{:S(2)}, u32[]{:S(2)}) collective-permute-start(f32[64,128]{1,0:T(8,128)S(1)} %get-tuple-element.41), channel_id=1, source_target_pairs={{0,4},{4,8},{8,12},{12,16},{16,20},{20,24},{24,28},{28,32},{32,36}... | collective-permute-start | bytes 98312 | tf_op jit(solution)/shard_map/ppermute | solution.py:79
  41.1 11.9 %collective-permute-start.9 = (f32[128,128]{1,0:T(8,128)S(1)}, f32[128,128]{1,0:T(8,128)S(1)}, u32[]{:S(2)}, u32[]{:S(2)}) collective-permute-start(f32[128,128]{1,0:T(8,128)S(1)} %get-tuple-element.44), channel_id=1, source_target_pairs={{4,0},{8,4},{12,8},{16,12},{20,16},{24,20},{28,24},{32,28},{36,32}... | collective-permute-start | bytes 196616 | tf_op jit(solution)/shard_map/ppermute | solution.py:80
  43.0 10.0 %collective-permute-start.8 = (f32[128,128]{1,0:T(8,128)S(1)}, f32[128,128]{1,0:T(8,128)S(1)}, u32[]{:S(2)}, u32[]{:S(2)}) collective-permute-start(f32[128,128]{1,0:T(8,128)S(1)} %get-tuple-element.44), channel_id=1, source_target_pairs={{0,4},{4,8},{8,12},{12,16},{16,20},{20,24},{24,28},{28,32},{32,36}... | collective-permute-start | bytes 196616 | tf_op jit(solution)/shard_map/ppermute | solution.py:79
  47.3 12.3 %collective-permute-start.12 = (f32[256,128]{1,0:T(8,128)S(1)}, f32[256,128]{1,0:T(8,128)S(1)}, u32[]{:S(2)}, u32[]{:S(2)}) collective-permute-start(f32[256,128]{1,0:T(8,128)S(1)} %get-tuple-element.47.m0), channel_id=1, source_target_pairs={{0,24},{8,0},{16,8},{24,16},{1,25},{9,1},{17,9},{25,17},{2,26},{10... | collective-permute-start | bytes 393224 | tf_op jit(solution)/shard_map/ppermute | solution.py:74
  52.3 8.3 %collective-permute-start.11 = (f32[256,128]{1,0:T(8,128)S(1)}, f32[256,128]{1,0:T(8,128)S(1)}, u32[]{:S(2)}, u32[]{:S(2)}) collective-permute-start(f32[256,128]{1,0:T(8,128)S(1)} %get-tuple-element.47.m0), channel_id=1, source_target_pairs={{0,16},{8,24},{16,0},{24,8},{1,17},{9,25},{17,1},{25,9},{2,18},{10... | collective-permute-start | bytes 393224 | tf_op jit(solution)/shard_map/ppermute | solution.py:74
  52.3 9.0 %collective-permute-start.10 = (f32[256,128]{1,0:T(8,128)S(1)}, f32[256,128]{1,0:T(8,128)S(1)}, u32[]{:S(2)}, u32[]{:S(2)}) collective-permute-start(f32[256,128]{1,0:T(8,128)S(1)} %get-tuple-element.47.m0), channel_id=1, source_target_pairs={{0,8},{8,16},{16,24},{24,0},{1,9},{9,17},{17,25},{25,1},{2,10},{10... | collective-permute-start | bytes 393224 | tf_op jit(solution)/shard_map/ppermute | solution.py:74
  55.5 14.4 %all-to-all-start.1 = ((f32[8,56,128]{2,1,0:T(8,128)}), f32[8,56,128]{2,1,0:T(8,128)S(1)}, u32[]{:S(2)}, u32[]{:S(2)}) async-start(f32[8,56,128]{2,1,0:T(8,128)} %get-tuple-element.45), calls=%async_computation.1 | async-start | bytes 458752 | tf_op jit(solution)/shard_map/all_to_all | solution.py:69
  59.5 3.0 %collective-permute-start.13 = (f32[256,128]{1,0:T(8,128)S(1)}, f32[256,128]{1,0:T(8,128)S(1)}, u32[]{:S(2)}, u32[]{:S(2)}) collective-permute-start(f32[256,128]{1,0:T(8,128)S(1)} %get-tuple-element.47.m0), channel_id=1, source_target_pairs={{0,4},{4,0},{1,5},{5,1},{2,6},{6,2},{3,7},{7,3},{8,12},{12,8},{9,1... | collective-permute-start | bytes 393224 | tf_op jit(solution)/shard_map/ppermute | solution.py:74
  59.6 2.9 %collective-permute-start.16 = (f32[256,128]{1,0:T(8,128)S(1)}, f32[256,128]{1,0:T(8,128)S(1)}, u32[]{:S(2)}, u32[]{:S(2)}) collective-permute-start(f32[256,128]{1,0:T(8,128)S(1)} %collective-permute-done.12.m3), channel_id=1, source_target_pairs={{0,4},{4,0},{1,5},{5,1},{2,6},{6,2},{3,7},{7,3},{8,12},{12,8},{9,1... | collective-permute-start | bytes 393224 | tf_op jit(solution)/shard_map/ppermute | solution.py:74
  60.0 0.7 copy-start.4
  60.6 1.8 %collective-permute-start.15 = (f32[256,128]{1,0:T(8,128)S(1)}, f32[256,128]{1,0:T(8,128)S(1)}, u32[]{:S(2)}, u32[]{:S(2)}) collective-permute-start(f32[256,128]{1,0:T(8,128)S(1)} %collective-permute-done.11.m2), channel_id=1, source_target_pairs={{0,4},{4,0},{1,5},{5,1},{2,6},{6,2},{3,7},{7,3},{8,12},{12,8},{9,1... | collective-permute-start | bytes 393224 | tf_op jit(solution)/shard_map/ppermute | solution.py:74
  60.7 0.6 copy-start.6
  61.4 1.4 collective-permute-start.14
  61.8 0.6 copy-start.8
  62.8 0.9 copy-start.3
  63.7 0.9 copy-start.5
  64.6 0.9 copy-start.7
  65.5 0.9 copy-start.9
  69.9 31.5 %copy-start.10 = (f32[192,128]{1,0:T(8,128)}, f32[192,128]{1,0:T(8,128)S(1)}, u32[]{:S(2)}) copy-start(f32[192,128]{1,0:T(8,128)S(1)} %get-tuple-element.52.p0) | copy-start | bytes 294916
  74.5 43.2 %all-to-all-start.2 = ((f32[8,72,128]{2,1,0:T(8,128)}), f32[8,72,128]{2,1,0:T(8,128)S(1)}, u32[]{:S(2)}, u32[]{:S(2)}) async-start(f32[8,72,128]{2,1,0:T(8,128)} %get-tuple-element.51), calls=%async_computation.2 | async-start | bytes 589824 | tf_op jit(solution)/shard_map/all_to_all | solution.py:69
  86.4 10.4 %collective-permute-start.17 = (f32[192,128]{1,0:T(8,128)S(1)}, f32[192,128]{1,0:T(8,128)S(1)}, u32[]{:S(2)}, u32[]{:S(2)}) collective-permute-start(f32[192,128]{1,0:T(8,128)S(1)} %get-tuple-element.52.p0), channel_id=1, source_target_pairs={{0,32},{32,64},{64,96},{96,128},{128,160},{160,192},{192,224},{224... | collective-permute-start | bytes 294920 | tf_op jit(solution)/shard_map/ppermute | solution.py:74
  87.8 8.9 %collective-permute-start.18 = (f32[192,128]{1,0:T(8,128)S(1)}, f32[192,128]{1,0:T(8,128)S(1)}, u32[]{:S(2)}, u32[]{:S(2)}) collective-permute-start(f32[192,128]{1,0:T(8,128)S(1)} %get-tuple-element.52.p0), channel_id=1, source_target_pairs={{0,224},{32,0},{64,32},{96,64},{128,96},{160,128},{192,160},{224,1... | collective-permute-start | bytes 294920 | tf_op jit(solution)/shard_map/ppermute | solution.py:74
  96.7 19.6 %copy-start.15 = (f32[192,128]{1,0:T(8,128)}, f32[192,128]{1,0:T(8,128)S(1)}, u32[]{:S(2)}) copy-start(f32[192,128]{1,0:T(8,128)S(1)} %collective-permute-done.17.p1) | copy-start | bytes 294916
  96.7 4.7 %collective-permute-start.19 = (f32[192,128]{1,0:T(8,128)S(1)}, f32[192,128]{1,0:T(8,128)S(1)}, u32[]{:S(2)}, u32[]{:S(2)}) collective-permute-start(f32[192,128]{1,0:T(8,128)S(1)} %collective-permute-done.17.p1), channel_id=1, source_target_pairs={{0,32},{32,64},{64,96},{96,128},{128,160},{160,192},{192,224},{224... | collective-permute-start | bytes 294920 | tf_op jit(solution)/shard_map/ppermute | solution.py:74
  96.8 19.6 %copy-start.16 = (f32[192,128]{1,0:T(8,128)}, f32[192,128]{1,0:T(8,128)S(1)}, u32[]{:S(2)}) copy-start(f32[192,128]{1,0:T(8,128)S(1)} %collective-permute-done.18.p2) | copy-start | bytes 294916
  96.8 8.5 %collective-permute-start.20 = (f32[192,128]{1,0:T(8,128)S(1)}, f32[192,128]{1,0:T(8,128)S(1)}, u32[]{:S(2)}, u32[]{:S(2)}) collective-permute-start(f32[192,128]{1,0:T(8,128)S(1)} %collective-permute-done.18.p2), channel_id=1, source_target_pairs={{0,224},{32,0},{64,32},{96,64},{128,96},{160,128},{192,160},{224,1... | collective-permute-start | bytes 294920 | tf_op jit(solution)/shard_map/ppermute | solution.py:74
  101.4 15.0 %copy-start.17 = (f32[192,128]{1,0:T(8,128)}, f32[192,128]{1,0:T(8,128)S(1)}, u32[]{:S(2)}) copy-start(f32[192,128]{1,0:T(8,128)S(1)} %collective-permute-done.19.p3) | copy-start | bytes 294916
  101.4 6.7 %collective-permute-start.21 = (f32[192,128]{1,0:T(8,128)S(1)}, f32[192,128]{1,0:T(8,128)S(1)}, u32[]{:S(2)}, u32[]{:S(2)}) collective-permute-start(f32[192,128]{1,0:T(8,128)S(1)} %collective-permute-done.19.p3), channel_id=1, source_target_pairs={{0,32},{32,64},{64,96},{96,128},{128,160},{160,192},{192,224},{224... | collective-permute-start | bytes 294920 | tf_op jit(solution)/shard_map/ppermute | solution.py:74
  101.4 6.7 %collective-permute-start.24 = (f32[192,128]{1,0:T(8,128)S(1)}, f32[192,128]{1,0:T(8,128)S(1)}, u32[]{:S(2)}, u32[]{:S(2)}) collective-permute-start(f32[192,128]{1,0:T(8,128)S(1)} %get-tuple-element.52.p0), channel_id=1, source_target_pairs={{0,4},{4,0},{1,5},{5,1},{2,6},{6,2},{3,7},{7,3},{8,12},{12,8},{9,1... | collective-permute-start | bytes 294920 | tf_op jit(solution)/shard_map/ppermute | solution.py:74
  104.8 5.8 %collective-permute-start.26 = (f32[192,128]{1,0:T(8,128)S(1)}, f32[192,128]{1,0:T(8,128)S(1)}, u32[]{:S(2)}, u32[]{:S(2)}) collective-permute-start(f32[192,128]{1,0:T(8,128)S(1)} %collective-permute-done.18.p2), channel_id=1, source_target_pairs={{0,4},{4,0},{1,5},{5,1},{2,6},{6,2},{3,7},{7,3},{8,12},{12,8},{9,1... | collective-permute-start | bytes 294920 | tf_op jit(solution)/shard_map/ppermute | solution.py:74
  104.9 5.9 %collective-permute-start.25 = (f32[192,128]{1,0:T(8,128)S(1)}, f32[192,128]{1,0:T(8,128)S(1)}, u32[]{:S(2)}, u32[]{:S(2)}) collective-permute-start(f32[192,128]{1,0:T(8,128)S(1)} %collective-permute-done.17.p1), channel_id=1, source_target_pairs={{0,4},{4,0},{1,5},{5,1},{2,6},{6,2},{3,7},{7,3},{8,12},{12,8},{9,1... | collective-permute-start | bytes 294920 | tf_op jit(solution)/shard_map/ppermute | solution.py:74
  105.3 11.1 %copy-start.18 = (f32[192,128]{1,0:T(8,128)}, f32[192,128]{1,0:T(8,128)S(1)}, u32[]{:S(2)}) copy-start(f32[192,128]{1,0:T(8,128)S(1)} %collective-permute-done.20.p4) | copy-start | bytes 294916
  105.3 5.8 %collective-permute-start.22 = (f32[192,128]{1,0:T(8,128)S(1)}, f32[192,128]{1,0:T(8,128)S(1)}, u32[]{:S(2)}, u32[]{:S(2)}) collective-permute-start(f32[192,128]{1,0:T(8,128)S(1)} %collective-permute-done.20.p4), channel_id=1, source_target_pairs={{0,224},{32,0},{64,32},{96,64},{128,96},{160,128},{192,160},{224,1... | collective-permute-start | bytes 294920 | tf_op jit(solution)/shard_map/ppermute | solution.py:74
  108.2 8.3 %copy-start.19 = (f32[192,128]{1,0:T(8,128)}, f32[192,128]{1,0:T(8,128)S(1)}, u32[]{:S(2)}) copy-start(f32[192,128]{1,0:T(8,128)S(1)} %collective-permute-done.21.p5) | copy-start | bytes 294916
  108.2 4.7 %collective-permute-start.23 = (f32[192,128]{1,0:T(8,128)S(1)}, f32[192,128]{1,0:T(8,128)S(1)}, u32[]{:S(2)}, u32[]{:S(2)}) collective-permute-start(f32[192,128]{1,0:T(8,128)S(1)} %collective-permute-done.21.p5), channel_id=1, source_target_pairs={{0,32},{32,64},{64,96},{96,128},{128,160},{160,192},{192,224},{224... | collective-permute-start | bytes 294920 | tf_op jit(solution)/shard_map/ppermute | solution.py:74
  108.2 8.3 %copy-start.20 = (f32[192,128]{1,0:T(8,128)}, f32[192,128]{1,0:T(8,128)S(1)}, u32[]{:S(2)}) copy-start(f32[192,128]{1,0:T(8,128)S(1)} %collective-permute-done.24.q0) | copy-start | bytes 294916
  108.2 8.2 %collective-permute-start.28 = (f32[192,128]{1,0:T(8,128)S(1)}, f32[192,128]{1,0:T(8,128)S(1)}, u32[]{:S(2)}, u32[]{:S(2)}) collective-permute-start(f32[192,128]{1,0:T(8,128)S(1)} %collective-permute-done.20.p4), channel_id=1, source_target_pairs={{0,4},{4,0},{1,5},{5,1},{2,6},{6,2},{3,7},{7,3},{8,12},{12,8},{9,1... | collective-permute-start | bytes 294920 | tf_op jit(solution)/shard_map/ppermute | solution.py:74
  110.6 5.8 %copy-start.21 = (f32[192,128]{1,0:T(8,128)}, f32[192,128]{1,0:T(8,128)S(1)}, u32[]{:S(2)}) copy-start(f32[192,128]{1,0:T(8,128)S(1)} %collective-permute-done.26.q2) | copy-start | bytes 294916
  110.6 5.7 %collective-permute-start.27 = (f32[192,128]{1,0:T(8,128)S(1)}, f32[192,128]{1,0:T(8,128)S(1)}, u32[]{:S(2)}, u32[]{:S(2)}) collective-permute-start(f32[192,128]{1,0:T(8,128)S(1)} %collective-permute-done.19.p3), channel_id=1, source_target_pairs={{0,4},{4,0},{1,5},{5,1},{2,6},{6,2},{3,7},{7,3},{8,12},{12,8},{9,1... | collective-permute-start | bytes 294920 | tf_op jit(solution)/shard_map/ppermute | solution.py:74
  110.7 5.7 %copy-start.22 = (f32[192,128]{1,0:T(8,128)}, f32[192,128]{1,0:T(8,128)S(1)}, u32[]{:S(2)}) copy-start(f32[192,128]{1,0:T(8,128)S(1)} %collective-permute-done.25.q1) | copy-start | bytes 294916
  110.7 5.6 %collective-permute-start.29 = (f32[192,128]{1,0:T(8,128)S(1)}, f32[192,128]{1,0:T(8,128)S(1)}, u32[]{:S(2)}, u32[]{:S(2)}) collective-permute-start(f32[192,128]{1,0:T(8,128)S(1)} %collective-permute-done.21.p5), channel_id=1, source_target_pairs={{0,4},{4,0},{1,5},{5,1},{2,6},{6,2},{3,7},{7,3},{8,12},{12,8},{9,1... | collective-permute-start | bytes 294920 | tf_op jit(solution)/shard_map/ppermute | solution.py:74
  111.1 5.3 %copy-start.23 = (f32[192,128]{1,0:T(8,128)}, f32[192,128]{1,0:T(8,128)S(1)}, u32[]{:S(2)}) copy-start(f32[192,128]{1,0:T(8,128)S(1)} %collective-permute-done.22.p6) | copy-start | bytes 294916
  111.1 5.2 %collective-permute-start.30 = (f32[192,128]{1,0:T(8,128)S(1)}, f32[192,128]{1,0:T(8,128)S(1)}, u32[]{:S(2)}, u32[]{:S(2)}) collective-permute-start(f32[192,128]{1,0:T(8,128)S(1)} %collective-permute-done.22.p6), channel_id=1, source_target_pairs={{0,4},{4,0},{1,5},{5,1},{2,6},{6,2},{3,7},{7,3},{8,12},{12,8},{9,1... | collective-permute-start | bytes 294920 | tf_op jit(solution)/shard_map/ppermute | solution.py:74
  112.8 3.6 %copy-start.24 = (f32[192,128]{1,0:T(8,128)}, f32[192,128]{1,0:T(8,128)S(1)}, u32[]{:S(2)}) copy-start(f32[192,128]{1,0:T(8,128)S(1)} %collective-permute-done.23.p7) | copy-start | bytes 294916
  112.8 4.9 %collective-permute-start.31 = (f32[192,128]{1,0:T(8,128)S(1)}, f32[192,128]{1,0:T(8,128)}, u32[]{:S(2)}, u32[]{:S(2)}) collective-permute-start(f32[192,128]{1,0:T(8,128)S(1)} %collective-permute-done.23.p7), channel_id=1, source_target_pairs={{0,4},{4,0},{1,5},{5,1},{2,6},{6,2},{3,7},{7,3},{8,12},{12,8},{9,1... | collective-permute-start | bytes 294920 | tf_op jit(solution)/shard_map/ppermute | solution.py:74
  116.3 1.4 copy-start.25
  116.4 0.7 copy-start.26
  116.4 0.7 copy-start.28
  117.1 0.6 copy-start.27
  117.7 13.9 %copy-start.1 = (f32[384,128]{1,0:T(8,128)S(1)}, f32[384,128]{1,0:T(8,128)}, u32[]{:S(2)}) copy-start(f32[384,128]{1,0:T(8,128)} %get-tuple-element.57.defect_ref) | copy-start | bytes 589828
  117.7 13.9 %copy-start.12 = (f32[256]{0:T(256)S(1)}, f32[256]{0:T(256)}, u32[]{:S(2)}) copy-start(f32[256]{0:T(256)} %param.15) | copy-start | bytes 3076
  131.7 10.6 %copy-start.13 = (f32[96,256]{1,0:T(8,128)S(1)}, f32[96,256]{1,0:T(8,128)}, u32[]{:S(2)}) copy-start(f32[96,256]{1,0:T(8,128)} %direction_ref) | copy-start | bytes 294916
  131.7 10.6 %copy-start.14 = (f32[96,256]{1,0:T(8,128)S(1)}, f32[96,256]{1,0:T(8,128)}, u32[]{:S(2)}) copy-start(f32[96,256]{1,0:T(8,128)} %residual_ref) | copy-start | bytes 294916
  131.7 10.6 %copy-start.29 = (f32[96,256]{1,0:T(8,128)S(1)}, f32[96,256]{1,0:T(8,128)}, u32[]{:S(2)}) copy-start(f32[96,256]{1,0:T(8,128)} %param.12) | copy-start | bytes 294916
